TPU v7x, 128 devices: a whole 4x4x4 slice. The times are simulated.
128 devices in a mesh: dp: 4 (over x), cp: 32 (over z, y, core).
Axes of the slice: x: 4, y: 4, z: 4, core: 2. Of those that a mesh axis runs over, the one named last changes fastest.
Arguments:
- tokens: bfloat16 [4, 4096, 4096], P('dp', 'cp'), may hold values from -60 to 60
- qkv_weight: bfloat16 [4096, 3072], replicated, may hold values from -0.09375 to 0.09375
- owner_slot: int32 [4, 32], P('dp', 'cp'), may hold values from 0 to 3, as said below
- slab_sequence: int32 [4, 32], replicated, may hold values from 0 to 16, as said below
- slab_order: int32 [4, 32], replicated, may hold values from 0 to 15, as said below
Outputs:
- context: bfloat16 [4, 4096, 2048], P('dp', 'cp')
Inputs may be any that keep to these rules, and one draw needn't show every extreme that they name: For every column c, the entries owner_slot[a, c] over all rows a are 0 to 3, each once. `slab_sequence`: in each row, the slabs with one sequence number carry the orders 0 to L-1, each once, L being their count; no sequence has more than 16 slabs. `slab_order`: see slab_sequence.
All inputs are finite; a program needn't handle non-finite values.
Results may differ from a plain program's by a relative error of at most 0.006.
The roundings to bfloat16 on the way count: a program that leaves them out, or rounds other values in their place, can miss the bound.
Values may be sent and summed in bfloat16 or wider, within the bound.
No kernel may reach another device: no remote copies, remote signals or barrier semaphores. Data moves between devices by JAX's collectives and lax.ppermute only.
A program may use at most 128 MiB of HBM per device.

v0:
```python
import functools

import jax
import jax.numpy as jnp
from jax import lax
from jax.experimental import pallas as pl
from jax.experimental.pallas import tpu as pltpu
from jax.sharding import PartitionSpec as P


QH = 16
KVH = 4
HD = 128
SLAB = 128
GROUP = QH // KVH
NEG_FILL = -1e30
AXES = ("dp", "cp")
SIDE = 4
Q_COLS = QH * HD


def pairs(move):
    out = []
    for x in range(SIDE):
        for z in range(SIDE):
            for y in range(SIDE):
                for c in range(2):
                    nx, nz, ny, nc = move(x, z, y, c)
                    here = x * 32 + (z * SIDE + y) * 2 + c
                    there = (nx % SIDE) * 32 + ((nz % SIDE) * SIDE + ny % SIDE) * 2 + nc % 2
                    out.append((here, there))
    return out


def shift_x(k):
    return pairs(lambda x, z, y, c: (x + k, z, y, c))


def shift_first(k):
    return pairs(lambda x, z, y, c: (x, z + k, y, c) if c == 0 else (x, z, y + k, c))


def shift_second(k):
    return pairs(lambda x, z, y, c: (x, z, y + k, c) if c == 0 else (x, z + k, y, c))


OTHER_CORE = pairs(lambda x, z, y, c: (x, z, y, c + 1))


def permute(value, table):
    return lax.ppermute(value, AXES, table)


def rope_tables(order, slot, cos_ref, sin_ref):
    lane = lax.broadcasted_iota(jnp.int32, (SLAB, HD), 1)
    half = jnp.where(lane < HD // 2, lane, lane - HD // 2).astype(jnp.float32)
    frequency = jnp.exp(half * (-2.0 / HD * 13.122363377404328))
    row = lax.broadcasted_iota(jnp.int32, (SLAB, HD), 0)
    angle = (order * SLAB + row).astype(jnp.float32) * frequency
    cos_ref[slot] = jnp.cos(angle)
    sine = jnp.sin(angle)
    sin_ref[slot] = jnp.where(lane < HD // 2, -sine, sine)


def rope(block, slot, cos_ref, sin_ref):
    return block * cos_ref[slot] + pltpu.roll(block, HD // 2, 1) * sin_ref[slot]


def begin(core_ref, other_ref, owner_ref, order_ref, cos_ref, sin_ref):
    column = lax.axis_index("cp")
    owners = (other_ref[0, 0], owner_ref[0, 0])
    columns = (column + 1 - 2 * core_ref[0], column)

    @pl.when(pl.program_id(0) == 0)
    def _():
        for slot in range(2):
            rope_tables(order_ref[owners[slot], columns[slot]], slot, cos_ref, sin_ref)

    return owners


def store_masked(outs, owner, rows, columns, value):
    my_row = lax.axis_index("dp")
    for k, out in enumerate(outs):
        mine = owner == lax.rem(my_row + k, SIDE)
        out[rows, columns] = jnp.where(mine, value, jnp.zeros_like(value))


def kv_kernel(core_ref, other_ref, owner_ref, order_ref, y_ref, x_ref, w_ref, *refs):
    outs, (cos_ref, sin_ref) = refs[:4], refs[4:]
    owners = begin(core_ref, other_ref, owner_ref, order_ref, cos_ref, sin_ref)
    both = jnp.concatenate([y_ref[...], x_ref[...]], axis=0)
    projected = jnp.dot(both, w_ref[...], preferred_element_type=jnp.float32)
    heads = w_ref.shape[1] // HD
    step = pl.program_id(0)

    @pl.when(step < 2 // heads)
    def _():
        for slot in range(2):
            rows = slice(slot * SLAB, (slot + 1) * SLAB)
            for h in range(heads):
                columns = slice(h * HD, (h + 1) * HD)
                value = rope(projected[rows, columns], slot, cos_ref, sin_ref).astype(jnp.bfloat16)
                store_masked(outs, owners[slot], rows, columns, value)

    @pl.when(step >= 2 // heads)
    def _():
        for slot in range(2):
            rows = slice(slot * SLAB, (slot + 1) * SLAB)
            for h in range(heads):
                columns = slice(h * HD, (h + 1) * HD)
                value = projected[rows, columns].T.astype(jnp.bfloat16)
                store_masked(outs, owners[slot], rows, columns, value)


def q_kernel(core_ref, other_ref, owner_ref, order_ref, y_ref, x_ref, w_ref, *refs):
    outs, (cos_ref, sin_ref) = refs[:8], refs[8:]
    owners = begin(core_ref, other_ref, owner_ref, order_ref, cos_ref, sin_ref)
    both = jnp.concatenate([y_ref[...], x_ref[...]], axis=0)
    projected = jnp.dot(both, w_ref[...], preferred_element_type=jnp.float32)
    for slot in range(2):
        for h in range(w_ref.shape[1] // HD):
            columns = slice(h * HD, (h + 1) * HD)
            block = projected[slot * SLAB : (slot + 1) * SLAB, columns]
            value = rope(block, slot, cos_ref, sin_ref).T.astype(jnp.bfloat16)
            store_masked(outs[4 * slot : 4 * slot + 4], owners[slot], slice(None), columns, value)


def in_vmem(value):
    return pltpu.with_memory_space_constraint(value, pltpu.VMEM)


def project(kernel, core, owners, slab_order, others, rows, weight, block, blocks, width, out):
    depth = rows.shape[1]
    smem = pl.BlockSpec(memory_space=pltpu.SMEM)
    return pl.pallas_call(
        kernel,
        grid_spec=pltpu.PrefetchScalarGridSpec(
            num_scalar_prefetch=1,
            grid=(blocks,),
            in_specs=[
                smem,
                smem,
                smem,
                pl.BlockSpec(memory_space=pltpu.VMEM),
                pl.BlockSpec(memory_space=pltpu.VMEM),
                pl.BlockSpec((depth, width), lambda j, c: (0, block(j, c[0]))),
            ],
            out_specs=[pl.BlockSpec((o.shape[0], width), lambda j, c: (0, j)) for o in out],
            scratch_shapes=[pltpu.VMEM((2, SLAB, HD), jnp.float32)] * 2,
        ),
        out_shape=out,
        compiler_params=pltpu.CompilerParams(
            dimension_semantics=("arbitrary",), vmem_limit_bytes=24 << 20
        ),
        cost_estimate=pl.CostEstimate(
            flops=4 * SLAB * depth * blocks * width,
            bytes_accessed=2 * depth * (2 * SLAB + blocks * width),
            transcendentals=0,
        ),
    )(core, *owners, slab_order, in_vmem(others), in_vmem(rows), weight)


FACTOR = HD**-0.5 * 1.4426950408889634
WIDE = GROUP * SLAB
LOW, HIGH = (0, 1), (3, 2)
LOCAL = ((LOW, 0), (HIGH, 0))
NEAR = ((LOW, 1), (HIGH, 1), (HIGH, 3), (LOW, 3))
FAR = ((LOW, 2), (HIGH, 2))


def attend_kernel(spots, t, first, last, sequence_ref, order_ref, *refs):
    parts, refs = refs[:4], refs[4:]
    pieces, refs = refs[: len(spots)], refs[len(spots) :]
    if not first:
        old, refs = refs[:3], refs[3:]
    if last:
        out, acc, peak, total, q_ref, kv, scores_ref, chosen = refs
    else:
        acc, peak, total, q_ref, kv, scores_ref, chosen = refs
    row = lax.axis_index("dp")
    column = lax.axis_index("cp")
    core, y, z = lax.rem(column, 2), lax.rem(column // 2, SIDE), column // (2 * SIDE)
    mine = column if t == 1 else column + 1 - 2 * core
    my_sequence, my_order = sequence_ref[row, mine], order_ref[row, mine]
    count = jnp.int32(0)
    for a, (chips, second) in enumerate(spots):
        for b, k in enumerate(chips):
            sz = lax.rem(z + 2 * SIDE - jnp.where(core == 0, k, second), SIDE)
            sy = lax.rem(y + 2 * SIDE - jnp.where(core == 0, second, k), SIDE)
            for c in range(2):
                source = (sz * SIDE + sy) * 2 + (core if c == 1 else 1 - core)
                wanted = (sequence_ref[row, source] == my_sequence) & (
                    order_ref[row, source] < my_order
                )

                @pl.when(wanted)
                def _():
                    kv[count] = pieces[a][(b * 2 + c) * SLAB : (b * 2 + c + 1) * SLAB, :]

                count = count + wanted.astype(jnp.int32)

    @pl.when(lax.rem(count, 2) == 1)
    def _():
        kv[count] = jnp.zeros((SLAB, 4 * HD), jnp.bfloat16)

    pairs_here = (count + 1) // 2
    q_ref[...] = parts[0][...] + parts[1][...] + parts[2][...] + parts[3][...]
    starts = []
    for g in range(2):
        if first:
            key_row = lax.broadcasted_iota(jnp.int32, (SLAB, WIDE), 0)
            token = lax.rem(lax.broadcasted_iota(jnp.int32, (SLAB, WIDE), 1), SLAB)
            scores = jnp.dot(
                pieces[0][t * SLAB : (t + 1) * SLAB, g * HD : (g + 1) * HD],
                q_ref[:, g * WIDE : (g + 1) * WIDE],
                preferred_element_type=jnp.float32,
            )
            scores = jnp.where(key_row <= token, scores, NEG_FILL)
            scores_ref[8, g, :SLAB] = scores
            peak[g] = jnp.max(scores.reshape(SLAB // 8, 8, WIDE), axis=0)
        else:
            peak[g] = old[1][g]
            starts.append(jnp.max(old[1][g], axis=0, keepdims=True))

    def score(p, carry):
        full = 2 * p + 1 < count
        for g in range(2):
            keys = slice(g * HD, (g + 1) * HD)
            both = jnp.concatenate([kv[2 * p, :, keys], kv[2 * p + 1, :, keys]], axis=0)
            scores = jnp.dot(
                both, q_ref[:, g * WIDE : (g + 1) * WIDE], preferred_element_type=jnp.float32
            )
            low = scores[:SLAB]
            high = jnp.where(full, scores[SLAB:], NEG_FILL)
            scores_ref[p, g, :SLAB] = low
            scores_ref[p, g, SLAB:] = high
            top = jnp.maximum(low, high).reshape(SLAB // 8, 8, WIDE)
            peak[g] = jnp.maximum(peak[g], jnp.max(top, axis=0))
        return carry

    lax.fori_loop(0, pairs_here, score, 0)
    tops = []
    for g in range(2):
        top = jnp.max(peak[g], axis=0, keepdims=True)
        tops.append(top * FACTOR)
        if first:
            weights = jnp.exp2(scores_ref[8, g, :SLAB] * FACTOR - tops[g])
            total[g] = jnp.sum(weights.reshape(SLAB // 8, 8, WIDE), axis=0)
            acc[g] = jnp.dot(
                pieces[0][t * SLAB : (t + 1) * SLAB, (2 + g) * HD : (3 + g) * HD],
                weights.astype(jnp.bfloat16),
                preferred_element_type=jnp.float32,
            )
        else:
            rescale = jnp.exp2((starts[g] - top) * FACTOR)
            total[g] = old[2][g] * rescale
            acc[g] = old[0][g] * rescale

    def weigh(p, carry):
        for g in range(2):
            values = slice((2 + g) * HD, (3 + g) * HD)
            weights = jnp.exp2(scores_ref[p, g] * FACTOR - tops[g])
            total[g] = total[g] + jnp.sum(weights.reshape(SLAB // 4, 8, WIDE), axis=0)
            both = jnp.concatenate([kv[2 * p, :, values], kv[2 * p + 1, :, values]], axis=1)
            acc[g] = acc[g] + jnp.dot(
                both, weights.astype(jnp.bfloat16), preferred_element_type=jnp.float32
            )
        return carry

    lax.fori_loop(0, pairs_here, weigh, 0)
    if last:
        for g in range(2):
            context = acc[g] / jnp.sum(total[g], axis=0, keepdims=True)
            for h in range(GROUP):
                head = g * GROUP + h
                out[:, head * HD : (head + 1) * HD] = context[:, h * SLAB : (h + 1) * SLAB].T.astype(
                    jnp.bfloat16
                )


STATE = ((2, HD, WIDE), (2, 8, WIDE), (2, 8, WIDE))
HALF = Q_COLS // 2


def attend(spots, t, slab_sequence, slab_order, parts, pieces, state, last):
    first = state is None
    vmem = pl.BlockSpec(memory_space=pltpu.VMEM)
    smem = pl.BlockSpec(memory_space=pltpu.SMEM)
    scratch = [
        pltpu.VMEM((SLAB, HALF), jnp.bfloat16),
        pltpu.VMEM((16, SLAB, 4 * HD), jnp.bfloat16),
        pltpu.VMEM((9, 2, 2 * SLAB, WIDE), jnp.float32),
    ]
    if last:
        out_shape = [pltpu.VMEM((SLAB, HALF), jnp.bfloat16)]
        scratch = [pltpu.VMEM(s, jnp.float32) for s in STATE] + scratch
    else:
        out_shape = [pltpu.VMEM(s, jnp.float32) for s in STATE]
    operands = [in_vmem(v) for v in (*parts, *pieces, *(state or ()))]
    return pl.pallas_call(
        functools.partial(attend_kernel, spots, t, first, last),
        in_specs=[smem, smem] + [vmem] * len(operands),
        out_specs=[vmem] * len(out_shape),
        out_shape=out_shape,
        scratch_shapes=scratch + [pltpu.SMEM((16,), jnp.int32)],
        compiler_params=pltpu.CompilerParams(vmem_limit_bytes=28 << 20),
        cost_estimate=pl.CostEstimate(
            flops=2 * SLAB * len(spots) * 4 * SLAB * HALF,
            bytes_accessed=2 << 20,
            transcendentals=0,
        ),
    )(slab_sequence, slab_order, *operands)


def join_kernel(core_ref, kept_ref, received_ref, out_ref):
    core = core_ref[0]
    out_ref[:, pl.ds(pl.multiple_of(core * HALF, HALF), HALF)] = kept_ref[...]
    out_ref[:, pl.ds(pl.multiple_of((1 - core) * HALF, HALF), HALF)] = received_ref[...]


def join(core, kept, received):
    vmem = pl.BlockSpec(memory_space=pltpu.VMEM)
    return pl.pallas_call(
        join_kernel,
        in_specs=[pl.BlockSpec(memory_space=pltpu.SMEM), vmem, vmem],
        out_specs=vmem,
        out_shape=jax.ShapeDtypeStruct((SLAB, Q_COLS), jnp.bfloat16),
        compiler_params=pltpu.CompilerParams(vmem_limit_bytes=8 << 20),
        cost_estimate=pl.CostEstimate(flops=SLAB * Q_COLS, bytes_accessed=1 << 20, transcendentals=0),
        name="join",
    )(core, in_vmem(kept), in_vmem(received))


def local(tokens, qkv_weight, owner_slot, slab_sequence, slab_order):
    rows = tokens[0]
    core = lax.rem(lax.axis_index("cp"), 2)
    others = permute(rows, OTHER_CORE)
    owners = (permute(owner_slot, OTHER_CORE), owner_slot)
    common = (core.reshape(1), owners, slab_order, others, rows, qkv_weight)
    kv = project(
        kv_kernel, *common, lambda j, c: QH // 2 + 2 * j + c, 2, 2 * HD,
        [jax.ShapeDtypeStruct((2 * SLAB, 4 * HD), jnp.bfloat16)] * 4,
    )
    queries = project(
        q_kernel, *common, lambda j, c: 4 * c + j, 4, 2 * HD,
        [jax.ShapeDtypeStruct((SLAB, HALF), jnp.bfloat16)] * 8,
    )
    moved = [permute(kv[k], shift_x(k)) for k in (1, 3, 2)]
    parts = [[queries[0]] + [permute(queries[k], shift_x(k)) for k in (1, 3, 2)]]
    own = kv[0] + moved[0] + moved[1] + moved[2]
    first = [permute(own, shift_first(k)) for k in (1, 3, 2)]
    parts.append([queries[4]] + [permute(queries[4 + k], shift_x(k)) for k in (1, 3, 2)])
    low = jnp.concatenate([own, first[0]], axis=0)
    high = jnp.concatenate([first[1], first[2]], axis=0)
    left = [permute(v, shift_second(1)) for v in (low, high)]
    right = [permute(v, shift_second(3)) for v in (high, low)]
    far = [permute(left[0], shift_second(1)), permute(right[0], shift_second(3))]
    near = [low, high, *left, *right]
    tables = (slab_sequence, slab_order)
    state = [attend(LOCAL + NEAR, t, *tables, parts[t], near, None, False) for t in range(2)]
    (sent,) = attend(FAR, 0, *tables, parts[0], far, state[0], True)
    received = permute(sent, OTHER_CORE)
    (kept,) = attend(FAR, 1, *tables, parts[1], far, state[1], True)
    return join(core.reshape(1), kept, received)[None]


def solution(mesh):
    in_specs = (P("dp", "cp", None), P(), P("dp", "cp"), P(), P())
    out_specs = P("dp", "cp", None)
    return jax.shard_map(local, mesh=mesh, in_specs=in_specs, out_specs=out_specs, check_vma=False)
```

profile of v0, /device:TPU:33, one launch (start us, length us, event | category | flops | bytes accessed | tf_op | source)
XLA Modules:
  0.0 95.9 jit_solution(7137001364469318217)
XLA Ops:
  0.0 0.7 collective-permute-start.1
  0.7 0.0 collective-permute-start
  1.3 1.8 %collective-permute-done.other_ref = s32[1,1]{1,0:T(1,128)} collective-permute-done((s32[1,1]{1,0:T(1,128)}, s32[1,1]{1,0:T(1,128)}, u32[]{:S(2)}, u32[]{:S(2)}) %collective-permute-start) | collective-permute-done | bytes 36 | tf_op jit(solution)/shard_map/ppermute | solution.py:51
  3.2 0.0 collective-permute-done.1.y_ref
  3.2 8.2 %copy-done = bf16[4096,3072]{1,0:T(8,128)(2,1)S(1)} copy-done((bf16[4096,3072]{1,0:T(8,128)(2,1)S(1)}, bf16[4096,3072]{1,0:T(8,128)(2,1)}, u32[]{:S(2)}) %copy-start) | copy-done | bytes 25165848
  11.3 1.2 %copy-done.1 = bf16[1,128,4096]{2,1,0:T(8,128)(2,1)S(1)} copy-done((bf16[1,128,4096]{2,1,0:T(8,128)(2,1)S(1)}, bf16[1,128,4096]{2,1,0:T(8,128)(2,1)}, u32[]{:S(2)}) %copy-start.1) | copy-done | bytes 1048600
  12.6 0.7 copy-done.2
  13.2 3.9 %shard_map.56 = (bf16[256,512]{1,0:T(8,128)(2,1)S(1)}, bf16[256,512]{1,0:T(8,128)(2,1)S(1)}, bf16[256,512]{1,0:T(8,128)(2,1)S(1)}, bf16[256,512]{1,0:T(8,128)(2,1)S(1)}) custom-call(s32[1]{0:T(128)} %bitcast.core_ref, s32[1,1]{1,0:T(1,128)} %collective-permute-done.other_ref, s32[1,1]{1,0:T(1,128)S(6)} %copy.7.owner_ref, s32[4,32]{1,0:T(4,128)S(1)} %copy-done.2, ...), custom_call_target="tpu_custom_call" | custom-call | flops 1073741824 | bytes 6291456 | tf_op jit(solution)/shard_map/pallas_call | solution.py:136
  17.2 1.3 %collective-permute-start.5 = (bf16[256,512]{1,0:T(8,128)(2,1)S(1)}, bf16[256,512]{1,0:T(8,128)(2,1)S(1)}, u32[]{:S(2)}, u32[]{:S(2)}) collective-permute-start(bf16[256,512]{1,0:T(8,128)(2,1)S(1)} %get-tuple-element.28), channel_id=1, source_target_pairs={{0,32},{1,33},{2,34},{3,35},{4,36},{5,37},{6,38},{7,39},{8,40},{9,... | collective-permute-start | bytes 786440 | tf_op jit(solution)/shard_map/ppermute | solution.py:51
  18.4 1.5 %collective-permute-start.6 = (bf16[256,512]{1,0:T(8,128)(2,1)S(1)}, bf16[256,512]{1,0:T(8,128)(2,1)S(1)}, u32[]{:S(2)}, u32[]{:S(2)}) collective-permute-start(bf16[256,512]{1,0:T(8,128)(2,1)S(1)} %get-tuple-element.29), channel_id=1, source_target_pairs={{0,96},{1,97},{2,98},{3,99},{4,100},{5,101},{6,102},{7,103},{8,104... | collective-permute-start | bytes 786440 | tf_op jit(solution)/shard_map/ppermute | solution.py:51
  19.9 1.5 %collective-permute-start.7 = (bf16[256,512]{1,0:T(8,128)(2,1)S(1)}, bf16[256,512]{1,0:T(8,128)(2,1)S(1)}, u32[]{:S(2)}, u32[]{:S(2)}) collective-permute-start(bf16[256,512]{1,0:T(8,128)(2,1)S(1)} %get-tuple-element.30), channel_id=1, source_target_pairs={{0,64},{1,65},{2,66},{3,67},{4,68},{5,69},{6,70},{7,71},{8,72},{9,... | collective-permute-start | bytes 786440 | tf_op jit(solution)/shard_map/ppermute | solution.py:51
  21.4 4.5 %collective-permute-done.5 = bf16[256,512]{1,0:T(8,128)(2,1)S(1)} collective-permute-done((bf16[256,512]{1,0:T(8,128)(2,1)S(1)}, bf16[256,512]{1,0:T(8,128)(2,1)S(1)}, u32[]{:S(2)}, u32[]{:S(2)}) %collective-permute-start.5) | collective-permute-done | bytes 262176 | tf_op jit(solution)/shard_map/ppermute | solution.py:51
  25.9 0.0 collective-permute-done.6
  25.9 6.6 %collective-permute-done.7 = bf16[256,512]{1,0:T(8,128)(2,1)S(1)} collective-permute-done((bf16[256,512]{1,0:T(8,128)(2,1)S(1)}, bf16[256,512]{1,0:T(8,128)(2,1)S(1)}, u32[]{:S(2)}, u32[]{:S(2)}) %collective-permute-start.7) | collective-permute-done | bytes 262176 | tf_op jit(solution)/shard_map/ppermute | solution.py:51
  32.5 0.1 add_add_fusion
  32.6 2.8 %collective-permute-start.11 = (bf16[256,512]{1,0:T(8,128)(2,1)S(1)}, bf16[256,512]{1,0:T(8,128)(2,1)S(1)}, u32[]{:S(2)}, u32[]{:S(2)}) collective-permute-start(bf16[256,512]{1,0:T(8,128)(2,1)S(1)} %add_add_fusion), channel_id=1, source_target_pairs={{0,24},{1,7},{2,26},{3,1},{4,28},{5,3},{6,30},{7,5},{8,0},{9,15},{... | collective-permute-start | bytes 786440 | tf_op jit(solution)/shard_map/ppermute | solution.py:51
  35.4 0.4 collective-permute-start.12
  35.8 0.7 collective-permute-start.8
  36.4 5.1 %collective-permute-done.11 = bf16[256,512]{1,0:T(8,128)(2,1)S(1)} collective-permute-done((bf16[256,512]{1,0:T(8,128)(2,1)S(1)}, bf16[256,512]{1,0:T(8,128)(2,1)S(1)}, u32[]{:S(2)}, u32[]{:S(2)}) %collective-permute-start.11) | collective-permute-done | bytes 262176 | tf_op jit(solution)/shard_map/ppermute | solution.py:51
  41.5 0.7 collective-permute-done.12
  42.2 0.1 collective-permute-start.13
  42.3 2.6 %collective-permute-done.8 = bf16[256,512]{1,0:T(8,128)(2,1)S(1)} collective-permute-done((bf16[256,512]{1,0:T(8,128)(2,1)S(1)}, bf16[256,512]{1,0:T(8,128)(2,1)S(1)}, u32[]{:S(2)}, u32[]{:S(2)}) %collective-permute-start.8) | collective-permute-done | bytes 262176 | tf_op jit(solution)/shard_map/ppermute | solution.py:51
  45.0 1.7 %collective-permute-start.9 = (bf16[512,512]{1,0:T(8,128)(2,1)S(1)}, bf16[512,512]{1,0:T(8,128)(2,1)S(1)}, u32[]{:S(2)}, u32[]{:S(2)}) collective-permute-start(bf16[512,512]{1,0:T(8,128)(2,1)S(1)} %pad_maximum_fusion.refs_4_), channel_id=1, source_target_pairs={{0,2},{1,9},{2,4},{3,11},{4,6},{5,13},{6,0},{7,15},{8,10},{9,17},{... | collective-permute-start | bytes 1572872 | tf_op jit(solution)/shard_map/ppermute | solution.py:51
  46.7 6.7 %shard_map.55 = (bf16[128,1024]{1,0:T(8,128)(2,1)S(1)}, bf16[128,1024]{1,0:T(8,128)(2,1)S(1)}, bf16[128,1024]{1,0:T(8,128)(2,1)S(1)}, bf16[128,1024]{1,0:T(8,128...) custom-call(s32[1]{0:T(128)} %bitcast.core_ref, ...), custom_call_target="tpu_custom_call" | custom-call | flops 2147483648 | bytes 10485760 | tf_op jit(solution)/shard_map/pallas_call | solution.py:136
  53.4 0.7 collective-permute-start.17
  54.1 2.1 %collective-permute-start.18 = (bf16[128,1024]{1,0:T(8,128)(2,1)S(1)}, bf16[128,1024]{1,0:T(8,128)(2,1)S(1)}, u32[]{:S(2)}, u32[]{:S(2)}) collective-permute-start(bf16[128,1024]{1,0:T(8,128)(2,1)S(1)} %get-tuple-element.36), channel_id=1, source_target_pairs={{0,96},{1,97},{2,98},{3,99},{4,100},{5,101},{6,102},{7,103},{8,104... | collective-permute-start | bytes 786440 | tf_op jit(solution)/shard_map/ppermute | solution.py:51
  56.2 1.3 %collective-permute-start.15 = (bf16[512,512]{1,0:T(8,128)(2,1)S(1)}, bf16[512,512]{1,0:T(8,128)(2,1)S(1)}, u32[]{:S(2)}, u32[]{:S(2)}) collective-permute-start(bf16[512,512]{1,0:T(8,128)(2,1)S(1)} %constant_dynamic-update-slice_fusion.refs_5_), channel_id=1, source_target_pairs={{0,2},{1,9},{2,4},{3,11},{4,6},{5,13},{6,0},{7,15},{8,10},{9,17},{... | collective-permute-start | bytes 1572872 | tf_op jit(solution)/shard_map/ppermute | solution.py:51
  57.5 4.1 %collective-permute-done.17.refs_1_ = bf16[128,1024]{1,0:T(8,128)(2,1)S(1)} collective-permute-done((bf16[128,1024]{1,0:T(8,128)(2,1)S(1)}, bf16[128,1024]{1,0:T(8,128)(2,1)S(1)}, u32[]{:S(2)}, u32[]{:S(2)}) %collective-permute-start.17) | collective-permute-done | bytes 262176 | tf_op jit(solution)/shard_map/ppermute | solution.py:51
  61.6 0.0 collective-permute-start.16
  61.6 0.0 collective-permute-done.13.refs_8_
  61.6 0.3 collective-permute-start.14
  61.9 2.0 %collective-permute-start.10 = (bf16[512,512]{1,0:T(8,128)(2,1)S(1)}, bf16[512,512]{1,0:T(8,128)(2,1)S(1)}, u32[]{:S(2)}, u32[]{:S(2)}) collective-permute-start(bf16[512,512]{1,0:T(8,128)(2,1)S(1)} %collective-permute-done.9.refs_6_), channel_id=1, source_target_pairs={{0,2},{1,9},{2,4},{3,11},{4,6},{5,13},{6,0},{7,15},{8,10},{9,17},{... | collective-permute-start | bytes 1572872 | tf_op jit(solution)/shard_map/ppermute | solution.py:51
  63.9 0.0 collective-permute-done.18.refs_2_
  63.9 0.0 collective-permute-start.19
  63.9 6.7 %collective-permute-done.19.refs_3_ = bf16[128,1024]{1,0:T(8,128)(2,1)S(1)} collective-permute-done((bf16[128,1024]{1,0:T(8,128)(2,1)S(1)}, bf16[128,1024]{1,0:T(8,128)(2,1)S(1)}, u32[]{:S(2)}, u32[]{:S(2)}) %collective-permute-start.19) | collective-permute-done | bytes 262176 | tf_op jit(solution)/shard_map/ppermute | solution.py:51
  70.7 0.0 collective-permute-start.2
  70.7 2.7 %collective-permute-start.3 = (bf16[128,1024]{1,0:T(8,128)(2,1)S(1)}, bf16[128,1024]{1,0:T(8,128)(2,1)S(1)}, u32[]{:S(2)}, u32[]{:S(2)}) collective-permute-start(bf16[128,1024]{1,0:T(8,128)(2,1)S(1)} %get-tuple-element.25), channel_id=1, source_target_pairs={{0,96},{1,97},{2,98},{3,99},{4,100},{5,101},{6,102},{7,103},{8,104... | collective-permute-start | bytes 786440 | tf_op jit(solution)/shard_map/ppermute | solution.py:51
  73.4 0.0 collective-permute-start.4
  73.4 1.5 %shard_map.59 = (f32[2,128,512]{2,1,0:T(8,128)S(1)}, f32[2,8,512]{2,1,0:T(8,128)S(1)}, f32[2,8,512]{2,1,0:T(8,128)S(1)}) custom-call(s32[4,32]{1,0:T(4,128)S(1)} %copy-done.4, s32[4,32]{1,0:T(4,128)S(1)} %copy-done.3, bf16[128,1024]{1,0:T(8,128)(2,1)S(1)} %get-tuple-element.34.refs_0_, bf16[128,1024]{1,0:T(8,128)(2,1)S(1)} %collective-permute-done.17.refs_1_, ...), custom_call_target="tpu_custom_call" | custom-call | flops 805306368 | bytes 2097152 | tf_op jit(solution)/shard_map/pallas_call | solution.py:301
  74.9 1.4 %collective-permute-done.14.refs_5_ = bf16[512,512]{1,0:T(8,128)(2,1)S(1)} collective-permute-done((bf16[512,512]{1,0:T(8,128)(2,1)S(1)}, bf16[512,512]{1,0:T(8,128)(2,1)S(1)}, u32[]{:S(2)}, u32[]{:S(2)}) %collective-permute-start.14) | collective-permute-done | bytes 524320 | tf_op jit(solution)/shard_map/ppermute | solution.py:51
  76.3 1.2 %shard_map.60 = bf16[128,1024]{1,0:T(8,128)(2,1)S(1)} custom-call(s32[4,32]{1,0:T(4,128)S(1)} %copy-done.4, s32[4,32]{1,0:T(4,128)S(1)} %copy-done.3, bf16[128,1024]{1,0:T(8,128)(2,1)S(1)} %get-tuple-element.34.refs_0_, bf16[128,1024]{1,0:T(8,128)(2,1)S(1)} %collective-permute-done.17.refs_1_, bf16[128,1024]{1,0:T(8,128)(2,1)S(1)} %collective-permute-done.18.refs_2_, ...), custom_call_target="tpu_custom_call" | custom-call | flops 268435456 | bytes 2097152 | tf_op jit(solution)/shard_map/pallas_call | solution.py:301
  77.6 10.5 %collective-permute-start.20 = (bf16[128,1024]{1,0:T(8,128)(2,1)S(1)}, bf16[128,1024]{1,0:T(8,128)(2,1)S(1)}, u32[]{:S(2)}, u32[]{:S(2)}) collective-permute-start(bf16[128,1024]{1,0:T(8,128)(2,1)S(1)} %shard_map.60), channel_id=1, source_target_pairs={{0,1},{1,0},{2,3},{3,2},{4,5},{5,4},{6,7},{7,6},{8,9},{9,8},{10,11... | collective-permute-start | bytes 786440 | tf_op jit(solution)/shard_map/ppermute | solution.py:51
  88.1 0.0 collective-permute-done.3.refs_2_
  88.1 0.0 collective-permute-done.4.refs_3_
  88.1 4.1 %shard_map.57 = (f32[2,128,512]{2,1,0:T(8,128)S(1)}, f32[2,8,512]{2,1,0:T(8,128)S(1)}, f32[2,8,512]{2,1,0:T(8,128)S(1)}) custom-call(s32[4,32]{1,0:T(4,128)S(1)} %copy-done.4, s32[4,32]{1,0:T(4,128)S(1)} %copy-done.3, bf16[128,1024]{1,0:T(8,128)(2,1)S(1)} %get-tuple-element.23.refs_0_, bf16[128,1024]{1,0:T(8,128)(2,1)S(1)} %collective-permute-done.2.refs_1_, ...), custom_call_target="tpu_custom_call" | custom-call | flops 805306368 | bytes 2097152 | tf_op jit(solution)/shard_map/pallas_call | solution.py:301
  92.2 2.9 %shard_map.58.kept_ref = bf16[128,1024]{1,0:T(8,128)(2,1)S(1)} custom-call(s32[4,32]{1,0:T(4,128)S(1)} %copy-done.4, s32[4,32]{1,0:T(4,128)S(1)} %copy-done.3, bf16[128,1024]{1,0:T(8,128)(2,1)S(1)} %get-tuple-element.23.refs_0_, bf16[128,1024]{1,0:T(8,128)(2,1)S(1)} %collective-permute-done.2.refs_1_, bf16[128,1024]{1,0:T(8,128)(2,1)S(1)} %collective-permute-done.3.refs_2_, ...), custom_call_target="tpu_custom_call" | custom-call | flops 268435456 | bytes 2097152 | tf_op jit(solution)/shard_map/pallas_call | solution.py:301
  95.1 0.0 collective-permute-done.20.received_ref
  95.1 0.8 join.1
  (15 shorter events, 0.1 us)
Async XLA Ops:
  0.0 3.2 %collective-permute-start.1 = (bf16[128,4096]{1,0:T(8,128)(2,1)}, bf16[128,4096]{1,0:T(8,128)(2,1)S(1)}, u32[]{:S(2)}, u32[]{:S(2)}) collective-permute-start(bf16[128,4096]{1,0:T(8,128)(2,1)} %bitcast.3), channel_id=1, source_target_pairs={{0,1},{1,0},{2,3},{3,2},{4,5},{5,4},{6,7},{7,6},{8,9},{9,8},{10,11... | collective-permute-start | bytes 3145736 | tf_op jit(solution)/shard_map/ppermute | solution.py:51
  0.7 2.5 %collective-permute-start = (s32[1,1]{1,0:T(1,128)}, s32[1,1]{1,0:T(1,128)}, u32[]{:S(2)}, u32[]{:S(2)}) collective-permute-start(s32[1,1]{1,0:T(1,128)} %param.7), channel_id=1, source_target_pairs={{0,1},{1,0},{2,3},{3,2},{4,5},{5,4},{6,7},{7,6},{8,9},{9,8},{10,11... | collective-permute-start | bytes 20 | tf_op jit(solution)/shard_map/ppermute | solution.py:51
  3.2 8.2 %copy-start = (bf16[4096,3072]{1,0:T(8,128)(2,1)S(1)}, bf16[4096,3072]{1,0:T(8,128)(2,1)}, u32[]{:S(2)}) copy-start(bf16[4096,3072]{1,0:T(8,128)(2,1)} %w_ref.3) | copy-start | bytes 75497472
  11.3 1.2 %copy-start.1 = (bf16[1,128,4096]{2,1,0:T(8,128)(2,1)S(1)}, bf16[1,128,4096]{2,1,0:T(8,128)(2,1)}, u32[]{:S(2)}) copy-start(bf16[1,128,4096]{2,1,0:T(8,128)(2,1)} %param.5) | copy-start | bytes 3145732
  12.6 0.7 copy-start.2
  13.2 60.1 %copy-start.3 = (s32[4,32]{1,0:T(4,128)S(1)}, s32[4,32]{1,0:T(4,128)}, u32[]{:S(2)}) copy-start(s32[4,32]{1,0:T(4,128)} %order_ref.11) | copy-start | bytes 1540
  13.2 60.1 %copy-start.4 = (s32[4,32]{1,0:T(4,128)S(1)}, s32[4,32]{1,0:T(4,128)}, u32[]{:S(2)}) copy-start(s32[4,32]{1,0:T(4,128)} %sequence_ref.7) | copy-start | bytes 1540
  17.2 8.8 %collective-permute-start.5 = (bf16[256,512]{1,0:T(8,128)(2,1)S(1)}, bf16[256,512]{1,0:T(8,128)(2,1)S(1)}, u32[]{:S(2)}, u32[]{:S(2)}) collective-permute-start(bf16[256,512]{1,0:T(8,128)(2,1)S(1)} %get-tuple-element.28), channel_id=1, source_target_pairs={{0,32},{1,33},{2,34},{3,35},{4,36},{5,37},{6,38},{7,39},{8,40},{9,... | collective-permute-start | bytes 786440 | tf_op jit(solution)/shard_map/ppermute | solution.py:51
  18.4 7.5 %collective-permute-start.6 = (bf16[256,512]{1,0:T(8,128)(2,1)S(1)}, bf16[256,512]{1,0:T(8,128)(2,1)S(1)}, u32[]{:S(2)}, u32[]{:S(2)}) collective-permute-start(bf16[256,512]{1,0:T(8,128)(2,1)S(1)} %get-tuple-element.29), channel_id=1, source_target_pairs={{0,96},{1,97},{2,98},{3,99},{4,100},{5,101},{6,102},{7,103},{8,104... | collective-permute-start | bytes 786440 | tf_op jit(solution)/shard_map/ppermute | solution.py:51
  19.9 12.6 %collective-permute-start.7 = (bf16[256,512]{1,0:T(8,128)(2,1)S(1)}, bf16[256,512]{1,0:T(8,128)(2,1)S(1)}, u32[]{:S(2)}, u32[]{:S(2)}) collective-permute-start(bf16[256,512]{1,0:T(8,128)(2,1)S(1)} %get-tuple-element.30), channel_id=1, source_target_pairs={{0,64},{1,65},{2,66},{3,67},{4,68},{5,69},{6,70},{7,71},{8,72},{9,... | collective-permute-start | bytes 786440 | tf_op jit(solution)/shard_map/ppermute | solution.py:51
  32.6 8.9 %collective-permute-start.11 = (bf16[256,512]{1,0:T(8,128)(2,1)S(1)}, bf16[256,512]{1,0:T(8,128)(2,1)S(1)}, u32[]{:S(2)}, u32[]{:S(2)}) collective-permute-start(bf16[256,512]{1,0:T(8,128)(2,1)S(1)} %add_add_fusion), channel_id=1, source_target_pairs={{0,24},{1,7},{2,26},{3,1},{4,28},{5,3},{6,30},{7,5},{8,0},{9,15},{... | collective-permute-start | bytes 786440 | tf_op jit(solution)/shard_map/ppermute | solution.py:51
  35.4 6.8 %collective-permute-start.12 = (bf16[256,512]{1,0:T(8,128)(2,1)S(1)}, bf16[256,512]{1,0:T(8,128)(2,1)S(1)}, u32[]{:S(2)}, u32[]{:S(2)}) collective-permute-start(bf16[256,512]{1,0:T(8,128)(2,1)S(1)} %add_add_fusion), channel_id=1, source_target_pairs={{0,16},{1,5},{2,18},{3,7},{4,20},{5,1},{6,22},{7,3},{8,24},{9,13},... | collective-permute-start | bytes 786440 | tf_op jit(solution)/shard_map/ppermute | solution.py:51
  35.8 9.2 %collective-permute-start.8 = (bf16[256,512]{1,0:T(8,128)(2,1)S(1)}, bf16[256,512]{1,0:T(8,128)(2,1)S(1)}, u32[]{:S(2)}, u32[]{:S(2)}) collective-permute-start(bf16[256,512]{1,0:T(8,128)(2,1)S(1)} %add_add_fusion), channel_id=1, source_target_pairs={{0,8},{1,3},{2,10},{3,5},{4,12},{5,7},{6,14},{7,1},{8,16},{9,11},{... | collective-permute-start | bytes 786440 | tf_op jit(solution)/shard_map/ppermute | solution.py:51
  42.2 19.3 %collective-permute-start.13 = (bf16[512,512]{1,0:T(8,128)(2,1)S(1)}, bf16[512,512]{1,0:T(8,128)(2,1)S(1)}, u32[]{:S(2)}, u32[]{:S(2)}) collective-permute-start(bf16[512,512]{1,0:T(8,128)(2,1)S(1)} %constant_dynamic-update-slice_fusion.refs_5_), channel_id=1, source_target_pairs={{0,6},{1,25},{2,0},{3,27},{4,2},{5,29},{6,4},{7,31},{8,14},{9,1},{... | collective-permute-start | bytes 1572872 | tf_op jit(solution)/shard_map/ppermute | solution.py:51
  45.0 17.0 %collective-permute-start.9 = (bf16[512,512]{1,0:T(8,128)(2,1)S(1)}, bf16[512,512]{1,0:T(8,128)(2,1)S(1)}, u32[]{:S(2)}, u32[]{:S(2)}) collective-permute-start(bf16[512,512]{1,0:T(8,128)(2,1)S(1)} %pad_maximum_fusion.refs_4_), channel_id=1, source_target_pairs={{0,2},{1,9},{2,4},{3,11},{4,6},{5,13},{6,0},{7,15},{8,10},{9,17},{... | collective-permute-start | bytes 1572872 | tf_op jit(solution)/shard_map/ppermute | solution.py:51
  53.4 8.2 %collective-permute-start.17 = (bf16[128,1024]{1,0:T(8,128)(2,1)S(1)}, bf16[128,1024]{1,0:T(8,128)(2,1)S(1)}, u32[]{:S(2)}, u32[]{:S(2)}) collective-permute-start(bf16[128,1024]{1,0:T(8,128)(2,1)S(1)} %get-tuple-element.35), channel_id=1, source_target_pairs={{0,32},{1,33},{2,34},{3,35},{4,36},{5,37},{6,38},{7,39},{8,40},{9,... | collective-permute-start | bytes 786440 | tf_op jit(solution)/shard_map/ppermute | solution.py:51
  54.1 9.9 %collective-permute-start.18 = (bf16[128,1024]{1,0:T(8,128)(2,1)S(1)}, bf16[128,1024]{1,0:T(8,128)(2,1)S(1)}, u32[]{:S(2)}, u32[]{:S(2)}) collective-permute-start(bf16[128,1024]{1,0:T(8,128)(2,1)S(1)} %get-tuple-element.36), channel_id=1, source_target_pairs={{0,96},{1,97},{2,98},{3,99},{4,100},{5,101},{6,102},{7,103},{8,104... | collective-permute-start | bytes 786440 | tf_op jit(solution)/shard_map/ppermute | solution.py:51
  56.2 14.5 %collective-permute-start.15 = (bf16[512,512]{1,0:T(8,128)(2,1)S(1)}, bf16[512,512]{1,0:T(8,128)(2,1)S(1)}, u32[]{:S(2)}, u32[]{:S(2)}) collective-permute-start(bf16[512,512]{1,0:T(8,128)(2,1)S(1)} %constant_dynamic-update-slice_fusion.refs_5_), channel_id=1, source_target_pairs={{0,2},{1,9},{2,4},{3,11},{4,6},{5,13},{6,0},{7,15},{8,10},{9,17},{... | collective-permute-start | bytes 1572872 | tf_op jit(solution)/shard_map/ppermute | solution.py:51
  61.6 11.8 %collective-permute-start.16 = (bf16[512,512]{1,0:T(8,128)(2,1)S(1)}, bf16[512,512]{1,0:T(8,128)(2,1)S(1)}, u32[]{:S(2)}, u32[]{:S(2)}) collective-permute-start(bf16[512,512]{1,0:T(8,128)(2,1)S(1)} %pad_maximum_fusion.refs_4_), channel_id=1, source_target_pairs={{0,6},{1,25},{2,0},{3,27},{4,2},{5,29},{6,4},{7,31},{8,14},{9,1},{... | collective-permute-start | bytes 1572872 | tf_op jit(solution)/shard_map/ppermute | solution.py:51
  61.6 14.7 %collective-permute-start.14 = (bf16[512,512]{1,0:T(8,128)(2,1)S(1)}, bf16[512,512]{1,0:T(8,128)(2,1)S(1)}, u32[]{:S(2)}, u32[]{:S(2)}) collective-permute-start(bf16[512,512]{1,0:T(8,128)(2,1)S(1)} %collective-permute-done.13.refs_8_), channel_id=1, source_target_pairs={{0,6},{1,25},{2,0},{3,27},{4,2},{5,29},{6,4},{7,31},{8,14},{9,1},{... | collective-permute-start | bytes 1572872 | tf_op jit(solution)/shard_map/ppermute | solution.py:51
  61.9 14.4 %collective-permute-start.10 = (bf16[512,512]{1,0:T(8,128)(2,1)S(1)}, bf16[512,512]{1,0:T(8,128)(2,1)S(1)}, u32[]{:S(2)}, u32[]{:S(2)}) collective-permute-start(bf16[512,512]{1,0:T(8,128)(2,1)S(1)} %collective-permute-done.9.refs_6_), channel_id=1, source_target_pairs={{0,2},{1,9},{2,4},{3,11},{4,6},{5,13},{6,0},{7,15},{8,10},{9,17},{... | collective-permute-start | bytes 1572872 | tf_op jit(solution)/shard_map/ppermute | solution.py:51
  63.9 6.7 %collective-permute-start.19 = (bf16[128,1024]{1,0:T(8,128)(2,1)S(1)}, bf16[128,1024]{1,0:T(8,128)(2,1)S(1)}, u32[]{:S(2)}, u32[]{:S(2)}) collective-permute-start(bf16[128,1024]{1,0:T(8,128)(2,1)S(1)} %get-tuple-element.37), channel_id=1, source_target_pairs={{0,64},{1,65},{2,66},{3,67},{4,68},{5,69},{6,70},{7,71},{8,72},{9,... | collective-permute-start | bytes 786440 | tf_op jit(solution)/shard_map/ppermute | solution.py:51
  70.7 17.4 %collective-permute-start.2 = (bf16[128,1024]{1,0:T(8,128)(2,1)S(1)}, bf16[128,1024]{1,0:T(8,128)(2,1)S(1)}, u32[]{:S(2)}, u32[]{:S(2)}) collective-permute-start(bf16[128,1024]{1,0:T(8,128)(2,1)S(1)} %get-tuple-element.24), channel_id=1, source_target_pairs={{0,32},{1,33},{2,34},{3,35},{4,36},{5,37},{6,38},{7,39},{8,40},{9,... | collective-permute-start | bytes 786440 | tf_op jit(solution)/shard_map/ppermute | solution.py:51
  70.7 17.4 %collective-permute-start.3 = (bf16[128,1024]{1,0:T(8,128)(2,1)S(1)}, bf16[128,1024]{1,0:T(8,128)(2,1)S(1)}, u32[]{:S(2)}, u32[]{:S(2)}) collective-permute-start(bf16[128,1024]{1,0:T(8,128)(2,1)S(1)} %get-tuple-element.25), channel_id=1, source_target_pairs={{0,96},{1,97},{2,98},{3,99},{4,100},{5,101},{6,102},{7,103},{8,104... | collective-permute-start | bytes 786440 | tf_op jit(solution)/shard_map/ppermute | solution.py:51
  73.4 14.7 %collective-permute-start.4 = (bf16[128,1024]{1,0:T(8,128)(2,1)S(1)}, bf16[128,1024]{1,0:T(8,128)(2,1)S(1)}, u32[]{:S(2)}, u32[]{:S(2)}) collective-permute-start(bf16[128,1024]{1,0:T(8,128)(2,1)S(1)} %get-tuple-element.26), channel_id=1, source_target_pairs={{0,64},{1,65},{2,66},{3,67},{4,68},{5,69},{6,70},{7,71},{8,72},{9,... | collective-permute-start | bytes 786440 | tf_op jit(solution)/shard_map/ppermute | solution.py:51
  77.6 17.5 %collective-permute-start.20 = (bf16[128,1024]{1,0:T(8,128)(2,1)S(1)}, bf16[128,1024]{1,0:T(8,128)(2,1)S(1)}, u32[]{:S(2)}, u32[]{:S(2)}) collective-permute-start(bf16[128,1024]{1,0:T(8,128)(2,1)S(1)} %shard_map.60), channel_id=1, source_target_pairs={{0,1},{1,0},{2,3},{3,2},{4,5},{5,4},{6,7},{7,6},{8,9},{9,8},{10,11... | collective-permute-start | bytes 786440 | tf_op jit(solution)/shard_map/ppermute | solution.py:51
where the time goes:
time: 96.2 us; the launch traced here: 95.9 us
  waiting for transfers between devices  33.5 us (35%)
  starting transfers between devices  30.2 us (31%)
  Pallas kernels  21.2 us (22%)
  local copies, waits for them, and re-layouts  10.1 us (10%)
    ppermute x21, waiting for transfers between devices, permute(): return lax.ppermute(value, AXES, table)  33.5 us
    ppermute x21, starting transfers between devices, permute(): return lax.ppermute(value, AXES, table)  30.2 us
    pallas_call x2, Pallas kernels, project(): pl.pallas_call(kernel, grid_spec=pltpu.PrefetchScalarGridSpec(num_scalar_...  10.6 us
    unnamed x11, local copies, waits for them, and re-layouts  10.1 us
    pallas_call x4, Pallas kernels, attend(): pl.pallas_call(functools.partial(attend_kernel, spots, t, first, last), i...  9.74 us
  transfers between devices with their start and end apart: 21, of which 9 were waited for; matrix products, arithmetic and copies ran while one was open for 0% of the time, Pallas kernels for 17%

commit v1 on v0

--- a/solution.py
+++ b/solution.py
@@ -128,6 +128,10 @@
 
 def in_vmem(value):
     return pltpu.with_memory_space_constraint(value, pltpu.VMEM)
+
+
+def in_hbm(value):
+    return pltpu.with_memory_space_constraint(value, pltpu.HBM)
 
 
 def project(kernel, core, owners, slab_order, others, rows, weight, block, blocks, width, out):
@@ -143,7 +147,7 @@
                 smem,
                 smem,
                 pl.BlockSpec(memory_space=pltpu.VMEM),
-                pl.BlockSpec(memory_space=pltpu.VMEM),
+                pl.BlockSpec((SLAB, depth), lambda j, c: (0, 0)),
                 pl.BlockSpec((depth, width), lambda j, c: (0, block(j, c[0]))),
             ],
             out_specs=[pl.BlockSpec((o.shape[0], width), lambda j, c: (0, j)) for o in out],
@@ -158,7 +162,7 @@
             bytes_accessed=2 * depth * (2 * SLAB + blocks * width),
             transcendentals=0,
         ),
-    )(core, *owners, slab_order, in_vmem(others), in_vmem(rows), weight)
+    )(core, *owners, in_hbm(slab_order), in_vmem(others), in_hbm(rows), in_hbm(weight))
 
 
 FACTOR = HD**-0.5 * 1.4426950408889634
@@ -310,7 +314,7 @@
             bytes_accessed=2 << 20,
             transcendentals=0,
         ),
-    )(slab_sequence, slab_order, *operands)
+    )(in_hbm(slab_sequence), in_hbm(slab_order), *operands)
 
 
 def join_kernel(core_ref, kept_ref, received_ref, out_ref):
@@ -343,7 +347,7 @@
         [jax.ShapeDtypeStruct((2 * SLAB, 4 * HD), jnp.bfloat16)] * 4,
     )
     queries = project(
-        q_kernel, *common, lambda j, c: 4 * c + j, 4, 2 * HD,
+        q_kernel, *common, lambda j, c: 2 * c + j, 2, 4 * HD,
         [jax.ShapeDtypeStruct((SLAB, HALF), jnp.bfloat16)] * 8,
     )
     moved = [permute(kv[k], shift_x(k)) for k in (1, 3, 2)]
@@ -356,9 +360,11 @@
     left = [permute(v, shift_second(1)) for v in (low, high)]
     right = [permute(v, shift_second(3)) for v in (high, low)]
     far = [permute(left[0], shift_second(1)), permute(right[0], shift_second(3))]
-    near = [low, high, *left, *right]
     tables = (slab_sequence, slab_order)
-    state = [attend(LOCAL + NEAR, t, *tables, parts[t], near, None, False) for t in range(2)]
+    state = [None, None]
+    for spots, pieces in ((LOCAL, [low, high]), (NEAR, left + right)):
+        for t in range(2):
+            state[t] = attend(spots, t, *tables, parts[t], pieces, state[t], False)
     (sent,) = attend(FAR, 0, *tables, parts[0], far, state[0], True)
     received = permute(sent, OTHER_CORE)
     (kept,) = attend(FAR, 1, *tables, parts[1], far, state[1], True)

time: 96.2 us -> 90.1 us (0.937)
  local copies, waits for them, and re-layouts: 10.1 us -> 0.04 us
  Pallas kernels: 21.2 us -> 24.9 us
  starting transfers between devices: 30.2 us -> 31.6 us
  waiting for transfers between devices: 33.5 us -> 32.3 us
    unnamed x11 -> x1, local copies, waits for them, and re-layouts: 10.1 us -> 0.02 us
    pallas_call x4 -> x6, Pallas kernels: 9.74 us -> 11.9 us  [attend(): pl.pallas_call(functools.partial(attend_kernel, spots, t, first, last), i...]
    pallas_call x2, Pallas kernels: 10.6 us -> 12.2 us  [project(): pl.pallas_call(kernel, grid_spec=pltpu.PrefetchScalarGridSpec(num_scalar_...]
    ppermute x21, starting transfers between devices: 30.2 us -> 31.6 us  [permute(): return lax.ppermute(value, AXES, table)]
    ppermute x21, waiting for transfers between devices: 33.5 us -> 32.3 us  [permute(): return lax.ppermute(value, AXES, table)]
  transfers between devices with their start and end apart: 21 -> 21, of which waited for: 9 -> 9; matrix products, arithmetic and copies ran while one was open for 0% -> 0% of each run, Pallas kernels for 17% -> 21%
where the time goes in v1:
time: 90.1 us; the launch traced here: 89.8 us
  waiting for transfers between devices  32.3 us (36%)
  starting transfers between devices  31.6 us (35%)
  Pallas kernels  24.9 us (28%)
    ppermute x21, waiting for transfers between devices, permute(): return lax.ppermute(value, AXES, table)  32.3 us
    ppermute x21, starting transfers between devices, permute(): return lax.ppermute(value, AXES, table)  31.6 us
    pallas_call x2, Pallas kernels, project(): pl.pallas_call(kernel, grid_spec=pltpu.PrefetchScalarGridSpec(num_scalar_...  12.2 us
    pallas_call x6, Pallas kernels, attend(): pl.pallas_call(functools.partial(attend_kernel, spots, t, first, last), i...  11.9 us
  transfers between devices with their start and end apart: 21, of which 9 were waited for; matrix products, arithmetic and copies ran while one was open for 0% of the time, Pallas kernels for 21%

profile of v1, /device:TPU:33, one launch (start us, length us, event | category | flops | bytes accessed | tf_op | source)
XLA Modules:
  0.0 89.8 jit_solution(1942685158882046166)
XLA Ops:
  0.0 0.7 collective-permute-start.1
  0.7 0.0 collective-permute-start
  1.3 1.8 %collective-permute-done.other_ref = s32[1,1]{1,0:T(1,128)} collective-permute-done((s32[1,1]{1,0:T(1,128)}, s32[1,1]{1,0:T(1,128)}, u32[]{:S(2)}, u32[]{:S(2)}) %collective-permute-start) | collective-permute-done | bytes 36 | tf_op jit(solution)/shard_map/ppermute | solution.py:51
  3.2 0.0 collective-permute-done.1.y_ref
  3.2 5.0 %shard_map.56 = (bf16[256,512]{1,0:T(8,128)(2,1)S(1)}, bf16[256,512]{1,0:T(8,128)(2,1)S(1)}, bf16[256,512]{1,0:T(8,128)(2,1)S(1)}, bf16[256,512]{1,0:T(8,128)(2,1)S(1)}) custom-call(s32[1]{0:T(128)} %bitcast.core_ref, s32[1,1]{1,0:T(1,128)} %collective-permute-done.other_ref, s32[1,1]{1,0:T(1,128)S(6)} %copy.7.owner_ref, s32[4,32]{1,0:T(4,128)} %order_ref.15, ...), custom_call_target="tpu_custom_call" | custom-call | flops 1073741824 | bytes 6291456 | tf_op jit(solution)/shard_map/pallas_call | solution.py:140
  8.2 1.3 %collective-permute-start.5 = (bf16[256,512]{1,0:T(8,128)(2,1)S(1)}, bf16[256,512]{1,0:T(8,128)(2,1)S(1)}, u32[]{:S(2)}, u32[]{:S(2)}) collective-permute-start(bf16[256,512]{1,0:T(8,128)(2,1)S(1)} %get-tuple-element.34), channel_id=1, source_target_pairs={{0,32},{1,33},{2,34},{3,35},{4,36},{5,37},{6,38},{7,39},{8,40},{9,... | collective-permute-start | bytes 786440 | tf_op jit(solution)/shard_map/ppermute | solution.py:51
  9.5 1.5 %collective-permute-start.6 = (bf16[256,512]{1,0:T(8,128)(2,1)S(1)}, bf16[256,512]{1,0:T(8,128)(2,1)S(1)}, u32[]{:S(2)}, u32[]{:S(2)}) collective-permute-start(bf16[256,512]{1,0:T(8,128)(2,1)S(1)} %get-tuple-element.35), channel_id=1, source_target_pairs={{0,96},{1,97},{2,98},{3,99},{4,100},{5,101},{6,102},{7,103},{8,104... | collective-permute-start | bytes 786440 | tf_op jit(solution)/shard_map/ppermute | solution.py:51
  10.9 1.5 %collective-permute-start.7 = (bf16[256,512]{1,0:T(8,128)(2,1)S(1)}, bf16[256,512]{1,0:T(8,128)(2,1)S(1)}, u32[]{:S(2)}, u32[]{:S(2)}) collective-permute-start(bf16[256,512]{1,0:T(8,128)(2,1)S(1)} %get-tuple-element.36), channel_id=1, source_target_pairs={{0,64},{1,65},{2,66},{3,67},{4,68},{5,69},{6,70},{7,71},{8,72},{9,... | collective-permute-start | bytes 786440 | tf_op jit(solution)/shard_map/ppermute | solution.py:51
  12.5 4.5 %collective-permute-done.5 = bf16[256,512]{1,0:T(8,128)(2,1)S(1)} collective-permute-done((bf16[256,512]{1,0:T(8,128)(2,1)S(1)}, bf16[256,512]{1,0:T(8,128)(2,1)S(1)}, u32[]{:S(2)}, u32[]{:S(2)}) %collective-permute-start.5) | collective-permute-done | bytes 262176 | tf_op jit(solution)/shard_map/ppermute | solution.py:51
  16.9 0.0 collective-permute-done.6
  16.9 6.6 %collective-permute-done.7 = bf16[256,512]{1,0:T(8,128)(2,1)S(1)} collective-permute-done((bf16[256,512]{1,0:T(8,128)(2,1)S(1)}, bf16[256,512]{1,0:T(8,128)(2,1)S(1)}, u32[]{:S(2)}, u32[]{:S(2)}) %collective-permute-start.7) | collective-permute-done | bytes 262176 | tf_op jit(solution)/shard_map/ppermute | solution.py:51
  23.5 0.1 add_add_fusion
  23.6 2.8 %collective-permute-start.11 = (bf16[256,512]{1,0:T(8,128)(2,1)S(1)}, bf16[256,512]{1,0:T(8,128)(2,1)S(1)}, u32[]{:S(2)}, u32[]{:S(2)}) collective-permute-start(bf16[256,512]{1,0:T(8,128)(2,1)S(1)} %add_add_fusion), channel_id=1, source_target_pairs={{0,24},{1,7},{2,26},{3,1},{4,28},{5,3},{6,30},{7,5},{8,0},{9,15},{... | collective-permute-start | bytes 786440 | tf_op jit(solution)/shard_map/ppermute | solution.py:51
  26.4 0.3 collective-permute-start.12
  26.8 0.7 collective-permute-start.8
  27.4 5.1 %collective-permute-done.11 = bf16[256,512]{1,0:T(8,128)(2,1)S(1)} collective-permute-done((bf16[256,512]{1,0:T(8,128)(2,1)S(1)}, bf16[256,512]{1,0:T(8,128)(2,1)S(1)}, u32[]{:S(2)}, u32[]{:S(2)}) %collective-permute-start.11) | collective-permute-done | bytes 262176 | tf_op jit(solution)/shard_map/ppermute | solution.py:51
  32.6 0.7 collective-permute-done.12
  33.3 0.1 collective-permute-start.13
  33.3 2.6 %collective-permute-done.8 = bf16[256,512]{1,0:T(8,128)(2,1)S(1)} collective-permute-done((bf16[256,512]{1,0:T(8,128)(2,1)S(1)}, bf16[256,512]{1,0:T(8,128)(2,1)S(1)}, u32[]{:S(2)}, u32[]{:S(2)}) %collective-permute-start.8) | collective-permute-done | bytes 262176 | tf_op jit(solution)/shard_map/ppermute | solution.py:51
  36.0 1.7 %collective-permute-start.9 = (bf16[512,512]{1,0:T(8,128)(2,1)S(1)}, bf16[512,512]{1,0:T(8,128)(2,1)S(1)}, u32[]{:S(2)}, u32[]{:S(2)}) collective-permute-start(bf16[512,512]{1,0:T(8,128)(2,1)S(1)} %pad_maximum_fusion.refs_4_), channel_id=1, source_target_pairs={{0,2},{1,9},{2,4},{3,11},{4,6},{5,13},{6,0},{7,15},{8,10},{9,17},{... | collective-permute-start | bytes 1572872 | tf_op jit(solution)/shard_map/ppermute | solution.py:51
  37.7 7.2 %shard_map.55 = (bf16[128,1024]{1,0:T(8,128)(2,1)S(1)}, bf16[128,1024]{1,0:T(8,128)(2,1)S(1)}, bf16[128,1024]{1,0:T(8,128)(2,1)S(1)}, bf16[128,1024]{1,0:T(8,128...) custom-call(s32[1]{0:T(128)} %bitcast.core_ref, ...), custom_call_target="tpu_custom_call" | custom-call | flops 2147483648 | bytes 10485760 | tf_op jit(solution)/shard_map/pallas_call | solution.py:140
  44.9 0.7 collective-permute-start.17
  45.5 2.1 %collective-permute-start.18 = (bf16[128,1024]{1,0:T(8,128)(2,1)S(1)}, bf16[128,1024]{1,0:T(8,128)(2,1)S(1)}, u32[]{:S(2)}, u32[]{:S(2)}) collective-permute-start(bf16[128,1024]{1,0:T(8,128)(2,1)S(1)} %get-tuple-element.45), channel_id=1, source_target_pairs={{0,96},{1,97},{2,98},{3,99},{4,100},{5,101},{6,102},{7,103},{8,104... | collective-permute-start | bytes 786440 | tf_op jit(solution)/shard_map/ppermute | solution.py:51
  47.6 1.3 %collective-permute-start.15 = (bf16[512,512]{1,0:T(8,128)(2,1)S(1)}, bf16[512,512]{1,0:T(8,128)(2,1)S(1)}, u32[]{:S(2)}, u32[]{:S(2)}) collective-permute-start(bf16[512,512]{1,0:T(8,128)(2,1)S(1)} %constant_dynamic-update-slice_fusion.refs_5_), channel_id=1, source_target_pairs={{0,2},{1,9},{2,4},{3,11},{4,6},{5,13},{6,0},{7,15},{8,10},{9,17},{... | collective-permute-start | bytes 1572872 | tf_op jit(solution)/shard_map/ppermute | solution.py:51
  49.0 4.0 %collective-permute-done.17.refs_1_ = bf16[128,1024]{1,0:T(8,128)(2,1)S(1)} collective-permute-done((bf16[128,1024]{1,0:T(8,128)(2,1)S(1)}, bf16[128,1024]{1,0:T(8,128)(2,1)S(1)}, u32[]{:S(2)}, u32[]{:S(2)}) %collective-permute-start.17) | collective-permute-done | bytes 262176 | tf_op jit(solution)/shard_map/ppermute | solution.py:51
  53.0 0.0 collective-permute-start.16
  53.0 0.0 collective-permute-done.13.refs_6_
  53.0 0.4 collective-permute-start.14
  53.4 0.0 collective-permute-done.9.refs_4_
  53.4 1.9 %collective-permute-start.10 = (bf16[512,512]{1,0:T(8,128)(2,1)S(1)}, bf16[512,512]{1,0:T(8,128)(2,1)S(1)}, u32[]{:S(2)}, u32[]{:S(2)}) collective-permute-start(bf16[512,512]{1,0:T(8,128)(2,1)S(1)} %collective-permute-done.9.refs_4_), channel_id=1, source_target_pairs={{0,2},{1,9},{2,4},{3,11},{4,6},{5,13},{6,0},{7,15},{8,10},{9,17},{... | collective-permute-start | bytes 1572872 | tf_op jit(solution)/shard_map/ppermute | solution.py:51
  55.3 0.0 collective-permute-done.18.refs_2_
  55.3 6.7 %collective-permute-done.19.refs_3_ = bf16[128,1024]{1,0:T(8,128)(2,1)S(1)} collective-permute-done((bf16[128,1024]{1,0:T(8,128)(2,1)S(1)}, bf16[128,1024]{1,0:T(8,128)(2,1)S(1)}, u32[]{:S(2)}, u32[]{:S(2)}) %collective-permute-start.19) | collective-permute-done | bytes 262176 | tf_op jit(solution)/shard_map/ppermute | solution.py:51
  62.1 0.0 collective-permute-done.15.refs_5_
  62.1 2.7 %collective-permute-start.3 = (bf16[128,1024]{1,0:T(8,128)(2,1)S(1)}, bf16[128,1024]{1,0:T(8,128)(2,1)S(1)}, u32[]{:S(2)}, u32[]{:S(2)}) collective-permute-start(bf16[128,1024]{1,0:T(8,128)(2,1)S(1)} %get-tuple-element.31), channel_id=1, source_target_pairs={{0,96},{1,97},{2,98},{3,99},{4,100},{5,101},{6,102},{7,103},{8,104... | collective-permute-start | bytes 786440 | tf_op jit(solution)/shard_map/ppermute | solution.py:51
  64.8 0.0 collective-permute-done.16.refs_7_
  64.8 0.0 collective-permute-start.4
  64.8 1.4 %shard_map.60 = (f32[2,128,512]{2,1,0:T(8,128)S(1)}, f32[2,8,512]{2,1,0:T(8,128)S(1)}, f32[2,8,512]{2,1,0:T(8,128)S(1)}) custom-call(s32[4,32]{1,0:T(4,128)} %sequence_ref.11, s32[4,32]{1,0:T(4,128)} %order_ref.15, bf16[128,1024]{1,0:T(8,128)(2,1)S(1)} %get-tuple-element.43.refs_0_, bf16[128,1024]{1,0:T(8,128)(2,1)S(1)} %collective-permute-done.17.refs_1_, ...), custom_call_target="tpu_custom_call" | custom-call | flops 268435456 | bytes 2097152 | tf_op jit(solution)/shard_map/pallas_call | solution.py:305
  66.1 1.3 %shard_map.61 = (f32[2,128,512]{2,1,0:T(8,128)S(1)}, f32[2,8,512]{2,1,0:T(8,128)S(1)}, f32[2,8,512]{2,1,0:T(8,128)S(1)}) custom-call(s32[4,32]{1,0:T(4,128)} %sequence_ref.11, s32[4,32]{1,0:T(4,128)} %order_ref.15, bf16[128,1024]{1,0:T(8,128)(2,1)S(1)} %get-tuple-element.43.refs_0_, bf16[128,1024]{1,0:T(8,128)(2,1)S(1)} %collective-permute-done.17.refs_1_, ...), custom_call_target="tpu_custom_call" | custom-call | flops 536870912 | bytes 2097152 | tf_op jit(solution)/shard_map/pallas_call | solution.py:305
  67.5 0.3 collective-permute-done.14.refs_5_
  67.7 0.0 collective-permute-done.10.refs_4_
  67.7 1.1 %shard_map.62 = bf16[128,1024]{1,0:T(8,128)(2,1)S(1)} custom-call(s32[4,32]{1,0:T(4,128)} %sequence_ref.11, s32[4,32]{1,0:T(4,128)} %order_ref.15, bf16[128,1024]{1,0:T(8,128)(2,1)S(1)} %get-tuple-element.43.refs_0_, bf16[128,1024]{1,0:T(8,128)(2,1)S(1)} %collective-permute-done.17.refs_1_, bf16[128,1024]{1,0:T(8,128)(2,1)S(1)} %collective-permute-done.18.refs_2_, ...), custom_call_target="tpu_custom_call" | custom-call | flops 268435456 | bytes 2097152 | tf_op jit(solution)/shard_map/pallas_call | solution.py:305
  68.9 11.9 %collective-permute-start.20 = (bf16[128,1024]{1,0:T(8,128)(2,1)S(1)}, bf16[128,1024]{1,0:T(8,128)(2,1)S(1)}, u32[]{:S(2)}, u32[]{:S(2)}) collective-permute-start(bf16[128,1024]{1,0:T(8,128)(2,1)S(1)} %shard_map.62), channel_id=1, source_target_pairs={{0,1},{1,0},{2,3},{3,2},{4,5},{5,4},{6,7},{7,6},{8,9},{9,8},{10,11... | collective-permute-start | bytes 786440 | tf_op jit(solution)/shard_map/ppermute | solution.py:51
  80.8 0.0 collective-permute-done.4.refs_3_
  80.8 2.7 %shard_map.57 = (f32[2,128,512]{2,1,0:T(8,128)S(1)}, f32[2,8,512]{2,1,0:T(8,128)S(1)}, f32[2,8,512]{2,1,0:T(8,128)S(1)}) custom-call(s32[4,32]{1,0:T(4,128)} %sequence_ref.11, s32[4,32]{1,0:T(4,128)} %order_ref.15, bf16[128,1024]{1,0:T(8,128)(2,1)S(1)} %get-tuple-element.29.refs_0_, bf16[128,1024]{1,0:T(8,128)(2,1)S(1)} %collective-permute-done.2.refs_1_, ...), custom_call_target="tpu_custom_call" | custom-call | flops 268435456 | bytes 2097152 | tf_op jit(solution)/shard_map/pallas_call | solution.py:305
  83.5 2.4 %shard_map.58 = (f32[2,128,512]{2,1,0:T(8,128)S(1)}, f32[2,8,512]{2,1,0:T(8,128)S(1)}, f32[2,8,512]{2,1,0:T(8,128)S(1)}) custom-call(s32[4,32]{1,0:T(4,128)} %sequence_ref.11, s32[4,32]{1,0:T(4,128)} %order_ref.15, bf16[128,1024]{1,0:T(8,128)(2,1)S(1)} %get-tuple-element.29.refs_0_, bf16[128,1024]{1,0:T(8,128)(2,1)S(1)} %collective-permute-done.2.refs_1_, ...), custom_call_target="tpu_custom_call" | custom-call | flops 536870912 | bytes 2097152 | tf_op jit(solution)/shard_map/pallas_call | solution.py:305
  85.9 3.0 %shard_map.59.kept_ref = bf16[128,1024]{1,0:T(8,128)(2,1)S(1)} custom-call(s32[4,32]{1,0:T(4,128)} %sequence_ref.11, s32[4,32]{1,0:T(4,128)} %order_ref.15, bf16[128,1024]{1,0:T(8,128)(2,1)S(1)} %get-tuple-element.29.refs_0_, bf16[128,1024]{1,0:T(8,128)(2,1)S(1)} %collective-permute-done.2.refs_1_, bf16[128,1024]{1,0:T(8,128)(2,1)S(1)} %collective-permute-done.3.refs_2_, ...), custom_call_target="tpu_custom_call" | custom-call | flops 268435456 | bytes 2097152 | tf_op jit(solution)/shard_map/pallas_call | solution.py:305
  88.9 0.0 collective-permute-done.20.received_ref
  88.9 0.8 join.1
  (7 shorter events, 0.1 us)
Async XLA Ops:
  0.0 3.2 %collective-permute-start.1 = (bf16[128,4096]{1,0:T(8,128)(2,1)}, bf16[128,4096]{1,0:T(8,128)(2,1)S(1)}, u32[]{:S(2)}, u32[]{:S(2)}) collective-permute-start(bf16[128,4096]{1,0:T(8,128)(2,1)} %bitcast.3), channel_id=1, source_target_pairs={{0,1},{1,0},{2,3},{3,2},{4,5},{5,4},{6,7},{7,6},{8,9},{9,8},{10,11... | collective-permute-start | bytes 3145736 | tf_op jit(solution)/shard_map/ppermute | solution.py:51
  0.7 2.5 %collective-permute-start = (s32[1,1]{1,0:T(1,128)}, s32[1,1]{1,0:T(1,128)}, u32[]{:S(2)}, u32[]{:S(2)}) collective-permute-start(s32[1,1]{1,0:T(1,128)} %param.7), channel_id=1, source_target_pairs={{0,1},{1,0},{2,3},{3,2},{4,5},{5,4},{6,7},{7,6},{8,9},{9,8},{10,11... | collective-permute-start | bytes 20 | tf_op jit(solution)/shard_map/ppermute | solution.py:51
  8.2 8.8 %collective-permute-start.5 = (bf16[256,512]{1,0:T(8,128)(2,1)S(1)}, bf16[256,512]{1,0:T(8,128)(2,1)S(1)}, u32[]{:S(2)}, u32[]{:S(2)}) collective-permute-start(bf16[256,512]{1,0:T(8,128)(2,1)S(1)} %get-tuple-element.34), channel_id=1, source_target_pairs={{0,32},{1,33},{2,34},{3,35},{4,36},{5,37},{6,38},{7,39},{8,40},{9,... | collective-permute-start | bytes 786440 | tf_op jit(solution)/shard_map/ppermute | solution.py:51
  9.5 7.5 %collective-permute-start.6 = (bf16[256,512]{1,0:T(8,128)(2,1)S(1)}, bf16[256,512]{1,0:T(8,128)(2,1)S(1)}, u32[]{:S(2)}, u32[]{:S(2)}) collective-permute-start(bf16[256,512]{1,0:T(8,128)(2,1)S(1)} %get-tuple-element.35), channel_id=1, source_target_pairs={{0,96},{1,97},{2,98},{3,99},{4,100},{5,101},{6,102},{7,103},{8,104... | collective-permute-start | bytes 786440 | tf_op jit(solution)/shard_map/ppermute | solution.py:51
  10.9 12.6 %collective-permute-start.7 = (bf16[256,512]{1,0:T(8,128)(2,1)S(1)}, bf16[256,512]{1,0:T(8,128)(2,1)S(1)}, u32[]{:S(2)}, u32[]{:S(2)}) collective-permute-start(bf16[256,512]{1,0:T(8,128)(2,1)S(1)} %get-tuple-element.36), channel_id=1, source_target_pairs={{0,64},{1,65},{2,66},{3,67},{4,68},{5,69},{6,70},{7,71},{8,72},{9,... | collective-permute-start | bytes 786440 | tf_op jit(solution)/shard_map/ppermute | solution.py:51
  23.6 8.9 %collective-permute-start.11 = (bf16[256,512]{1,0:T(8,128)(2,1)S(1)}, bf16[256,512]{1,0:T(8,128)(2,1)S(1)}, u32[]{:S(2)}, u32[]{:S(2)}) collective-permute-start(bf16[256,512]{1,0:T(8,128)(2,1)S(1)} %add_add_fusion), channel_id=1, source_target_pairs={{0,24},{1,7},{2,26},{3,1},{4,28},{5,3},{6,30},{7,5},{8,0},{9,15},{... | collective-permute-start | bytes 786440 | tf_op jit(solution)/shard_map/ppermute | solution.py:51
  26.4 6.8 %collective-permute-start.12 = (bf16[256,512]{1,0:T(8,128)(2,1)S(1)}, bf16[256,512]{1,0:T(8,128)(2,1)S(1)}, u32[]{:S(2)}, u32[]{:S(2)}) collective-permute-start(bf16[256,512]{1,0:T(8,128)(2,1)S(1)} %add_add_fusion), channel_id=1, source_target_pairs={{0,16},{1,5},{2,18},{3,7},{4,20},{5,1},{6,22},{7,3},{8,24},{9,13},... | collective-permute-start | bytes 786440 | tf_op jit(solution)/shard_map/ppermute | solution.py:51
  26.8 9.2 %collective-permute-start.8 = (bf16[256,512]{1,0:T(8,128)(2,1)S(1)}, bf16[256,512]{1,0:T(8,128)(2,1)S(1)}, u32[]{:S(2)}, u32[]{:S(2)}) collective-permute-start(bf16[256,512]{1,0:T(8,128)(2,1)S(1)} %add_add_fusion), channel_id=1, source_target_pairs={{0,8},{1,3},{2,10},{3,5},{4,12},{5,7},{6,14},{7,1},{8,16},{9,11},{... | collective-permute-start | bytes 786440 | tf_op jit(solution)/shard_map/ppermute | solution.py:51
  33.3 19.7 %collective-permute-start.13 = (bf16[512,512]{1,0:T(8,128)(2,1)S(1)}, bf16[512,512]{1,0:T(8,128)(2,1)S(1)}, u32[]{:S(2)}, u32[]{:S(2)}) collective-permute-start(bf16[512,512]{1,0:T(8,128)(2,1)S(1)} %constant_dynamic-update-slice_fusion.refs_5_), channel_id=1, source_target_pairs={{0,6},{1,25},{2,0},{3,27},{4,2},{5,29},{6,4},{7,31},{8,14},{9,1},{... | collective-permute-start | bytes 1572872 | tf_op jit(solution)/shard_map/ppermute | solution.py:51
  36.0 17.4 %collective-permute-start.9 = (bf16[512,512]{1,0:T(8,128)(2,1)S(1)}, bf16[512,512]{1,0:T(8,128)(2,1)S(1)}, u32[]{:S(2)}, u32[]{:S(2)}) collective-permute-start(bf16[512,512]{1,0:T(8,128)(2,1)S(1)} %pad_maximum_fusion.refs_4_), channel_id=1, source_target_pairs={{0,2},{1,9},{2,4},{3,11},{4,6},{5,13},{6,0},{7,15},{8,10},{9,17},{... | collective-permute-start | bytes 1572872 | tf_op jit(solution)/shard_map/ppermute | solution.py:51
  44.9 8.1 %collective-permute-start.17 = (bf16[128,1024]{1,0:T(8,128)(2,1)S(1)}, bf16[128,1024]{1,0:T(8,128)(2,1)S(1)}, u32[]{:S(2)}, u32[]{:S(2)}) collective-permute-start(bf16[128,1024]{1,0:T(8,128)(2,1)S(1)} %get-tuple-element.44), channel_id=1, source_target_pairs={{0,32},{1,33},{2,34},{3,35},{4,36},{5,37},{6,38},{7,39},{8,40},{9,... | collective-permute-start | bytes 786440 | tf_op jit(solution)/shard_map/ppermute | solution.py:51
  45.5 9.8 %collective-permute-start.18 = (bf16[128,1024]{1,0:T(8,128)(2,1)S(1)}, bf16[128,1024]{1,0:T(8,128)(2,1)S(1)}, u32[]{:S(2)}, u32[]{:S(2)}) collective-permute-start(bf16[128,1024]{1,0:T(8,128)(2,1)S(1)} %get-tuple-element.45), channel_id=1, source_target_pairs={{0,96},{1,97},{2,98},{3,99},{4,100},{5,101},{6,102},{7,103},{8,104... | collective-permute-start | bytes 786440 | tf_op jit(solution)/shard_map/ppermute | solution.py:51
  47.6 14.5 %collective-permute-start.15 = (bf16[512,512]{1,0:T(8,128)(2,1)S(1)}, bf16[512,512]{1,0:T(8,128)(2,1)S(1)}, u32[]{:S(2)}, u32[]{:S(2)}) collective-permute-start(bf16[512,512]{1,0:T(8,128)(2,1)S(1)} %constant_dynamic-update-slice_fusion.refs_5_), channel_id=1, source_target_pairs={{0,2},{1,9},{2,4},{3,11},{4,6},{5,13},{6,0},{7,15},{8,10},{9,17},{... | collective-permute-start | bytes 1572872 | tf_op jit(solution)/shard_map/ppermute | solution.py:51
  53.0 11.8 %collective-permute-start.16 = (bf16[512,512]{1,0:T(8,128)(2,1)S(1)}, bf16[512,512]{1,0:T(8,128)(2,1)S(1)}, u32[]{:S(2)}, u32[]{:S(2)}) collective-permute-start(bf16[512,512]{1,0:T(8,128)(2,1)S(1)} %pad_maximum_fusion.refs_4_), channel_id=1, source_target_pairs={{0,6},{1,25},{2,0},{3,27},{4,2},{5,29},{6,4},{7,31},{8,14},{9,1},{... | collective-permute-start | bytes 1572872 | tf_op jit(solution)/shard_map/ppermute | solution.py:51
  53.0 14.8 %collective-permute-start.14 = (bf16[512,512]{1,0:T(8,128)(2,1)S(1)}, bf16[512,512]{1,0:T(8,128)(2,1)S(1)}, u32[]{:S(2)}, u32[]{:S(2)}) collective-permute-start(bf16[512,512]{1,0:T(8,128)(2,1)S(1)} %collective-permute-done.13.refs_6_), channel_id=1, source_target_pairs={{0,6},{1,25},{2,0},{3,27},{4,2},{5,29},{6,4},{7,31},{8,14},{9,1},{... | collective-permute-start | bytes 1572872 | tf_op jit(solution)/shard_map/ppermute | solution.py:51
  53.4 14.3 %collective-permute-start.10 = (bf16[512,512]{1,0:T(8,128)(2,1)S(1)}, bf16[512,512]{1,0:T(8,128)(2,1)S(1)}, u32[]{:S(2)}, u32[]{:S(2)}) collective-permute-start(bf16[512,512]{1,0:T(8,128)(2,1)S(1)} %collective-permute-done.9.refs_4_), channel_id=1, source_target_pairs={{0,2},{1,9},{2,4},{3,11},{4,6},{5,13},{6,0},{7,15},{8,10},{9,17},{... | collective-permute-start | bytes 1572872 | tf_op jit(solution)/shard_map/ppermute | solution.py:51
  55.3 6.7 %collective-permute-start.19 = (bf16[128,1024]{1,0:T(8,128)(2,1)S(1)}, bf16[128,1024]{1,0:T(8,128)(2,1)S(1)}, u32[]{:S(2)}, u32[]{:S(2)}) collective-permute-start(bf16[128,1024]{1,0:T(8,128)(2,1)S(1)} %get-tuple-element.46), channel_id=1, source_target_pairs={{0,64},{1,65},{2,66},{3,67},{4,68},{5,69},{6,70},{7,71},{8,72},{9,... | collective-permute-start | bytes 786440 | tf_op jit(solution)/shard_map/ppermute | solution.py:51
  62.1 18.7 %collective-permute-start.2 = (bf16[128,1024]{1,0:T(8,128)(2,1)S(1)}, bf16[128,1024]{1,0:T(8,128)(2,1)S(1)}, u32[]{:S(2)}, u32[]{:S(2)}) collective-permute-start(bf16[128,1024]{1,0:T(8,128)(2,1)S(1)} %get-tuple-element.30), channel_id=1, source_target_pairs={{0,32},{1,33},{2,34},{3,35},{4,36},{5,37},{6,38},{7,39},{8,40},{9,... | collective-permute-start | bytes 786440 | tf_op jit(solution)/shard_map/ppermute | solution.py:51
  62.1 18.7 %collective-permute-start.3 = (bf16[128,1024]{1,0:T(8,128)(2,1)S(1)}, bf16[128,1024]{1,0:T(8,128)(2,1)S(1)}, u32[]{:S(2)}, u32[]{:S(2)}) collective-permute-start(bf16[128,1024]{1,0:T(8,128)(2,1)S(1)} %get-tuple-element.31), channel_id=1, source_target_pairs={{0,96},{1,97},{2,98},{3,99},{4,100},{5,101},{6,102},{7,103},{8,104... | collective-permute-start | bytes 786440 | tf_op jit(solution)/shard_map/ppermute | solution.py:51
  64.8 16.0 %collective-permute-start.4 = (bf16[128,1024]{1,0:T(8,128)(2,1)S(1)}, bf16[128,1024]{1,0:T(8,128)(2,1)S(1)}, u32[]{:S(2)}, u32[]{:S(2)}) collective-permute-start(bf16[128,1024]{1,0:T(8,128)(2,1)S(1)} %get-tuple-element.32), channel_id=1, source_target_pairs={{0,64},{1,65},{2,66},{3,67},{4,68},{5,69},{6,70},{7,71},{8,72},{9,... | collective-permute-start | bytes 786440 | tf_op jit(solution)/shard_map/ppermute | solution.py:51
  68.9 20.0 %collective-permute-start.20 = (bf16[128,1024]{1,0:T(8,128)(2,1)S(1)}, bf16[128,1024]{1,0:T(8,128)(2,1)S(1)}, u32[]{:S(2)}, u32[]{:S(2)}) collective-permute-start(bf16[128,1024]{1,0:T(8,128)(2,1)S(1)} %shard_map.62), channel_id=1, source_target_pairs={{0,1},{1,0},{2,3},{3,2},{4,5},{5,4},{6,7},{7,6},{8,9},{9,8},{10,11... | collective-permute-start | bytes 786440 | tf_op jit(solution)/shard_map/ppermute | solution.py:51

commit v2 on v1

--- a/solution.py
+++ b/solution.py
@@ -79,8 +79,9 @@
     return owners
 
 
-def store_masked(outs, owner, rows, columns, value):
+def store_masked(outs, owner, rows, first, value):
     my_row = lax.axis_index("dp")
+    columns = pl.ds(pl.multiple_of(first, HD), HD)
     for k, out in enumerate(outs):
         mine = owner == lax.rem(my_row + k, SIDE)
         out[rows, columns] = jnp.where(mine, value, jnp.zeros_like(value))
@@ -101,7 +102,7 @@
             for h in range(heads):
                 columns = slice(h * HD, (h + 1) * HD)
                 value = rope(projected[rows, columns], slot, cos_ref, sin_ref).astype(jnp.bfloat16)
-                store_masked(outs, owners[slot], rows, columns, value)
+                store_masked(outs, owners[slot], rows, (step * heads + h) * HD, value)
 
     @pl.when(step >= 2 // heads)
     def _():
@@ -110,7 +111,7 @@
             for h in range(heads):
                 columns = slice(h * HD, (h + 1) * HD)
                 value = projected[rows, columns].T.astype(jnp.bfloat16)
-                store_masked(outs, owners[slot], rows, columns, value)
+                store_masked(outs, owners[slot], rows, (step * heads + h) * HD, value)
 
 
 def q_kernel(core_ref, other_ref, owner_ref, order_ref, y_ref, x_ref, w_ref, *refs):
@@ -118,12 +119,14 @@
     owners = begin(core_ref, other_ref, owner_ref, order_ref, cos_ref, sin_ref)
     both = jnp.concatenate([y_ref[...], x_ref[...]], axis=0)
     projected = jnp.dot(both, w_ref[...], preferred_element_type=jnp.float32)
+    heads = w_ref.shape[1] // HD
     for slot in range(2):
-        for h in range(w_ref.shape[1] // HD):
+        for h in range(heads):
             columns = slice(h * HD, (h + 1) * HD)
+            first = (pl.program_id(0) * heads + h) * HD
             block = projected[slot * SLAB : (slot + 1) * SLAB, columns]
             value = rope(block, slot, cos_ref, sin_ref).T.astype(jnp.bfloat16)
-            store_masked(outs[4 * slot : 4 * slot + 4], owners[slot], slice(None), columns, value)
+            store_masked(outs[4 * slot : 4 * slot + 4], owners[slot], slice(None), first, value)
 
 
 def in_vmem(value):
@@ -150,7 +153,7 @@
                 pl.BlockSpec((SLAB, depth), lambda j, c: (0, 0)),
                 pl.BlockSpec((depth, width), lambda j, c: (0, block(j, c[0]))),
             ],
-            out_specs=[pl.BlockSpec((o.shape[0], width), lambda j, c: (0, j)) for o in out],
+            out_specs=[pl.BlockSpec(memory_space=pltpu.VMEM)] * len(out),
             scratch_shapes=[pltpu.VMEM((2, SLAB, HD), jnp.float32)] * 2,
         ),
         out_shape=out,
@@ -167,28 +170,19 @@
 
 FACTOR = HD**-0.5 * 1.4426950408889634
 WIDE = GROUP * SLAB
-LOW, HIGH = (0, 1), (3, 2)
-LOCAL = ((LOW, 0), (HIGH, 0))
-NEAR = ((LOW, 1), (HIGH, 1), (HIGH, 3), (LOW, 3))
-FAR = ((LOW, 2), (HIGH, 2))
-
-
-def attend_kernel(spots, t, first, last, sequence_ref, order_ref, *refs):
-    parts, refs = refs[:4], refs[4:]
-    pieces, refs = refs[: len(spots)], refs[len(spots) :]
-    if not first:
-        old, refs = refs[:3], refs[3:]
-    if last:
-        out, acc, peak, total, q_ref, kv, scores_ref, chosen = refs
-    else:
-        acc, peak, total, q_ref, kv, scores_ref, chosen = refs
+HALF = Q_COLS // 2
+STATE = ((2, HD, WIDE), (2, 8, WIDE), (2, 8, WIDE))
+OWN, ONE, TWO = (0,), (1,), (3, 2)
+
+
+def collect(t, spots, pieces, sequence_ref, order_ref, kv):
     row = lax.axis_index("dp")
     column = lax.axis_index("cp")
     core, y, z = lax.rem(column, 2), lax.rem(column // 2, SIDE), column // (2 * SIDE)
     mine = column if t == 1 else column + 1 - 2 * core
     my_sequence, my_order = sequence_ref[row, mine], order_ref[row, mine]
     count = jnp.int32(0)
-    for a, (chips, second) in enumerate(spots):
+    for piece, (chips, second) in zip(pieces, spots):
         for b, k in enumerate(chips):
             sz = lax.rem(z + 2 * SIDE - jnp.where(core == 0, k, second), SIDE)
             sy = lax.rem(y + 2 * SIDE - jnp.where(core == 0, second, k), SIDE)
@@ -200,7 +194,7 @@
 
                 @pl.when(wanted)
                 def _():
-                    kv[count] = pieces[a][(b * 2 + c) * SLAB : (b * 2 + c + 1) * SLAB, :]
+                    kv[count] = piece[(b * 2 + c) * SLAB : (b * 2 + c + 1) * SLAB, :]
 
                 count = count + wanted.astype(jnp.int32)
 
@@ -208,6 +202,13 @@
     def _():
         kv[count] = jnp.zeros((SLAB, 4 * HD), jnp.bfloat16)
 
+    return count
+
+
+def attend_slab(t, spots, pieces, parts, old, new, out, sequence_ref, order_ref, q_ref, kv, scores_ref):
+    acc, peak, total = new
+    first = old is None
+    count = collect(t, spots, pieces, sequence_ref, order_ref, kv)
     pairs_here = (count + 1) // 2
     q_ref[...] = parts[0][...] + parts[1][...] + parts[2][...] + parts[3][...]
     starts = []
@@ -224,8 +225,8 @@
             scores_ref[8, g, :SLAB] = scores
             peak[g] = jnp.max(scores.reshape(SLAB // 8, 8, WIDE), axis=0)
         else:
+            starts.append(jnp.max(old[1][g], axis=0, keepdims=True))
             peak[g] = old[1][g]
-            starts.append(jnp.max(old[1][g], axis=0, keepdims=True))
 
     def score(p, carry):
         full = 2 * p + 1 < count
@@ -273,7 +274,7 @@
         return carry
 
     lax.fori_loop(0, pairs_here, weigh, 0)
-    if last:
+    if out is not None:
         for g in range(2):
             context = acc[g] / jnp.sum(total[g], axis=0, keepdims=True)
             for h in range(GROUP):
@@ -283,12 +284,30 @@
                 )
 
 
-STATE = ((2, HD, WIDE), (2, 8, WIDE), (2, 8, WIDE))
-HALF = Q_COLS // 2
-
-
-def attend(spots, t, slab_sequence, slab_order, parts, pieces, state, last):
-    first = state is None
+def attend_kernel(jobs, spots, last, sequence_ref, order_ref, *refs):
+    pieces, refs = refs[: len(spots)], refs[len(spots) :]
+    given = []
+    for t, start, first in jobs:
+        parts, refs = refs[:4], refs[4:]
+        old = None
+        if not first:
+            old, refs = refs[:3], refs[3:]
+        given.append((parts, old))
+    per = 1 if last else 3
+    outs, refs = refs[: per * len(jobs)], refs[per * len(jobs) :]
+    state, refs = (refs[:3], refs[3:]) if last else (None, refs)
+    q_ref, kv, scores_ref = refs
+    for n, (t, start, first) in enumerate(jobs):
+        parts, old = given[n]
+        new = state if last else outs[3 * n : 3 * n + 3]
+        out = outs[n] if last else None
+        attend_slab(
+            t, spots[start:], pieces[start:], parts, old, new, out,
+            sequence_ref, order_ref, q_ref, kv, scores_ref,
+        )
+
+
+def attend(jobs, slab_sequence, slab_order, items, parts, states, last):
     vmem = pl.BlockSpec(memory_space=pltpu.VMEM)
     smem = pl.BlockSpec(memory_space=pltpu.SMEM)
     scratch = [
@@ -296,25 +315,30 @@
         pltpu.VMEM((16, SLAB, 4 * HD), jnp.bfloat16),
         pltpu.VMEM((9, 2, 2 * SLAB, WIDE), jnp.float32),
     ]
+    operands = [v for v, _, _ in items]
+    spots = [(chips, second) for _, chips, second in items]
+    for t, start, first in jobs:
+        operands += parts[t]
+        if not first:
+            operands += states[t]
     if last:
-        out_shape = [pltpu.VMEM((SLAB, HALF), jnp.bfloat16)]
+        out_shape = [pltpu.VMEM((SLAB, HALF), jnp.bfloat16)] * len(jobs)
         scratch = [pltpu.VMEM(s, jnp.float32) for s in STATE] + scratch
     else:
-        out_shape = [pltpu.VMEM(s, jnp.float32) for s in STATE]
-    operands = [in_vmem(v) for v in (*parts, *pieces, *(state or ()))]
+        out_shape = [pltpu.VMEM(s, jnp.float32) for s in STATE] * len(jobs)
     return pl.pallas_call(
-        functools.partial(attend_kernel, spots, t, first, last),
+        functools.partial(attend_kernel, jobs, spots, last),
         in_specs=[smem, smem] + [vmem] * len(operands),
         out_specs=[vmem] * len(out_shape),
         out_shape=out_shape,
-        scratch_shapes=scratch + [pltpu.SMEM((16,), jnp.int32)],
+        scratch_shapes=scratch,
         compiler_params=pltpu.CompilerParams(vmem_limit_bytes=28 << 20),
         cost_estimate=pl.CostEstimate(
             flops=2 * SLAB * len(spots) * 4 * SLAB * HALF,
             bytes_accessed=2 << 20,
             transcendentals=0,
         ),
-    )(in_hbm(slab_sequence), in_hbm(slab_order), *operands)
+    )(in_hbm(slab_sequence), in_hbm(slab_order), *[in_vmem(v) for v in operands])
 
 
 def join_kernel(core_ref, kept_ref, received_ref, out_ref):
@@ -344,30 +368,41 @@
     common = (core.reshape(1), owners, slab_order, others, rows, qkv_weight)
     kv = project(
         kv_kernel, *common, lambda j, c: QH // 2 + 2 * j + c, 2, 2 * HD,
-        [jax.ShapeDtypeStruct((2 * SLAB, 4 * HD), jnp.bfloat16)] * 4,
+        [pltpu.VMEM((2 * SLAB, 4 * HD), jnp.bfloat16)] * 4,
     )
     queries = project(
         q_kernel, *common, lambda j, c: 2 * c + j, 2, 4 * HD,
-        [jax.ShapeDtypeStruct((SLAB, HALF), jnp.bfloat16)] * 8,
+        [pltpu.VMEM((SLAB, HALF), jnp.bfloat16)] * 8,
     )
     moved = [permute(kv[k], shift_x(k)) for k in (1, 3, 2)]
     parts = [[queries[0]] + [permute(queries[k], shift_x(k)) for k in (1, 3, 2)]]
     own = kv[0] + moved[0] + moved[1] + moved[2]
     first = [permute(own, shift_first(k)) for k in (1, 3, 2)]
+    left = [permute(own, shift_second(1))]
+    right = [permute(own, shift_second(3))]
     parts.append([queries[4]] + [permute(queries[4 + k], shift_x(k)) for k in (1, 3, 2)])
-    low = jnp.concatenate([own, first[0]], axis=0)
-    high = jnp.concatenate([first[1], first[2]], axis=0)
-    left = [permute(v, shift_second(1)) for v in (low, high)]
-    right = [permute(v, shift_second(3)) for v in (high, low)]
-    far = [permute(left[0], shift_second(1)), permute(right[0], shift_second(3))]
+    two = jnp.concatenate([first[1], first[2]], axis=0)
+    left += [permute(v, shift_second(1)) for v in (first[0], two)]
+    right += [permute(v, shift_second(3)) for v in (two, first[0])]
+    far = [permute(left[0], shift_second(1))]
+    far += [permute(left[1], shift_second(1)), permute(right[1], shift_second(3))]
+    local_items = [
+        (own, OWN, 0), (first[0], ONE, 0), (two, TWO, 0), (left[0], OWN, 1), (right[0], OWN, 3)
+    ]
+    near_items = [
+        (left[1], ONE, 1), (right[2], ONE, 3), (far[0], OWN, 2), (left[2], TWO, 1), (right[1], TWO, 3)
+    ]
+    far_items = [(far[1], ONE, 2), (far[2], TWO, 2)]
     tables = (slab_sequence, slab_order)
     state = [None, None]
-    for spots, pieces in ((LOCAL, [low, high]), (NEAR, left + right)):
-        for t in range(2):
-            state[t] = attend(spots, t, *tables, parts[t], pieces, state[t], False)
-    (sent,) = attend(FAR, 0, *tables, parts[0], far, state[0], True)
+    state[0] = attend([(0, 0, True)], *tables, local_items, parts, state, False)
+    both = attend(
+        [(0, len(local_items), False), (1, 0, True)],
+        *tables, local_items + near_items, parts, state, False,
+    )
+    state = [both[:3], both[3:]]
+    sent, kept = attend([(0, 0, False), (1, 0, False)], *tables, far_items, parts, state, True)
     received = permute(sent, OTHER_CORE)
-    (kept,) = attend(FAR, 1, *tables, parts[1], far, state[1], True)
     return join(core.reshape(1), kept, received)[None]
 
 

time: 90.1 us -> 92.6 us (1.028)
  the two profiles are of different devices: /device:TPU:33 before, /device:TPU:75 now
where the time goes in v2:
time: 92.6 us; the launch traced here: 92.4 us
  starting transfers between devices  39.7 us (43%)
  Pallas kernels  26.7 us (29%)
  waiting for transfers between devices  25.2 us (27%)
    ppermute x24, starting transfers between devices, permute(): return lax.ppermute(value, AXES, table)  39.7 us
    ppermute x24, waiting for transfers between devices, permute(): return lax.ppermute(value, AXES, table)  25.2 us
    pallas_call x3, Pallas kernels, attend(): pl.pallas_call(functools.partial(attend_kernel, jobs, spots, last), in_sp...  14 us
    pallas_call x2, Pallas kernels, project(): pl.pallas_call(kernel, grid_spec=pltpu.PrefetchScalarGridSpec(num_scalar_...  11.9 us
  transfers between devices with their start and end apart: 24, of which 9 were waited for; matrix products, arithmetic and copies ran while one was open for 0% of the time, Pallas kernels for 19%

profile of v2, /device:TPU:75, one launch (start us, length us, event | category | flops | bytes accessed | tf_op | source)
XLA Modules:
  0.0 92.4 jit_solution(15222731376521282605)
XLA Ops:
  0.0 0.7 collective-permute-start.1
  0.7 0.0 collective-permute-start
  1.3 2.0 %collective-permute-done.other_ref = s32[1,1]{1,0:T(1,128)} collective-permute-done((s32[1,1]{1,0:T(1,128)}, s32[1,1]{1,0:T(1,128)}, u32[]{:S(2)}, u32[]{:S(2)}) %collective-permute-start) | collective-permute-done | bytes 36 | tf_op jit(solution)/shard_map/ppermute | solution.py:51
  3.3 4.9 %shard_map.55 = (bf16[256,512]{1,0:T(8,128)(2,1)S(1)}, bf16[256,512]{1,0:T(8,128)(2,1)S(1)}, bf16[256,512]{1,0:T(8,128)(2,1)S(1)}, bf16[256,512]{1,0:T(8,128)(2,1)S(1)}) custom-call(s32[1]{0:T(128)} %bitcast.core_ref, s32[1,1]{1,0:T(1,128)} %collective-permute-done.other_ref, s32[1,1]{1,0:T(1,128)S(6)} %copy.7.owner_ref, s32[4,32]{1,0:T(4,128)} %order_ref.9, ...), custom_call_target="tpu_custom_call" | custom-call | flops 1073741824 | bytes 6291456 | tf_op jit(solution)/shard_map/pallas_call | solution.py:143
  8.2 1.3 %collective-permute-start.2 = (bf16[256,512]{1,0:T(8,128)(2,1)S(1)}, bf16[256,512]{1,0:T(8,128)(2,1)S(1)}, u32[]{:S(2)}, u32[]{:S(2)}) collective-permute-start(bf16[256,512]{1,0:T(8,128)(2,1)S(1)} %get-tuple-element.29), channel_id=1, source_target_pairs={{0,32},{1,33},{2,34},{3,35},{4,36},{5,37},{6,38},{7,39},{8,40},{9,... | collective-permute-start | bytes 786440 | tf_op jit(solution)/shard_map/ppermute | solution.py:51
  9.5 0.3 collective-permute-start.3
  9.7 1.8 %collective-permute-start.4 = (bf16[256,512]{1,0:T(8,128)(2,1)S(1)}, bf16[256,512]{1,0:T(8,128)(2,1)S(1)}, u32[]{:S(2)}, u32[]{:S(2)}) collective-permute-start(bf16[256,512]{1,0:T(8,128)(2,1)S(1)} %get-tuple-element.31), channel_id=1, source_target_pairs={{0,64},{1,65},{2,66},{3,67},{4,68},{5,69},{6,70},{7,71},{8,72},{9,... | collective-permute-start | bytes 786440 | tf_op jit(solution)/shard_map/ppermute | solution.py:51
  11.6 4.2 %collective-permute-done.2 = bf16[256,512]{1,0:T(8,128)(2,1)S(1)} collective-permute-done((bf16[256,512]{1,0:T(8,128)(2,1)S(1)}, bf16[256,512]{1,0:T(8,128)(2,1)S(1)}, u32[]{:S(2)}, u32[]{:S(2)}) %collective-permute-start.2) | collective-permute-done | bytes 262176 | tf_op jit(solution)/shard_map/ppermute | solution.py:51
  15.7 0.9 %collective-permute-done.3 = bf16[256,512]{1,0:T(8,128)(2,1)S(1)} collective-permute-done((bf16[256,512]{1,0:T(8,128)(2,1)S(1)}, bf16[256,512]{1,0:T(8,128)(2,1)S(1)}, u32[]{:S(2)}, u32[]{:S(2)}) %collective-permute-start.3) | collective-permute-done | bytes 262176 | tf_op jit(solution)/shard_map/ppermute | solution.py:51
  16.7 6.3 %collective-permute-done.4 = bf16[256,512]{1,0:T(8,128)(2,1)S(1)} collective-permute-done((bf16[256,512]{1,0:T(8,128)(2,1)S(1)}, bf16[256,512]{1,0:T(8,128)(2,1)S(1)}, u32[]{:S(2)}, u32[]{:S(2)}) %collective-permute-start.4) | collective-permute-done | bytes 262176 | tf_op jit(solution)/shard_map/ppermute | solution.py:51
  22.9 0.1 add_add_fusion.refs_0_
  23.0 0.2 collective-permute-start.8
  23.2 2.3 %collective-permute-start.9 = (bf16[256,512]{1,0:T(8,128)(2,1)S(1)}, bf16[256,512]{1,0:T(8,128)(2,1)S(1)}, u32[]{:S(2)}, u32[]{:S(2)}) collective-permute-start(bf16[256,512]{1,0:T(8,128)(2,1)S(1)} %add_add_fusion.refs_0_), channel_id=1, source_target_pairs={{0,16},{1,5},{2,18},{3,7},{4,20},{5,1},{6,22},{7,3},{8,24},{9,13},... | collective-permute-start | bytes 786440 | tf_op jit(solution)/shard_map/ppermute | solution.py:51
  25.5 7.0 %shard_map.56 = (bf16[128,1024]{1,0:T(8,128)(2,1)S(1)}, bf16[128,1024]{1,0:T(8,128)(2,1)S(1)}, bf16[128,1024]{1,0:T(8,128)(2,1)S(1)}, bf16[128,1024]{1,0:T(8,128...) custom-call(s32[1]{0:T(128)} %bitcast.core_ref, ...), custom_call_target="tpu_custom_call" | custom-call | flops 2147483648 | bytes 10485760 | tf_op jit(solution)/shard_map/pallas_call | solution.py:143
  32.6 0.1 collective-permute-start.12
  32.6 1.5 %collective-permute-start.13 = (bf16[128,1024]{1,0:T(8,128)(2,1)S(1)}, bf16[128,1024]{1,0:T(8,128)(2,1)S(1)}, u32[]{:S(2)}, u32[]{:S(2)}) collective-permute-start(bf16[128,1024]{1,0:T(8,128)(2,1)S(1)} %get-tuple-element.34), channel_id=1, source_target_pairs={{0,96},{1,97},{2,98},{3,99},{4,100},{5,101},{6,102},{7,103},{8,104... | collective-permute-start | bytes 786440 | tf_op jit(solution)/shard_map/ppermute | solution.py:51
  34.1 1.2 %collective-permute-start.14 = (bf16[128,1024]{1,0:T(8,128)(2,1)S(1)}, bf16[128,1024]{1,0:T(8,128)(2,1)S(1)}, u32[]{:S(2)}, u32[]{:S(2)}) collective-permute-start(bf16[128,1024]{1,0:T(8,128)(2,1)S(1)} %get-tuple-element.35), channel_id=1, source_target_pairs={{0,64},{1,65},{2,66},{3,67},{4,68},{5,69},{6,70},{7,71},{8,72},{9,... | collective-permute-start | bytes 786440 | tf_op jit(solution)/shard_map/ppermute | solution.py:51
  35.3 0.0 collective-permute-done.8
  35.3 0.0 collective-permute-done.9
  35.4 0.1 collective-permute-start.10
  35.5 2.1 %collective-permute-start.20 = (bf16[128,1024]{1,0:T(8,128)(2,1)S(1)}, bf16[128,1024]{1,0:T(8,128)(2,1)S(1)}, u32[]{:S(2)}, u32[]{:S(2)}) collective-permute-start(bf16[128,1024]{1,0:T(8,128)(2,1)S(1)} %get-tuple-element.40), channel_id=1, source_target_pairs={{0,32},{1,33},{2,34},{3,35},{4,36},{5,37},{6,38},{7,39},{8,40},{9,... | collective-permute-start | bytes 786440 | tf_op jit(solution)/shard_map/ppermute | solution.py:51
  37.6 0.3 collective-permute-done.12.refs_6_.refs_11_.refs_3_
  37.9 2.1 %collective-permute-start.21 = (bf16[128,1024]{1,0:T(8,128)(2,1)S(1)}, bf16[128,1024]{1,0:T(8,128)(2,1)S(1)}, u32[]{:S(2)}, u32[]{:S(2)}) collective-permute-start(bf16[128,1024]{1,0:T(8,128)(2,1)S(1)} %get-tuple-element.41), channel_id=1, source_target_pairs={{0,96},{1,97},{2,98},{3,99},{4,100},{5,101},{6,102},{7,103},{8,104... | collective-permute-start | bytes 786440 | tf_op jit(solution)/shard_map/ppermute | solution.py:51
  40.0 0.0 collective-permute-done.13.refs_7_.refs_12_.refs_4_
  40.0 4.9 %collective-permute-start.22 = (bf16[128,1024]{1,0:T(8,128)(2,1)S(1)}, bf16[128,1024]{1,0:T(8,128)(2,1)S(1)}, u32[]{:S(2)}, u32[]{:S(2)}) collective-permute-start(bf16[128,1024]{1,0:T(8,128)(2,1)S(1)} %get-tuple-element.42), channel_id=1, source_target_pairs={{0,64},{1,65},{2,66},{3,67},{4,68},{5,69},{6,70},{7,71},{8,72},{9,... | collective-permute-start | bytes 786440 | tf_op jit(solution)/shard_map/ppermute | solution.py:51
  44.9 1.3 %collective-permute-start.5 = (bf16[256,512]{1,0:T(8,128)(2,1)S(1)}, bf16[256,512]{1,0:T(8,128)(2,1)S(1)}, u32[]{:S(2)}, u32[]{:S(2)}) collective-permute-start(bf16[256,512]{1,0:T(8,128)(2,1)S(1)} %add_add_fusion.refs_0_), channel_id=1, source_target_pairs={{0,8},{1,3},{2,10},{3,5},{4,12},{5,7},{6,14},{7,1},{8,16},{9,11},{... | collective-permute-start | bytes 786440 | tf_op jit(solution)/shard_map/ppermute | solution.py:51
  46.2 2.8 %collective-permute-done.20.refs_18_.refs_10_ = bf16[128,1024]{1,0:T(8,128)(2,1)S(1)} collective-permute-done((bf16[128,1024]{1,0:T(8,128)(2,1)S(1)}, bf16[128,1024]{1,0:T(8,128)(2,1)S(1)}, u32[]{:S(2)}, u32[]{:S(2)}) %collective-permute-start.20) | collective-permute-done | bytes 262176 | tf_op jit(solution)/shard_map/ppermute | solution.py:51
  48.9 4.5 %collective-permute-start.15 = (bf16[256,512]{1,0:T(8,128)(2,1)S(1)}, bf16[256,512]{1,0:T(8,128)(2,1)S(1)}, u32[]{:S(2)}, u32[]{:S(2)}) collective-permute-start(bf16[256,512]{1,0:T(8,128)(2,1)S(1)} %add_add_fusion.refs_0_), channel_id=1, source_target_pairs={{0,2},{1,9},{2,4},{3,11},{4,6},{5,13},{6,0},{7,15},{8,10},{9,17},{... | collective-permute-start | bytes 786440 | tf_op jit(solution)/shard_map/ppermute | solution.py:51
  53.4 0.0 collective-permute-done.21.refs_19_.refs_11_
  53.4 0.0 collective-permute-start.16
  53.4 1.6 %collective-permute-done.22.refs_20_.refs_12_ = bf16[128,1024]{1,0:T(8,128)(2,1)S(1)} collective-permute-done((bf16[128,1024]{1,0:T(8,128)(2,1)S(1)}, bf16[128,1024]{1,0:T(8,128)(2,1)S(1)}, u32[]{:S(2)}, u32[]{:S(2)}) %collective-permute-start.22) | collective-permute-done | bytes 262176 | tf_op jit(solution)/shard_map/ppermute | solution.py:51
  55.0 5.8 %collective-permute-start.19 = (bf16[512,512]{1,0:T(8,128)(2,1)S(1)}, bf16[512,512]{1,0:T(8,128)(2,1)S(1)}, u32[]{:S(2)}, u32[]{:S(2)}) collective-permute-start(bf16[512,512]{1,0:T(8,128)(2,1)S(1)} %constant_dynamic-update-slice_fusion.refs_2_), channel_id=1, source_target_pairs={{0,2},{1,9},{2,4},{3,11},{4,6},{5,13},{6,0},{7,15},{8,10},{9,17},{... | collective-permute-start | bytes 1572872 | tf_op jit(solution)/shard_map/ppermute | solution.py:51
  60.9 0.0 collective-permute-start.6
  60.9 1.4 %collective-permute-start.11 = (bf16[512,512]{1,0:T(8,128)(2,1)S(1)}, bf16[512,512]{1,0:T(8,128)(2,1)S(1)}, u32[]{:S(2)}, u32[]{:S(2)}) collective-permute-start(bf16[512,512]{1,0:T(8,128)(2,1)S(1)} %collective-permute-done.10.refs_9_), channel_id=1, source_target_pairs={{0,6},{1,25},{2,0},{3,27},{4,2},{5,29},{6,4},{7,31},{8,14},{9,1},{... | collective-permute-start | bytes 1572872 | tf_op jit(solution)/shard_map/ppermute | solution.py:51
  62.4 0.0 collective-permute-done.15.refs_3_
  62.4 0.1 collective-permute-start.17
  62.4 1.4 %collective-permute-start.18 = (bf16[256,512]{1,0:T(8,128)(2,1)S(1)}, bf16[256,512]{1,0:T(8,128)(2,1)S(1)}, u32[]{:S(2)}, u32[]{:S(2)}) collective-permute-start(bf16[256,512]{1,0:T(8,128)(2,1)S(1)} %collective-permute-done.15.refs_3_), channel_id=1, source_target_pairs={{0,2},{1,9},{2,4},{3,11},{4,6},{5,13},{6,0},{7,15},{8,10},{9,17},{... | collective-permute-start | bytes 786440 | tf_op jit(solution)/shard_map/ppermute | solution.py:51
  63.8 6.0 %collective-permute-done.6.refs_5_ = bf16[256,512]{1,0:T(8,128)(2,1)S(1)} collective-permute-done((bf16[256,512]{1,0:T(8,128)(2,1)S(1)}, bf16[256,512]{1,0:T(8,128)(2,1)S(1)}, u32[]{:S(2)}, u32[]{:S(2)}) %collective-permute-start.6) | collective-permute-done | bytes 262176 | tf_op jit(solution)/shard_map/ppermute | solution.py:51
  69.8 2.2 %collective-permute-start.7 = (bf16[256,512]{1,0:T(8,128)(2,1)S(1)}, bf16[256,512]{1,0:T(8,128)(2,1)S(1)}, u32[]{:S(2)}, u32[]{:S(2)}) collective-permute-start(bf16[256,512]{1,0:T(8,128)(2,1)S(1)} %collective-permute-done.6.refs_5_), channel_id=1, source_target_pairs={{0,2},{1,9},{2,4},{3,11},{4,6},{5,13},{6,0},{7,15},{8,10},{9,17},{... | collective-permute-start | bytes 786440 | tf_op jit(solution)/shard_map/ppermute | solution.py:51
  72.0 3.5 %shard_map.57 = (f32[2,128,512]{2,1,0:T(8,128)S(1)}, f32[2,8,512]{2,1,0:T(8,128)S(1)}, f32[2,8,512]{2,1,0:T(8,128)S(1)}) custom-call(s32[4,32]{1,0:T(4,128)} %sequence_ref.5, s32[4,32]{1,0:T(4,128)} %order_ref.9, bf16[256,512]{1,0:T(8,128)(2,1)S(1)} %add_add_fusion.refs_0_, bf16[256,512]{1,0:T(8,128)(2,1)S(1)} %collective-permute-done.5.refs_1_, ...), custom_call_target="tpu_custom_call" | custom-call | flops 671088640 | bytes 2097152 | tf_op jit(solution)/shard_map/pallas_call | solution.py:329
  75.6 0.0 collective-permute-done.17.refs_6_
  75.6 0.0 collective-permute-done.19.refs_8_
  75.6 7.1 %shard_map.58 = (f32[2,128,512]{2,1,0:T(8,128)S(1)}, f32[2,8,512]{2,1,0:T(8,128)S(1)}, f32[2,8,512]{2,1,0:T(8,128)S(1)}, f32[2,128,512]{2,1,0:T(8,128)S(1)}, f32...) custom-call(s32[4,32]{1,0:T(4,128)} %sequence_ref.5, s32[4,32]{1,0:T(4,128)} %order_ref.9, ...), custom_call_target="tpu_custom_call" | custom-call | flops 1342177280 | bytes 2097152 | tf_op jit(solution)/shard_map/pallas_call | solution.py:329
  82.7 0.0 collective-permute-done.11.refs_1_
  82.7 3.4 %shard_map.59 = (bf16[128,1024]{1,0:T(8,128)(2,1)S(1)}, bf16[128,1024]{1,0:T(8,128)(2,1)S(1)}) custom-call(s32[4,32]{1,0:T(4,128)} %sequence_ref.5, s32[4,32]{1,0:T(4,128)} %order_ref.9, bf16[256,512]{1,0:T(8,128)(2,1)S(1)} %collective-permute-done.7.refs_0_, bf16[512,512]{1,0:T(8,128)(2,1)S(1)} %collective-permute-done.11.refs_1_, ...), custom_call_target="tpu_custom_call" | custom-call | flops 268435456 | bytes 2097152 | tf_op jit(solution)/shard_map/pallas_call | solution.py:329
  86.1 4.3 %collective-permute-start.23 = (bf16[128,1024]{1,0:T(8,128)(2,1)S(1)}, bf16[128,1024]{1,0:T(8,128)(2,1)S(1)}, u32[]{:S(2)}, u32[]{:S(2)}) collective-permute-start(bf16[128,1024]{1,0:T(8,128)(2,1)S(1)} %get-tuple-element.50), channel_id=1, source_target_pairs={{0,1},{1,0},{2,3},{3,2},{4,5},{5,4},{6,7},{7,6},{8,9},{9,8},{10,11... | collective-permute-start | bytes 786440 | tf_op jit(solution)/shard_map/ppermute | solution.py:51
  90.4 1.2 %collective-permute-done.23.received_ref = bf16[128,1024]{1,0:T(8,128)(2,1)S(1)} collective-permute-done((bf16[128,1024]{1,0:T(8,128)(2,1)S(1)}, bf16[128,1024]{1,0:T(8,128)(2,1)S(1)}, u32[]{:S(2)}, u32[]{:S(2)}) %collective-permute-start.23) | collective-permute-done | bytes 262176 | tf_op jit(solution)/shard_map/ppermute | solution.py:51
  91.6 0.8 join.1
  (9 shorter events, 0.1 us)
Async XLA Ops:
  0.0 3.3 %collective-permute-start.1 = (bf16[128,4096]{1,0:T(8,128)(2,1)}, bf16[128,4096]{1,0:T(8,128)(2,1)S(1)}, u32[]{:S(2)}, u32[]{:S(2)}) collective-permute-start(bf16[128,4096]{1,0:T(8,128)(2,1)} %bitcast.3), channel_id=1, source_target_pairs={{0,1},{1,0},{2,3},{3,2},{4,5},{5,4},{6,7},{7,6},{8,9},{9,8},{10,11... | collective-permute-start | bytes 3145736 | tf_op jit(solution)/shard_map/ppermute | solution.py:51
  0.7 2.6 %collective-permute-start = (s32[1,1]{1,0:T(1,128)}, s32[1,1]{1,0:T(1,128)}, u32[]{:S(2)}, u32[]{:S(2)}) collective-permute-start(s32[1,1]{1,0:T(1,128)} %param.7), channel_id=1, source_target_pairs={{0,1},{1,0},{2,3},{3,2},{4,5},{5,4},{6,7},{7,6},{8,9},{9,8},{10,11... | collective-permute-start | bytes 20 | tf_op jit(solution)/shard_map/ppermute | solution.py:51
  8.2 7.6 %collective-permute-start.2 = (bf16[256,512]{1,0:T(8,128)(2,1)S(1)}, bf16[256,512]{1,0:T(8,128)(2,1)S(1)}, u32[]{:S(2)}, u32[]{:S(2)}) collective-permute-start(bf16[256,512]{1,0:T(8,128)(2,1)S(1)} %get-tuple-element.29), channel_id=1, source_target_pairs={{0,32},{1,33},{2,34},{3,35},{4,36},{5,37},{6,38},{7,39},{8,40},{9,... | collective-permute-start | bytes 786440 | tf_op jit(solution)/shard_map/ppermute | solution.py:51
  9.5 7.2 %collective-permute-start.3 = (bf16[256,512]{1,0:T(8,128)(2,1)S(1)}, bf16[256,512]{1,0:T(8,128)(2,1)S(1)}, u32[]{:S(2)}, u32[]{:S(2)}) collective-permute-start(bf16[256,512]{1,0:T(8,128)(2,1)S(1)} %get-tuple-element.30), channel_id=1, source_target_pairs={{0,96},{1,97},{2,98},{3,99},{4,100},{5,101},{6,102},{7,103},{8,104... | collective-permute-start | bytes 786440 | tf_op jit(solution)/shard_map/ppermute | solution.py:51
  9.7 13.2 %collective-permute-start.4 = (bf16[256,512]{1,0:T(8,128)(2,1)S(1)}, bf16[256,512]{1,0:T(8,128)(2,1)S(1)}, u32[]{:S(2)}, u32[]{:S(2)}) collective-permute-start(bf16[256,512]{1,0:T(8,128)(2,1)S(1)} %get-tuple-element.31), channel_id=1, source_target_pairs={{0,64},{1,65},{2,66},{3,67},{4,68},{5,69},{6,70},{7,71},{8,72},{9,... | collective-permute-start | bytes 786440 | tf_op jit(solution)/shard_map/ppermute | solution.py:51
  23.0 12.3 %collective-permute-start.8 = (bf16[256,512]{1,0:T(8,128)(2,1)S(1)}, bf16[256,512]{1,0:T(8,128)(2,1)S(1)}, u32[]{:S(2)}, u32[]{:S(2)}) collective-permute-start(bf16[256,512]{1,0:T(8,128)(2,1)S(1)} %add_add_fusion.refs_0_), channel_id=1, source_target_pairs={{0,24},{1,7},{2,26},{3,1},{4,28},{5,3},{6,30},{7,5},{8,0},{9,15},{... | collective-permute-start | bytes 786440 | tf_op jit(solution)/shard_map/ppermute | solution.py:51
  23.2 12.1 %collective-permute-start.9 = (bf16[256,512]{1,0:T(8,128)(2,1)S(1)}, bf16[256,512]{1,0:T(8,128)(2,1)S(1)}, u32[]{:S(2)}, u32[]{:S(2)}) collective-permute-start(bf16[256,512]{1,0:T(8,128)(2,1)S(1)} %add_add_fusion.refs_0_), channel_id=1, source_target_pairs={{0,16},{1,5},{2,18},{3,7},{4,20},{5,1},{6,22},{7,3},{8,24},{9,13},... | collective-permute-start | bytes 786440 | tf_op jit(solution)/shard_map/ppermute | solution.py:51
  32.6 5.3 %collective-permute-start.12 = (bf16[128,1024]{1,0:T(8,128)(2,1)S(1)}, bf16[128,1024]{1,0:T(8,128)(2,1)S(1)}, u32[]{:S(2)}, u32[]{:S(2)}) collective-permute-start(bf16[128,1024]{1,0:T(8,128)(2,1)S(1)} %get-tuple-element.33), channel_id=1, source_target_pairs={{0,32},{1,33},{2,34},{3,35},{4,36},{5,37},{6,38},{7,39},{8,40},{9,... | collective-permute-start | bytes 786440 | tf_op jit(solution)/shard_map/ppermute | solution.py:51
  32.6 7.3 %collective-permute-start.13 = (bf16[128,1024]{1,0:T(8,128)(2,1)S(1)}, bf16[128,1024]{1,0:T(8,128)(2,1)S(1)}, u32[]{:S(2)}, u32[]{:S(2)}) collective-permute-start(bf16[128,1024]{1,0:T(8,128)(2,1)S(1)} %get-tuple-element.34), channel_id=1, source_target_pairs={{0,96},{1,97},{2,98},{3,99},{4,100},{5,101},{6,102},{7,103},{8,104... | collective-permute-start | bytes 786440 | tf_op jit(solution)/shard_map/ppermute | solution.py:51
  34.1 10.8 %collective-permute-start.14 = (bf16[128,1024]{1,0:T(8,128)(2,1)S(1)}, bf16[128,1024]{1,0:T(8,128)(2,1)S(1)}, u32[]{:S(2)}, u32[]{:S(2)}) collective-permute-start(bf16[128,1024]{1,0:T(8,128)(2,1)S(1)} %get-tuple-element.35), channel_id=1, source_target_pairs={{0,64},{1,65},{2,66},{3,67},{4,68},{5,69},{6,70},{7,71},{8,72},{9,... | collective-permute-start | bytes 786440 | tf_op jit(solution)/shard_map/ppermute | solution.py:51
  35.4 25.5 %collective-permute-start.10 = (bf16[512,512]{1,0:T(8,128)(2,1)S(1)}, bf16[512,512]{1,0:T(8,128)(2,1)S(1)}, u32[]{:S(2)}, u32[]{:S(2)}) collective-permute-start(bf16[512,512]{1,0:T(8,128)(2,1)S(1)} %constant_dynamic-update-slice_fusion.refs_2_), channel_id=1, source_target_pairs={{0,6},{1,25},{2,0},{3,27},{4,2},{5,29},{6,4},{7,31},{8,14},{9,1},{... | collective-permute-start | bytes 1572872 | tf_op jit(solution)/shard_map/ppermute | solution.py:51
  35.5 13.5 %collective-permute-start.20 = (bf16[128,1024]{1,0:T(8,128)(2,1)S(1)}, bf16[128,1024]{1,0:T(8,128)(2,1)S(1)}, u32[]{:S(2)}, u32[]{:S(2)}) collective-permute-start(bf16[128,1024]{1,0:T(8,128)(2,1)S(1)} %get-tuple-element.40), channel_id=1, source_target_pairs={{0,32},{1,33},{2,34},{3,35},{4,36},{5,37},{6,38},{7,39},{8,40},{9,... | collective-permute-start | bytes 786440 | tf_op jit(solution)/shard_map/ppermute | solution.py:51
  37.9 15.6 %collective-permute-start.21 = (bf16[128,1024]{1,0:T(8,128)(2,1)S(1)}, bf16[128,1024]{1,0:T(8,128)(2,1)S(1)}, u32[]{:S(2)}, u32[]{:S(2)}) collective-permute-start(bf16[128,1024]{1,0:T(8,128)(2,1)S(1)} %get-tuple-element.41), channel_id=1, source_target_pairs={{0,96},{1,97},{2,98},{3,99},{4,100},{5,101},{6,102},{7,103},{8,104... | collective-permute-start | bytes 786440 | tf_op jit(solution)/shard_map/ppermute | solution.py:51
  40.0 15.1 %collective-permute-start.22 = (bf16[128,1024]{1,0:T(8,128)(2,1)S(1)}, bf16[128,1024]{1,0:T(8,128)(2,1)S(1)}, u32[]{:S(2)}, u32[]{:S(2)}) collective-permute-start(bf16[128,1024]{1,0:T(8,128)(2,1)S(1)} %get-tuple-element.42), channel_id=1, source_target_pairs={{0,64},{1,65},{2,66},{3,67},{4,68},{5,69},{6,70},{7,71},{8,72},{9,... | collective-permute-start | bytes 786440 | tf_op jit(solution)/shard_map/ppermute | solution.py:51
  44.9 16.0 %collective-permute-start.5 = (bf16[256,512]{1,0:T(8,128)(2,1)S(1)}, bf16[256,512]{1,0:T(8,128)(2,1)S(1)}, u32[]{:S(2)}, u32[]{:S(2)}) collective-permute-start(bf16[256,512]{1,0:T(8,128)(2,1)S(1)} %add_add_fusion.refs_0_), channel_id=1, source_target_pairs={{0,8},{1,3},{2,10},{3,5},{4,12},{5,7},{6,14},{7,1},{8,16},{9,11},{... | collective-permute-start | bytes 786440 | tf_op jit(solution)/shard_map/ppermute | solution.py:51
  48.9 13.4 %collective-permute-start.15 = (bf16[256,512]{1,0:T(8,128)(2,1)S(1)}, bf16[256,512]{1,0:T(8,128)(2,1)S(1)}, u32[]{:S(2)}, u32[]{:S(2)}) collective-permute-start(bf16[256,512]{1,0:T(8,128)(2,1)S(1)} %add_add_fusion.refs_0_), channel_id=1, source_target_pairs={{0,2},{1,9},{2,4},{3,11},{4,6},{5,13},{6,0},{7,15},{8,10},{9,17},{... | collective-permute-start | bytes 786440 | tf_op jit(solution)/shard_map/ppermute | solution.py:51
  53.4 9.0 %collective-permute-start.16 = (bf16[256,512]{1,0:T(8,128)(2,1)S(1)}, bf16[256,512]{1,0:T(8,128)(2,1)S(1)}, u32[]{:S(2)}, u32[]{:S(2)}) collective-permute-start(bf16[256,512]{1,0:T(8,128)(2,1)S(1)} %add_add_fusion.refs_0_), channel_id=1, source_target_pairs={{0,6},{1,25},{2,0},{3,27},{4,2},{5,29},{6,4},{7,31},{8,14},{9,1},{... | collective-permute-start | bytes 786440 | tf_op jit(solution)/shard_map/ppermute | solution.py:51
  55.0 20.5 %collective-permute-start.19 = (bf16[512,512]{1,0:T(8,128)(2,1)S(1)}, bf16[512,512]{1,0:T(8,128)(2,1)S(1)}, u32[]{:S(2)}, u32[]{:S(2)}) collective-permute-start(bf16[512,512]{1,0:T(8,128)(2,1)S(1)} %constant_dynamic-update-slice_fusion.refs_2_), channel_id=1, source_target_pairs={{0,2},{1,9},{2,4},{3,11},{4,6},{5,13},{6,0},{7,15},{8,10},{9,17},{... | collective-permute-start | bytes 1572872 | tf_op jit(solution)/shard_map/ppermute | solution.py:51
  60.9 8.9 %collective-permute-start.6 = (bf16[256,512]{1,0:T(8,128)(2,1)S(1)}, bf16[256,512]{1,0:T(8,128)(2,1)S(1)}, u32[]{:S(2)}, u32[]{:S(2)}) collective-permute-start(bf16[256,512]{1,0:T(8,128)(2,1)S(1)} %collective-permute-done.5.refs_1_), channel_id=1, source_target_pairs={{0,2},{1,9},{2,4},{3,11},{4,6},{5,13},{6,0},{7,15},{8,10},{9,17},{... | collective-permute-start | bytes 786440 | tf_op jit(solution)/shard_map/ppermute | solution.py:51
  60.9 21.8 %collective-permute-start.11 = (bf16[512,512]{1,0:T(8,128)(2,1)S(1)}, bf16[512,512]{1,0:T(8,128)(2,1)S(1)}, u32[]{:S(2)}, u32[]{:S(2)}) collective-permute-start(bf16[512,512]{1,0:T(8,128)(2,1)S(1)} %collective-permute-done.10.refs_9_), channel_id=1, source_target_pairs={{0,6},{1,25},{2,0},{3,27},{4,2},{5,29},{6,4},{7,31},{8,14},{9,1},{... | collective-permute-start | bytes 1572872 | tf_op jit(solution)/shard_map/ppermute | solution.py:51
  62.4 13.2 %collective-permute-start.17 = (bf16[256,512]{1,0:T(8,128)(2,1)S(1)}, bf16[256,512]{1,0:T(8,128)(2,1)S(1)}, u32[]{:S(2)}, u32[]{:S(2)}) collective-permute-start(bf16[256,512]{1,0:T(8,128)(2,1)S(1)} %collective-permute-done.5.refs_1_), channel_id=1, source_target_pairs={{0,6},{1,25},{2,0},{3,27},{4,2},{5,29},{6,4},{7,31},{8,14},{9,1},{... | collective-permute-start | bytes 786440 | tf_op jit(solution)/shard_map/ppermute | solution.py:51
  62.4 13.1 %collective-permute-start.18 = (bf16[256,512]{1,0:T(8,128)(2,1)S(1)}, bf16[256,512]{1,0:T(8,128)(2,1)S(1)}, u32[]{:S(2)}, u32[]{:S(2)}) collective-permute-start(bf16[256,512]{1,0:T(8,128)(2,1)S(1)} %collective-permute-done.15.refs_3_), channel_id=1, source_target_pairs={{0,2},{1,9},{2,4},{3,11},{4,6},{5,13},{6,0},{7,15},{8,10},{9,17},{... | collective-permute-start | bytes 786440 | tf_op jit(solution)/shard_map/ppermute | solution.py:51
  69.8 12.9 %collective-permute-start.7 = (bf16[256,512]{1,0:T(8,128)(2,1)S(1)}, bf16[256,512]{1,0:T(8,128)(2,1)S(1)}, u32[]{:S(2)}, u32[]{:S(2)}) collective-permute-start(bf16[256,512]{1,0:T(8,128)(2,1)S(1)} %collective-permute-done.6.refs_5_), channel_id=1, source_target_pairs={{0,2},{1,9},{2,4},{3,11},{4,6},{5,13},{6,0},{7,15},{8,10},{9,17},{... | collective-permute-start | bytes 786440 | tf_op jit(solution)/shard_map/ppermute | solution.py:51
  86.1 5.5 %collective-permute-start.23 = (bf16[128,1024]{1,0:T(8,128)(2,1)S(1)}, bf16[128,1024]{1,0:T(8,128)(2,1)S(1)}, u32[]{:S(2)}, u32[]{:S(2)}) collective-permute-start(bf16[128,1024]{1,0:T(8,128)(2,1)S(1)} %get-tuple-element.50), channel_id=1, source_target_pairs={{0,1},{1,0},{2,3},{3,2},{4,5},{5,4},{6,7},{7,6},{8,9},{9,8},{10,11... | collective-permute-start | bytes 786440 | tf_op jit(solution)/shard_map/ppermute | solution.py:51

commit v3 on v2

--- a/solution.py
+++ b/solution.py
@@ -172,7 +172,7 @@
 WIDE = GROUP * SLAB
 HALF = Q_COLS // 2
 STATE = ((2, HD, WIDE), (2, 8, WIDE), (2, 8, WIDE))
-OWN, ONE, TWO = (0,), (1,), (3, 2)
+LOW, HIGH = (0, 1), (3, 2)
 
 
 def collect(t, spots, pieces, sequence_ref, order_ref, kv):
@@ -378,28 +378,20 @@
     parts = [[queries[0]] + [permute(queries[k], shift_x(k)) for k in (1, 3, 2)]]
     own = kv[0] + moved[0] + moved[1] + moved[2]
     first = [permute(own, shift_first(k)) for k in (1, 3, 2)]
-    left = [permute(own, shift_second(1))]
-    right = [permute(own, shift_second(3))]
     parts.append([queries[4]] + [permute(queries[4 + k], shift_x(k)) for k in (1, 3, 2)])
-    two = jnp.concatenate([first[1], first[2]], axis=0)
-    left += [permute(v, shift_second(1)) for v in (first[0], two)]
-    right += [permute(v, shift_second(3)) for v in (two, first[0])]
-    far = [permute(left[0], shift_second(1))]
-    far += [permute(left[1], shift_second(1)), permute(right[1], shift_second(3))]
-    local_items = [
-        (own, OWN, 0), (first[0], ONE, 0), (two, TWO, 0), (left[0], OWN, 1), (right[0], OWN, 3)
-    ]
-    near_items = [
-        (left[1], ONE, 1), (right[2], ONE, 3), (far[0], OWN, 2), (left[2], TWO, 1), (right[1], TWO, 3)
-    ]
-    far_items = [(far[1], ONE, 2), (far[2], TWO, 2)]
+    low = jnp.concatenate([own, first[0]], axis=0)
+    high = jnp.concatenate([first[1], first[2]], axis=0)
+    left = [permute(v, shift_second(1)) for v in (low, high)]
+    right = [permute(v, shift_second(3)) for v in (high, low)]
+    far = [permute(left[0], shift_second(1)), permute(right[0], shift_second(3))]
+    local_items = [(low, LOW, 0), (high, HIGH, 0)]
+    near_items = [(left[0], LOW, 1), (left[1], HIGH, 1), (right[0], HIGH, 3), (right[1], LOW, 3)]
+    far_items = [(far[0], LOW, 2), (far[1], HIGH, 2)]
     tables = (slab_sequence, slab_order)
     state = [None, None]
-    state[0] = attend([(0, 0, True)], *tables, local_items, parts, state, False)
-    both = attend(
-        [(0, len(local_items), False), (1, 0, True)],
-        *tables, local_items + near_items, parts, state, False,
-    )
+    for t in (0, 1):
+        state[t] = attend([(t, 0, True)], *tables, local_items, parts, state, False)
+    both = attend([(0, 0, False), (1, 0, False)], *tables, near_items, parts, state, False)
     state = [both[:3], both[3:]]
     sent, kept = attend([(0, 0, False), (1, 0, False)], *tables, far_items, parts, state, True)
     received = permute(sent, OTHER_CORE)

time: 92.6 us -> 85.4 us (0.922)
  the two profiles are of different devices: /device:TPU:75 before, /device:TPU:115 now
where the time goes in v3:
time: 85.4 us; the launch traced here: 85.2 us
  starting transfers between devices  30.7 us (36%)
  Pallas kernels  29 us (34%)
  waiting for transfers between devices  24.5 us (29%)
    ppermute x21, starting transfers between devices, permute(): return lax.ppermute(value, AXES, table)  30.7 us
    ppermute x21, waiting for transfers between devices, permute(): return lax.ppermute(value, AXES, table)  24.5 us
    pallas_call x4, Pallas kernels, attend(): pl.pallas_call(functools.partial(attend_kernel, jobs, spots, last), in_sp...  16.1 us
    pallas_call x2, Pallas kernels, project(): pl.pallas_call(kernel, grid_spec=pltpu.PrefetchScalarGridSpec(num_scalar_...  12 us
  transfers between devices with their start and end apart: 21, of which 10 were waited for; matrix products, arithmetic and copies ran while one was open for 0% of the time, Pallas kernels for 22%

profile of v3, /device:TPU:115, one launch (start us, length us, event | category | flops | bytes accessed | tf_op | source)
XLA Modules:
  0.0 85.2 jit_solution(6868703209897615074)
XLA Ops:
  0.0 0.7 collective-permute-start.1
  0.7 0.0 collective-permute-start
  1.3 1.8 %collective-permute-done.other_ref = s32[1,1]{1,0:T(1,128)} collective-permute-done((s32[1,1]{1,0:T(1,128)}, s32[1,1]{1,0:T(1,128)}, u32[]{:S(2)}, u32[]{:S(2)}) %collective-permute-start) | collective-permute-done | bytes 36 | tf_op jit(solution)/shard_map/ppermute | solution.py:51
  3.2 0.0 collective-permute-done.1.y_ref
  3.2 4.9 %shard_map.55 = (bf16[256,512]{1,0:T(8,128)(2,1)S(1)}, bf16[256,512]{1,0:T(8,128)(2,1)S(1)}, bf16[256,512]{1,0:T(8,128)(2,1)S(1)}, bf16[256,512]{1,0:T(8,128)(2,1)S(1)}) custom-call(s32[1]{0:T(128)} %bitcast.core_ref, s32[1,1]{1,0:T(1,128)} %collective-permute-done.other_ref, s32[1,1]{1,0:T(1,128)S(6)} %copy.7.owner_ref, s32[4,32]{1,0:T(4,128)} %order_ref.11, ...), custom_call_target="tpu_custom_call" | custom-call | flops 1073741824 | bytes 6291456 | tf_op jit(solution)/shard_map/pallas_call | solution.py:143
  8.1 1.3 %collective-permute-start.2 = (bf16[256,512]{1,0:T(8,128)(2,1)S(1)}, bf16[256,512]{1,0:T(8,128)(2,1)S(1)}, u32[]{:S(2)}, u32[]{:S(2)}) collective-permute-start(bf16[256,512]{1,0:T(8,128)(2,1)S(1)} %get-tuple-element.32), channel_id=1, source_target_pairs={{0,32},{1,33},{2,34},{3,35},{4,36},{5,37},{6,38},{7,39},{8,40},{9,... | collective-permute-start | bytes 786440 | tf_op jit(solution)/shard_map/ppermute | solution.py:51
  9.4 0.3 collective-permute-start.3
  9.6 1.8 %collective-permute-start.4 = (bf16[256,512]{1,0:T(8,128)(2,1)S(1)}, bf16[256,512]{1,0:T(8,128)(2,1)S(1)}, u32[]{:S(2)}, u32[]{:S(2)}) collective-permute-start(bf16[256,512]{1,0:T(8,128)(2,1)S(1)} %get-tuple-element.34), channel_id=1, source_target_pairs={{0,64},{1,65},{2,66},{3,67},{4,68},{5,69},{6,70},{7,71},{8,72},{9,... | collective-permute-start | bytes 786440 | tf_op jit(solution)/shard_map/ppermute | solution.py:51
  11.5 4.2 %collective-permute-done.2 = bf16[256,512]{1,0:T(8,128)(2,1)S(1)} collective-permute-done((bf16[256,512]{1,0:T(8,128)(2,1)S(1)}, bf16[256,512]{1,0:T(8,128)(2,1)S(1)}, u32[]{:S(2)}, u32[]{:S(2)}) %collective-permute-start.2) | collective-permute-done | bytes 262176 | tf_op jit(solution)/shard_map/ppermute | solution.py:51
  15.6 0.9 %collective-permute-done.3 = bf16[256,512]{1,0:T(8,128)(2,1)S(1)} collective-permute-done((bf16[256,512]{1,0:T(8,128)(2,1)S(1)}, bf16[256,512]{1,0:T(8,128)(2,1)S(1)}, u32[]{:S(2)}, u32[]{:S(2)}) %collective-permute-start.3) | collective-permute-done | bytes 262176 | tf_op jit(solution)/shard_map/ppermute | solution.py:51
  16.6 6.3 %collective-permute-done.4 = bf16[256,512]{1,0:T(8,128)(2,1)S(1)} collective-permute-done((bf16[256,512]{1,0:T(8,128)(2,1)S(1)}, bf16[256,512]{1,0:T(8,128)(2,1)S(1)}, u32[]{:S(2)}, u32[]{:S(2)}) %collective-permute-start.4) | collective-permute-done | bytes 262176 | tf_op jit(solution)/shard_map/ppermute | solution.py:51
  22.8 0.1 add_add_fusion
  22.9 0.2 collective-permute-start.8
  23.1 2.6 %collective-permute-start.9 = (bf16[256,512]{1,0:T(8,128)(2,1)S(1)}, bf16[256,512]{1,0:T(8,128)(2,1)S(1)}, u32[]{:S(2)}, u32[]{:S(2)}) collective-permute-start(bf16[256,512]{1,0:T(8,128)(2,1)S(1)} %add_add_fusion), channel_id=1, source_target_pairs={{0,16},{1,5},{2,18},{3,7},{4,20},{5,1},{6,22},{7,3},{8,24},{9,13},... | collective-permute-start | bytes 786440 | tf_op jit(solution)/shard_map/ppermute | solution.py:51
  25.7 0.0 collective-permute-start.5
  25.7 7.1 %shard_map.56 = (bf16[128,1024]{1,0:T(8,128)(2,1)S(1)}, bf16[128,1024]{1,0:T(8,128)(2,1)S(1)}, bf16[128,1024]{1,0:T(8,128)(2,1)S(1)}, bf16[128,1024]{1,0:T(8,128...) custom-call(s32[1]{0:T(128)} %bitcast.core_ref, ...), custom_call_target="tpu_custom_call" | custom-call | flops 2147483648 | bytes 10485760 | tf_op jit(solution)/shard_map/pallas_call | solution.py:143
  32.9 0.1 collective-permute-start.17
  33.0 0.0 collective-permute-done.8
  33.0 0.0 collective-permute-done.9
  33.0 0.2 collective-permute-start.10
  33.2 0.0 collective-permute-done.5
  33.3 2.6 %collective-permute-start.6 = (bf16[512,512]{1,0:T(8,128)(2,1)S(1)}, bf16[512,512]{1,0:T(8,128)(2,1)S(1)}, u32[]{:S(2)}, u32[]{:S(2)}) collective-permute-start(bf16[512,512]{1,0:T(8,128)(2,1)S(1)} %pad_maximum_fusion.refs_0_), channel_id=1, source_target_pairs={{0,2},{1,9},{2,4},{3,11},{4,6},{5,13},{6,0},{7,15},{8,10},{9,17},{... | collective-permute-start | bytes 1572872 | tf_op jit(solution)/shard_map/ppermute | solution.py:51
  35.9 1.4 %collective-permute-start.18 = (bf16[128,1024]{1,0:T(8,128)(2,1)S(1)}, bf16[128,1024]{1,0:T(8,128)(2,1)S(1)}, u32[]{:S(2)}, u32[]{:S(2)}) collective-permute-start(bf16[128,1024]{1,0:T(8,128)(2,1)S(1)} %get-tuple-element.44), channel_id=1, source_target_pairs={{0,96},{1,97},{2,98},{3,99},{4,100},{5,101},{6,102},{7,103},{8,104... | collective-permute-start | bytes 786440 | tf_op jit(solution)/shard_map/ppermute | solution.py:51
  37.3 1.2 %collective-permute-start.19 = (bf16[128,1024]{1,0:T(8,128)(2,1)S(1)}, bf16[128,1024]{1,0:T(8,128)(2,1)S(1)}, u32[]{:S(2)}, u32[]{:S(2)}) collective-permute-start(bf16[128,1024]{1,0:T(8,128)(2,1)S(1)} %get-tuple-element.45), channel_id=1, source_target_pairs={{0,64},{1,65},{2,66},{3,67},{4,68},{5,69},{6,70},{7,71},{8,72},{9,... | collective-permute-start | bytes 786440 | tf_op jit(solution)/shard_map/ppermute | solution.py:51
  38.6 0.2 collective-permute-done.17.refs_3_.refs_12_.refs_10_
  38.8 1.8 %collective-permute-start.12 = (bf16[128,1024]{1,0:T(8,128)(2,1)S(1)}, bf16[128,1024]{1,0:T(8,128)(2,1)S(1)}, u32[]{:S(2)}, u32[]{:S(2)}) collective-permute-start(bf16[128,1024]{1,0:T(8,128)(2,1)S(1)} %get-tuple-element.36), channel_id=1, source_target_pairs={{0,32},{1,33},{2,34},{3,35},{4,36},{5,37},{6,38},{7,39},{8,40},{9,... | collective-permute-start | bytes 786440 | tf_op jit(solution)/shard_map/ppermute | solution.py:51
  40.6 1.6 %collective-permute-done.18.refs_4_.refs_13_.refs_11_ = bf16[128,1024]{1,0:T(8,128)(2,1)S(1)} collective-permute-done((bf16[128,1024]{1,0:T(8,128)(2,1)S(1)}, bf16[128,1024]{1,0:T(8,128)(2,1)S(1)}, u32[]{:S(2)}, u32[]{:S(2)}) %collective-permute-start.18) | collective-permute-done | bytes 262176 | tf_op jit(solution)/shard_map/ppermute | solution.py:51
  42.2 2.2 %collective-permute-start.13 = (bf16[128,1024]{1,0:T(8,128)(2,1)S(1)}, bf16[128,1024]{1,0:T(8,128)(2,1)S(1)}, u32[]{:S(2)}, u32[]{:S(2)}) collective-permute-start(bf16[128,1024]{1,0:T(8,128)(2,1)S(1)} %get-tuple-element.37), channel_id=1, source_target_pairs={{0,96},{1,97},{2,98},{3,99},{4,100},{5,101},{6,102},{7,103},{8,104... | collective-permute-start | bytes 786440 | tf_op jit(solution)/shard_map/ppermute | solution.py:51
  44.4 4.3 %collective-permute-done.19.refs_5_.refs_14_.refs_12_ = bf16[128,1024]{1,0:T(8,128)(2,1)S(1)} collective-permute-done((bf16[128,1024]{1,0:T(8,128)(2,1)S(1)}, bf16[128,1024]{1,0:T(8,128)(2,1)S(1)}, u32[]{:S(2)}, u32[]{:S(2)}) %collective-permute-start.19) | collective-permute-done | bytes 262176 | tf_op jit(solution)/shard_map/ppermute | solution.py:51
  48.8 0.0 collective-permute-start.15
  48.8 2.6 %collective-permute-done.12.refs_3_.refs_5_ = bf16[128,1024]{1,0:T(8,128)(2,1)S(1)} collective-permute-done((bf16[128,1024]{1,0:T(8,128)(2,1)S(1)}, bf16[128,1024]{1,0:T(8,128)(2,1)S(1)}, u32[]{:S(2)}, u32[]{:S(2)}) %collective-permute-start.12) | collective-permute-done | bytes 262176 | tf_op jit(solution)/shard_map/ppermute | solution.py:51
  51.4 0.0 collective-permute-start.16
  51.4 0.0 collective-permute-done.10.refs_2_
  51.4 0.0 collective-permute-start.11
  51.4 0.0 collective-permute-done.6.refs_0_
  51.4 2.7 %collective-permute-start.7 = (bf16[512,512]{1,0:T(8,128)(2,1)S(1)}, bf16[512,512]{1,0:T(8,128)(2,1)S(1)}, u32[]{:S(2)}, u32[]{:S(2)}) collective-permute-start(bf16[512,512]{1,0:T(8,128)(2,1)S(1)} %collective-permute-done.6.refs_0_), channel_id=1, source_target_pairs={{0,2},{1,9},{2,4},{3,11},{4,6},{5,13},{6,0},{7,15},{8,10},{9,17},{... | collective-permute-start | bytes 1572872 | tf_op jit(solution)/shard_map/ppermute | solution.py:51
  54.2 0.0 collective-permute-done.13.refs_4_.refs_6_
  54.2 2.1 %collective-permute-start.14 = (bf16[128,1024]{1,0:T(8,128)(2,1)S(1)}, bf16[128,1024]{1,0:T(8,128)(2,1)S(1)}, u32[]{:S(2)}, u32[]{:S(2)}) collective-permute-start(bf16[128,1024]{1,0:T(8,128)(2,1)S(1)} %get-tuple-element.38), channel_id=1, source_target_pairs={{0,64},{1,65},{2,66},{3,67},{4,68},{5,69},{6,70},{7,71},{8,72},{9,... | collective-permute-start | bytes 786440 | tf_op jit(solution)/shard_map/ppermute | solution.py:51
  56.2 3.3 %shard_map.58 = (f32[2,128,512]{2,1,0:T(8,128)S(1)}, f32[2,8,512]{2,1,0:T(8,128)S(1)}, f32[2,8,512]{2,1,0:T(8,128)S(1)}) custom-call(s32[4,32]{1,0:T(4,128)} %sequence_ref.7, s32[4,32]{1,0:T(4,128)} %order_ref.11, bf16[512,512]{1,0:T(8,128)(2,1)S(1)} %pad_maximum_fusion.refs_0_, bf16[512,512]{1,0:T(8,128)(2,1)S(1)} %constant_dynamic-update-slice_fusion.refs_1_, ...), custom_call_target="tpu_custom_call" | custom-call | flops 268435456 | bytes 2097152 | tf_op jit(solution)/shard_map/pallas_call | solution.py:329
  59.5 1.4 %collective-permute-done.14.refs_5_.refs_7_ = bf16[128,1024]{1,0:T(8,128)(2,1)S(1)} collective-permute-done((bf16[128,1024]{1,0:T(8,128)(2,1)S(1)}, bf16[128,1024]{1,0:T(8,128)(2,1)S(1)}, u32[]{:S(2)}, u32[]{:S(2)}) %collective-permute-start.14) | collective-permute-done | bytes 262176 | tf_op jit(solution)/shard_map/ppermute | solution.py:51
  60.9 3.5 %shard_map.57 = (f32[2,128,512]{2,1,0:T(8,128)S(1)}, f32[2,8,512]{2,1,0:T(8,128)S(1)}, f32[2,8,512]{2,1,0:T(8,128)S(1)}) custom-call(s32[4,32]{1,0:T(4,128)} %sequence_ref.7, s32[4,32]{1,0:T(4,128)} %order_ref.11, bf16[512,512]{1,0:T(8,128)(2,1)S(1)} %pad_maximum_fusion.refs_0_, bf16[512,512]{1,0:T(8,128)(2,1)S(1)} %constant_dynamic-update-slice_fusion.refs_1_, ...), custom_call_target="tpu_custom_call" | custom-call | flops 268435456 | bytes 2097152 | tf_op jit(solution)/shard_map/pallas_call | solution.py:329
  64.4 0.0 collective-permute-done.15.refs_1_
  64.4 5.3 %shard_map.59 = (f32[2,128,512]{2,1,0:T(8,128)S(1)}, f32[2,8,512]{2,1,0:T(8,128)S(1)}, f32[2,8,512]{2,1,0:T(8,128)S(1)}, f32[2,128,512]{2,1,0:T(8,128)S(1)}, f32...) custom-call(s32[4,32]{1,0:T(4,128)} %sequence_ref.7, s32[4,32]{1,0:T(4,128)} %order_ref.11, ...), custom_call_target="tpu_custom_call" | custom-call | flops 536870912 | bytes 2097152 | tf_op jit(solution)/shard_map/pallas_call | solution.py:329
  69.7 0.0 collective-permute-done.7.refs_0_
  69.7 4.1 %shard_map.60 = (bf16[128,1024]{1,0:T(8,128)(2,1)S(1)}, bf16[128,1024]{1,0:T(8,128)(2,1)S(1)}) custom-call(s32[4,32]{1,0:T(4,128)} %sequence_ref.7, s32[4,32]{1,0:T(4,128)} %order_ref.11, bf16[512,512]{1,0:T(8,128)(2,1)S(1)} %collective-permute-done.7.refs_0_, bf16[512,512]{1,0:T(8,128)(2,1)S(1)} %collective-permute-done.11.refs_1_, ...), custom_call_target="tpu_custom_call" | custom-call | flops 268435456 | bytes 2097152 | tf_op jit(solution)/shard_map/pallas_call | solution.py:329
  73.8 9.4 %collective-permute-start.20 = (bf16[128,1024]{1,0:T(8,128)(2,1)S(1)}, bf16[128,1024]{1,0:T(8,128)(2,1)S(1)}, u32[]{:S(2)}, u32[]{:S(2)}) collective-permute-start(bf16[128,1024]{1,0:T(8,128)(2,1)S(1)} %get-tuple-element.56), channel_id=1, source_target_pairs={{0,1},{1,0},{2,3},{3,2},{4,5},{5,4},{6,7},{7,6},{8,9},{9,8},{10,11... | collective-permute-start | bytes 786440 | tf_op jit(solution)/shard_map/ppermute | solution.py:51
  83.2 1.2 %collective-permute-done.20.received_ref = bf16[128,1024]{1,0:T(8,128)(2,1)S(1)} collective-permute-done((bf16[128,1024]{1,0:T(8,128)(2,1)S(1)}, bf16[128,1024]{1,0:T(8,128)(2,1)S(1)}, u32[]{:S(2)}, u32[]{:S(2)}) %collective-permute-start.20) | collective-permute-done | bytes 262176 | tf_op jit(solution)/shard_map/ppermute | solution.py:51
  84.3 0.8 join.1
  (5 shorter events, 0.1 us)
Async XLA Ops:
  0.0 3.2 %collective-permute-start.1 = (bf16[128,4096]{1,0:T(8,128)(2,1)}, bf16[128,4096]{1,0:T(8,128)(2,1)S(1)}, u32[]{:S(2)}, u32[]{:S(2)}) collective-permute-start(bf16[128,4096]{1,0:T(8,128)(2,1)} %bitcast.3), channel_id=1, source_target_pairs={{0,1},{1,0},{2,3},{3,2},{4,5},{5,4},{6,7},{7,6},{8,9},{9,8},{10,11... | collective-permute-start | bytes 3145736 | tf_op jit(solution)/shard_map/ppermute | solution.py:51
  0.7 2.5 %collective-permute-start = (s32[1,1]{1,0:T(1,128)}, s32[1,1]{1,0:T(1,128)}, u32[]{:S(2)}, u32[]{:S(2)}) collective-permute-start(s32[1,1]{1,0:T(1,128)} %param.7), channel_id=1, source_target_pairs={{0,1},{1,0},{2,3},{3,2},{4,5},{5,4},{6,7},{7,6},{8,9},{9,8},{10,11... | collective-permute-start | bytes 20 | tf_op jit(solution)/shard_map/ppermute | solution.py:51
  8.1 7.6 %collective-permute-start.2 = (bf16[256,512]{1,0:T(8,128)(2,1)S(1)}, bf16[256,512]{1,0:T(8,128)(2,1)S(1)}, u32[]{:S(2)}, u32[]{:S(2)}) collective-permute-start(bf16[256,512]{1,0:T(8,128)(2,1)S(1)} %get-tuple-element.32), channel_id=1, source_target_pairs={{0,32},{1,33},{2,34},{3,35},{4,36},{5,37},{6,38},{7,39},{8,40},{9,... | collective-permute-start | bytes 786440 | tf_op jit(solution)/shard_map/ppermute | solution.py:51
  9.4 7.2 %collective-permute-start.3 = (bf16[256,512]{1,0:T(8,128)(2,1)S(1)}, bf16[256,512]{1,0:T(8,128)(2,1)S(1)}, u32[]{:S(2)}, u32[]{:S(2)}) collective-permute-start(bf16[256,512]{1,0:T(8,128)(2,1)S(1)} %get-tuple-element.33), channel_id=1, source_target_pairs={{0,96},{1,97},{2,98},{3,99},{4,100},{5,101},{6,102},{7,103},{8,104... | collective-permute-start | bytes 786440 | tf_op jit(solution)/shard_map/ppermute | solution.py:51
  9.6 13.2 %collective-permute-start.4 = (bf16[256,512]{1,0:T(8,128)(2,1)S(1)}, bf16[256,512]{1,0:T(8,128)(2,1)S(1)}, u32[]{:S(2)}, u32[]{:S(2)}) collective-permute-start(bf16[256,512]{1,0:T(8,128)(2,1)S(1)} %get-tuple-element.34), channel_id=1, source_target_pairs={{0,64},{1,65},{2,66},{3,67},{4,68},{5,69},{6,70},{7,71},{8,72},{9,... | collective-permute-start | bytes 786440 | tf_op jit(solution)/shard_map/ppermute | solution.py:51
  22.9 10.1 %collective-permute-start.8 = (bf16[256,512]{1,0:T(8,128)(2,1)S(1)}, bf16[256,512]{1,0:T(8,128)(2,1)S(1)}, u32[]{:S(2)}, u32[]{:S(2)}) collective-permute-start(bf16[256,512]{1,0:T(8,128)(2,1)S(1)} %add_add_fusion), channel_id=1, source_target_pairs={{0,24},{1,7},{2,26},{3,1},{4,28},{5,3},{6,30},{7,5},{8,0},{9,15},{... | collective-permute-start | bytes 786440 | tf_op jit(solution)/shard_map/ppermute | solution.py:51
  23.1 9.9 %collective-permute-start.9 = (bf16[256,512]{1,0:T(8,128)(2,1)S(1)}, bf16[256,512]{1,0:T(8,128)(2,1)S(1)}, u32[]{:S(2)}, u32[]{:S(2)}) collective-permute-start(bf16[256,512]{1,0:T(8,128)(2,1)S(1)} %add_add_fusion), channel_id=1, source_target_pairs={{0,16},{1,5},{2,18},{3,7},{4,20},{5,1},{6,22},{7,3},{8,24},{9,13},... | collective-permute-start | bytes 786440 | tf_op jit(solution)/shard_map/ppermute | solution.py:51
  25.7 7.5 %collective-permute-start.5 = (bf16[256,512]{1,0:T(8,128)(2,1)S(1)}, bf16[256,512]{1,0:T(8,128)(2,1)S(1)}, u32[]{:S(2)}, u32[]{:S(2)}) collective-permute-start(bf16[256,512]{1,0:T(8,128)(2,1)S(1)} %add_add_fusion), channel_id=1, source_target_pairs={{0,8},{1,3},{2,10},{3,5},{4,12},{5,7},{6,14},{7,1},{8,16},{9,11},{... | collective-permute-start | bytes 786440 | tf_op jit(solution)/shard_map/ppermute | solution.py:51
  32.9 5.9 %collective-permute-start.17 = (bf16[128,1024]{1,0:T(8,128)(2,1)S(1)}, bf16[128,1024]{1,0:T(8,128)(2,1)S(1)}, u32[]{:S(2)}, u32[]{:S(2)}) collective-permute-start(bf16[128,1024]{1,0:T(8,128)(2,1)S(1)} %get-tuple-element.43), channel_id=1, source_target_pairs={{0,32},{1,33},{2,34},{3,35},{4,36},{5,37},{6,38},{7,39},{8,40},{9,... | collective-permute-start | bytes 786440 | tf_op jit(solution)/shard_map/ppermute | solution.py:51
  33.0 18.4 %collective-permute-start.10 = (bf16[512,512]{1,0:T(8,128)(2,1)S(1)}, bf16[512,512]{1,0:T(8,128)(2,1)S(1)}, u32[]{:S(2)}, u32[]{:S(2)}) collective-permute-start(bf16[512,512]{1,0:T(8,128)(2,1)S(1)} %constant_dynamic-update-slice_fusion.refs_1_), channel_id=1, source_target_pairs={{0,6},{1,25},{2,0},{3,27},{4,2},{5,29},{6,4},{7,31},{8,14},{9,1},{... | collective-permute-start | bytes 1572872 | tf_op jit(solution)/shard_map/ppermute | solution.py:51
  33.3 18.1 %collective-permute-start.6 = (bf16[512,512]{1,0:T(8,128)(2,1)S(1)}, bf16[512,512]{1,0:T(8,128)(2,1)S(1)}, u32[]{:S(2)}, u32[]{:S(2)}) collective-permute-start(bf16[512,512]{1,0:T(8,128)(2,1)S(1)} %pad_maximum_fusion.refs_0_), channel_id=1, source_target_pairs={{0,2},{1,9},{2,4},{3,11},{4,6},{5,13},{6,0},{7,15},{8,10},{9,17},{... | collective-permute-start | bytes 1572872 | tf_op jit(solution)/shard_map/ppermute | solution.py:51
  35.9 6.3 %collective-permute-start.18 = (bf16[128,1024]{1,0:T(8,128)(2,1)S(1)}, bf16[128,1024]{1,0:T(8,128)(2,1)S(1)}, u32[]{:S(2)}, u32[]{:S(2)}) collective-permute-start(bf16[128,1024]{1,0:T(8,128)(2,1)S(1)} %get-tuple-element.44), channel_id=1, source_target_pairs={{0,96},{1,97},{2,98},{3,99},{4,100},{5,101},{6,102},{7,103},{8,104... | collective-permute-start | bytes 786440 | tf_op jit(solution)/shard_map/ppermute | solution.py:51
  37.3 11.4 %collective-permute-start.19 = (bf16[128,1024]{1,0:T(8,128)(2,1)S(1)}, bf16[128,1024]{1,0:T(8,128)(2,1)S(1)}, u32[]{:S(2)}, u32[]{:S(2)}) collective-permute-start(bf16[128,1024]{1,0:T(8,128)(2,1)S(1)} %get-tuple-element.45), channel_id=1, source_target_pairs={{0,64},{1,65},{2,66},{3,67},{4,68},{5,69},{6,70},{7,71},{8,72},{9,... | collective-permute-start | bytes 786440 | tf_op jit(solution)/shard_map/ppermute | solution.py:51
  38.8 12.6 %collective-permute-start.12 = (bf16[128,1024]{1,0:T(8,128)(2,1)S(1)}, bf16[128,1024]{1,0:T(8,128)(2,1)S(1)}, u32[]{:S(2)}, u32[]{:S(2)}) collective-permute-start(bf16[128,1024]{1,0:T(8,128)(2,1)S(1)} %get-tuple-element.36), channel_id=1, source_target_pairs={{0,32},{1,33},{2,34},{3,35},{4,36},{5,37},{6,38},{7,39},{8,40},{9,... | collective-permute-start | bytes 786440 | tf_op jit(solution)/shard_map/ppermute | solution.py:51
  42.2 12.0 %collective-permute-start.13 = (bf16[128,1024]{1,0:T(8,128)(2,1)S(1)}, bf16[128,1024]{1,0:T(8,128)(2,1)S(1)}, u32[]{:S(2)}, u32[]{:S(2)}) collective-permute-start(bf16[128,1024]{1,0:T(8,128)(2,1)S(1)} %get-tuple-element.37), channel_id=1, source_target_pairs={{0,96},{1,97},{2,98},{3,99},{4,100},{5,101},{6,102},{7,103},{8,104... | collective-permute-start | bytes 786440 | tf_op jit(solution)/shard_map/ppermute | solution.py:51
  48.8 15.6 %collective-permute-start.15 = (bf16[512,512]{1,0:T(8,128)(2,1)S(1)}, bf16[512,512]{1,0:T(8,128)(2,1)S(1)}, u32[]{:S(2)}, u32[]{:S(2)}) collective-permute-start(bf16[512,512]{1,0:T(8,128)(2,1)S(1)} %constant_dynamic-update-slice_fusion.refs_1_), channel_id=1, source_target_pairs={{0,2},{1,9},{2,4},{3,11},{4,6},{5,13},{6,0},{7,15},{8,10},{9,17},{... | collective-permute-start | bytes 1572872 | tf_op jit(solution)/shard_map/ppermute | solution.py:51
  51.4 13.0 %collective-permute-start.16 = (bf16[512,512]{1,0:T(8,128)(2,1)S(1)}, bf16[512,512]{1,0:T(8,128)(2,1)S(1)}, u32[]{:S(2)}, u32[]{:S(2)}) collective-permute-start(bf16[512,512]{1,0:T(8,128)(2,1)S(1)} %pad_maximum_fusion.refs_0_), channel_id=1, source_target_pairs={{0,6},{1,25},{2,0},{3,27},{4,2},{5,29},{6,4},{7,31},{8,14},{9,1},{... | collective-permute-start | bytes 1572872 | tf_op jit(solution)/shard_map/ppermute | solution.py:51
  51.4 18.3 %collective-permute-start.11 = (bf16[512,512]{1,0:T(8,128)(2,1)S(1)}, bf16[512,512]{1,0:T(8,128)(2,1)S(1)}, u32[]{:S(2)}, u32[]{:S(2)}) collective-permute-start(bf16[512,512]{1,0:T(8,128)(2,1)S(1)} %collective-permute-done.10.refs_2_), channel_id=1, source_target_pairs={{0,6},{1,25},{2,0},{3,27},{4,2},{5,29},{6,4},{7,31},{8,14},{9,1},{... | collective-permute-start | bytes 1572872 | tf_op jit(solution)/shard_map/ppermute | solution.py:51
  51.4 18.3 %collective-permute-start.7 = (bf16[512,512]{1,0:T(8,128)(2,1)S(1)}, bf16[512,512]{1,0:T(8,128)(2,1)S(1)}, u32[]{:S(2)}, u32[]{:S(2)}) collective-permute-start(bf16[512,512]{1,0:T(8,128)(2,1)S(1)} %collective-permute-done.6.refs_0_), channel_id=1, source_target_pairs={{0,2},{1,9},{2,4},{3,11},{4,6},{5,13},{6,0},{7,15},{8,10},{9,17},{... | collective-permute-start | bytes 1572872 | tf_op jit(solution)/shard_map/ppermute | solution.py:51
  54.2 6.7 %collective-permute-start.14 = (bf16[128,1024]{1,0:T(8,128)(2,1)S(1)}, bf16[128,1024]{1,0:T(8,128)(2,1)S(1)}, u32[]{:S(2)}, u32[]{:S(2)}) collective-permute-start(bf16[128,1024]{1,0:T(8,128)(2,1)S(1)} %get-tuple-element.38), channel_id=1, source_target_pairs={{0,64},{1,65},{2,66},{3,67},{4,68},{5,69},{6,70},{7,71},{8,72},{9,... | collective-permute-start | bytes 786440 | tf_op jit(solution)/shard_map/ppermute | solution.py:51
  73.8 10.6 %collective-permute-start.20 = (bf16[128,1024]{1,0:T(8,128)(2,1)S(1)}, bf16[128,1024]{1,0:T(8,128)(2,1)S(1)}, u32[]{:S(2)}, u32[]{:S(2)}) collective-permute-start(bf16[128,1024]{1,0:T(8,128)(2,1)S(1)} %get-tuple-element.56), channel_id=1, source_target_pairs={{0,1},{1,0},{2,3},{3,2},{4,5},{5,4},{6,7},{7,6},{8,9},{9,8},{10,11... | collective-permute-start | bytes 786440 | tf_op jit(solution)/shard_map/ppermute | solution.py:51

commit v4 on v3

--- a/solution.py
+++ b/solution.py
@@ -51,82 +51,132 @@
     return lax.ppermute(value, AXES, table)
 
 
-def rope_tables(order, slot, cos_ref, sin_ref):
+def rope_tables(order, cos_ref, sin_ref):
     lane = lax.broadcasted_iota(jnp.int32, (SLAB, HD), 1)
     half = jnp.where(lane < HD // 2, lane, lane - HD // 2).astype(jnp.float32)
     frequency = jnp.exp(half * (-2.0 / HD * 13.122363377404328))
     row = lax.broadcasted_iota(jnp.int32, (SLAB, HD), 0)
     angle = (order * SLAB + row).astype(jnp.float32) * frequency
-    cos_ref[slot] = jnp.cos(angle)
+    cos_ref[...] = jnp.cos(angle)
     sine = jnp.sin(angle)
-    sin_ref[slot] = jnp.where(lane < HD // 2, -sine, sine)
-
-
-def rope(block, slot, cos_ref, sin_ref):
-    return block * cos_ref[slot] + pltpu.roll(block, HD // 2, 1) * sin_ref[slot]
-
-
-def begin(core_ref, other_ref, owner_ref, order_ref, cos_ref, sin_ref):
-    column = lax.axis_index("cp")
-    owners = (other_ref[0, 0], owner_ref[0, 0])
-    columns = (column + 1 - 2 * core_ref[0], column)
-
-    @pl.when(pl.program_id(0) == 0)
-    def _():
-        for slot in range(2):
-            rope_tables(order_ref[owners[slot], columns[slot]], slot, cos_ref, sin_ref)
-
-    return owners
+    sin_ref[...] = jnp.where(lane < HD // 2, -sine, sine)
+
+
+def rope(block, table):
+    return block * table[0][...] + pltpu.roll(block, HD // 2, 1) * table[1][...]
+
+
+CHUNKS = 4
+
+
+def prepare_kernel(core_ref, owner_ref, order_ref, x_ref, w_ref, *refs):
+    x_out, w_out, cos_ref, sin_ref, sems = refs
+    core = core_ref[0]
+    width = 2 * HD
+    rows = w_out.shape[0] // CHUNKS
+    copies = [pltpu.make_async_copy(x_ref, x_out, sems.at[2 * CHUNKS])]
+    for part in range(2):
+        base = pl.multiple_of((QH + part * KVH) * HD + core * width, width)
+        for n in range(CHUNKS):
+            piece = pl.ds(n * rows, rows)
+            copies.append(
+                pltpu.make_async_copy(
+                    w_ref.at[piece, pl.ds(base, width)],
+                    w_out.at[piece, part * width : (part + 1) * width],
+                    sems.at[part * CHUNKS + n],
+                )
+            )
+    for copy in copies:
+        copy.start()
+    rope_tables(order_ref[owner_ref[0, 0], lax.axis_index("cp")], cos_ref, sin_ref)
+    for copy in copies:
+        copy.wait()
+
+
+def prepare(core, owner, slab_order, rows, weight):
+    smem = pl.BlockSpec(memory_space=pltpu.SMEM)
+    anywhere = pl.BlockSpec(memory_space=pl.ANY)
+    vmem = pl.BlockSpec(memory_space=pltpu.VMEM)
+    depth = rows.shape[1]
+    return pl.pallas_call(
+        prepare_kernel,
+        in_specs=[smem] * 3 + [anywhere] * 2,
+        out_specs=[vmem] * 4,
+        out_shape=[
+            pltpu.VMEM(rows.shape, rows.dtype),
+            pltpu.VMEM((depth, 4 * HD), weight.dtype),
+            pltpu.VMEM((SLAB, HD), jnp.float32),
+            pltpu.VMEM((SLAB, HD), jnp.float32),
+        ],
+        scratch_shapes=[pltpu.SemaphoreType.DMA((2 * CHUNKS + 1,))],
+        compiler_params=pltpu.CompilerParams(vmem_limit_bytes=8 << 20),
+        cost_estimate=pl.CostEstimate(flops=1 << 26, bytes_accessed=5 << 20, transcendentals=1 << 16),
+        name="prepare",
+    )(core, owner, in_hbm(slab_order), in_hbm(rows), in_hbm(weight))
 
 
 def store_masked(outs, owner, rows, first, value):
     my_row = lax.axis_index("dp")
-    columns = pl.ds(pl.multiple_of(first, HD), HD)
+    columns = pl.ds(first if isinstance(first, int) else pl.multiple_of(first, HD), HD)
     for k, out in enumerate(outs):
         mine = owner == lax.rem(my_row + k, SIDE)
         out[rows, columns] = jnp.where(mine, value, jnp.zeros_like(value))
 
 
 def kv_kernel(core_ref, other_ref, owner_ref, order_ref, y_ref, x_ref, w_ref, *refs):
-    outs, (cos_ref, sin_ref) = refs[:4], refs[4:]
-    owners = begin(core_ref, other_ref, owner_ref, order_ref, cos_ref, sin_ref)
+    ropes, outs = (refs[2:4], refs[:2]), refs[4:]
+    column = lax.axis_index("cp") + 1 - 2 * core_ref[0]
+    rope_tables(order_ref[other_ref[0, 0], column], *ropes[0])
+    owners = (other_ref[0, 0], owner_ref[0, 0])
     both = jnp.concatenate([y_ref[...], x_ref[...]], axis=0)
-    projected = jnp.dot(both, w_ref[...], preferred_element_type=jnp.float32)
-    heads = w_ref.shape[1] // HD
-    step = pl.program_id(0)
-
-    @pl.when(step < 2 // heads)
-    def _():
+    wide = 512
+    for first in range(0, 4 * HD, wide):
+        projected = jnp.dot(
+            both, w_ref[:, first : first + wide], preferred_element_type=jnp.float32
+        )
         for slot in range(2):
             rows = slice(slot * SLAB, (slot + 1) * SLAB)
-            for h in range(heads):
-                columns = slice(h * HD, (h + 1) * HD)
-                value = rope(projected[rows, columns], slot, cos_ref, sin_ref).astype(jnp.bfloat16)
-                store_masked(outs, owners[slot], rows, (step * heads + h) * HD, value)
-
-    @pl.when(step >= 2 // heads)
-    def _():
+            for h in range(wide // HD):
+                block = projected[rows, h * HD : (h + 1) * HD]
+                if first + h * HD < 2 * HD:
+                    value = rope(block, ropes[slot]).astype(jnp.bfloat16)
+                else:
+                    value = block.T.astype(jnp.bfloat16)
+                store_masked(outs, owners[slot], rows, first + h * HD, value)
+
+
+def q_kernel(core_ref, other_ref, owner_ref, w_ref, y_ref, x_ref, *refs):
+    ropes, outs = (refs[:2], refs[2:4]), refs[4:12]
+    w_scr, sems = refs[12:]
+    owners = (other_ref[0, 0], owner_ref[0, 0])
+    depth, width = w_scr.shape[1:]
+    rows = depth // CHUNKS
+    copies = []
+    for part in range(QPARTS):
+        base = pl.multiple_of(core_ref[0] * HALF + part * width, width)
+        for n in range(CHUNKS):
+            piece = pl.ds(n * rows, rows)
+            copies.append(
+                pltpu.make_async_copy(
+                    w_ref.at[piece, pl.ds(base, width)],
+                    w_scr.at[part, piece, :],
+                    sems.at[part * CHUNKS + n],
+                )
+            )
+    for copy in copies:
+        copy.start()
+    for part in range(QPARTS):
+        for copy in copies[part * CHUNKS : (part + 1) * CHUNKS]:
+            copy.wait()
+        both = jnp.concatenate([y_ref[...], x_ref[...]], axis=0)
+        projected = jnp.dot(both, w_scr[part], preferred_element_type=jnp.float32)
         for slot in range(2):
-            rows = slice(slot * SLAB, (slot + 1) * SLAB)
-            for h in range(heads):
-                columns = slice(h * HD, (h + 1) * HD)
-                value = projected[rows, columns].T.astype(jnp.bfloat16)
-                store_masked(outs, owners[slot], rows, (step * heads + h) * HD, value)
-
-
-def q_kernel(core_ref, other_ref, owner_ref, order_ref, y_ref, x_ref, w_ref, *refs):
-    outs, (cos_ref, sin_ref) = refs[:8], refs[8:]
-    owners = begin(core_ref, other_ref, owner_ref, order_ref, cos_ref, sin_ref)
-    both = jnp.concatenate([y_ref[...], x_ref[...]], axis=0)
-    projected = jnp.dot(both, w_ref[...], preferred_element_type=jnp.float32)
-    heads = w_ref.shape[1] // HD
-    for slot in range(2):
-        for h in range(heads):
-            columns = slice(h * HD, (h + 1) * HD)
-            first = (pl.program_id(0) * heads + h) * HD
-            block = projected[slot * SLAB : (slot + 1) * SLAB, columns]
-            value = rope(block, slot, cos_ref, sin_ref).T.astype(jnp.bfloat16)
-            store_masked(outs[4 * slot : 4 * slot + 4], owners[slot], slice(None), first, value)
+            for h in range(width // HD):
+                block = projected[slot * SLAB : (slot + 1) * SLAB, h * HD : (h + 1) * HD]
+                value = rope(block, ropes[slot]).T.astype(jnp.bfloat16)
+                store_masked(
+                    outs[4 * slot : 4 * slot + 4], owners[slot], slice(None), part * width + h * HD, value
+                )
 
 
 def in_vmem(value):
@@ -137,35 +187,47 @@
     return pltpu.with_memory_space_constraint(value, pltpu.HBM)
 
 
-def project(kernel, core, owners, slab_order, others, rows, weight, block, blocks, width, out):
-    depth = rows.shape[1]
+def project_kv(core, owners, slab_order, others, rows, weight, tables):
     smem = pl.BlockSpec(memory_space=pltpu.SMEM)
+    vmem = pl.BlockSpec(memory_space=pltpu.VMEM)
+    operands = [in_vmem(v) for v in (others, rows, weight, *tables)]
     return pl.pallas_call(
-        kernel,
-        grid_spec=pltpu.PrefetchScalarGridSpec(
-            num_scalar_prefetch=1,
-            grid=(blocks,),
-            in_specs=[
-                smem,
-                smem,
-                smem,
-                pl.BlockSpec(memory_space=pltpu.VMEM),
-                pl.BlockSpec((SLAB, depth), lambda j, c: (0, 0)),
-                pl.BlockSpec((depth, width), lambda j, c: (0, block(j, c[0]))),
-            ],
-            out_specs=[pl.BlockSpec(memory_space=pltpu.VMEM)] * len(out),
-            scratch_shapes=[pltpu.VMEM((2, SLAB, HD), jnp.float32)] * 2,
+        kv_kernel,
+        in_specs=[smem] * 4 + [vmem] * len(operands),
+        out_specs=[vmem] * 6,
+        out_shape=[pltpu.VMEM((SLAB, HD), jnp.float32)] * 2
+        + [pltpu.VMEM((2 * SLAB, 4 * HD), jnp.bfloat16)] * 4,
+        compiler_params=pltpu.CompilerParams(vmem_limit_bytes=24 << 20),
+        cost_estimate=pl.CostEstimate(
+            flops=4 * SLAB * rows.shape[1] * 4 * HD, bytes_accessed=4 << 20, transcendentals=0
         ),
-        out_shape=out,
-        compiler_params=pltpu.CompilerParams(
-            dimension_semantics=("arbitrary",), vmem_limit_bytes=24 << 20
+        name="kv_proj",
+    )(core, *owners, in_hbm(slab_order), *operands)
+
+
+QPARTS = 2
+
+
+def project_q(core, owners, others, rows, weight, tables):
+    depth, width = rows.shape[1], HALF // QPARTS
+    smem = pl.BlockSpec(memory_space=pltpu.SMEM)
+    vmem = pl.BlockSpec(memory_space=pltpu.VMEM)
+    operands = [in_vmem(v) for v in (others, rows, *tables)]
+    return pl.pallas_call(
+        q_kernel,
+        in_specs=[smem] * 3 + [pl.BlockSpec(memory_space=pl.ANY)] + [vmem] * len(operands),
+        out_specs=[vmem] * 8,
+        out_shape=[pltpu.VMEM((SLAB, HALF), jnp.bfloat16)] * 8,
+        scratch_shapes=[
+            pltpu.VMEM((QPARTS, depth, width), weight.dtype),
+            pltpu.SemaphoreType.DMA((QPARTS * CHUNKS,)),
+        ],
+        compiler_params=pltpu.CompilerParams(vmem_limit_bytes=28 << 20),
+        cost_estimate=pl.CostEstimate(
+            flops=4 * SLAB * depth * HALF, bytes_accessed=2 * depth * HALF, transcendentals=0
         ),
-        cost_estimate=pl.CostEstimate(
-            flops=4 * SLAB * depth * blocks * width,
-            bytes_accessed=2 * depth * (2 * SLAB + blocks * width),
-            transcendentals=0,
-        ),
-    )(core, *owners, in_hbm(slab_order), in_vmem(others), in_hbm(rows), in_hbm(weight))
+        name="q_proj",
+    )(core, *owners, in_hbm(weight), *operands)
 
 
 FACTOR = HD**-0.5 * 1.4426950408889634
@@ -365,15 +427,13 @@
     core = lax.rem(lax.axis_index("cp"), 2)
     others = permute(rows, OTHER_CORE)
     owners = (permute(owner_slot, OTHER_CORE), owner_slot)
-    common = (core.reshape(1), owners, slab_order, others, rows, qkv_weight)
-    kv = project(
-        kv_kernel, *common, lambda j, c: QH // 2 + 2 * j + c, 2, 2 * HD,
-        [pltpu.VMEM((2 * SLAB, 4 * HD), jnp.bfloat16)] * 4,
+    core = core.reshape(1)
+    rows, kv_weight, *tables = prepare(core, owner_slot, slab_order, rows, qkv_weight)
+    other_cos, other_sin, *kv = project_kv(
+        core, owners, slab_order, others, rows, kv_weight, tables
     )
-    queries = project(
-        q_kernel, *common, lambda j, c: 2 * c + j, 2, 4 * HD,
-        [pltpu.VMEM((SLAB, HALF), jnp.bfloat16)] * 8,
-    )
+    tables = (other_cos, other_sin, *tables)
+    queries = project_q(core, owners, others, rows, qkv_weight, tables)
     moved = [permute(kv[k], shift_x(k)) for k in (1, 3, 2)]
     parts = [[queries[0]] + [permute(queries[k], shift_x(k)) for k in (1, 3, 2)]]
     own = kv[0] + moved[0] + moved[1] + moved[2]
@@ -395,7 +455,7 @@
     state = [both[:3], both[3:]]
     sent, kept = attend([(0, 0, False), (1, 0, False)], *tables, far_items, parts, state, True)
     received = permute(sent, OTHER_CORE)
-    return join(core.reshape(1), kept, received)[None]
+    return join(core, kept, received)[None]
 
 
 def solution(mesh):

time: 85.4 us -> 81.6 us (0.956)
  the two profiles are of different devices: /device:TPU:115 before, /device:TPU:35 now
where the time goes in v4:
time: 81.6 us; the launch traced here: 81.3 us
  starting transfers between devices  37.1 us (45%)
  Pallas kernels  26.1 us (32%)
  waiting for transfers between devices  17.2 us (21%)
  between operations  0.83 us (1%)
    ppermute x21, starting transfers between devices, permute(): return lax.ppermute(value, AXES, table)  37.1 us
    ppermute x21, waiting for transfers between devices, permute(): return lax.ppermute(value, AXES, table)  17.2 us
    pallas_call x4, Pallas kernels, attend(): pl.pallas_call(functools.partial(attend_kernel, jobs, spots, last), in_sp...  12.9 us
    pallas_call x1, Pallas kernels, project_q(): pl.pallas_call(q_kernel, in_specs=[smem] * 3 + [pl.BlockSpec(memory_space...  6.17 us
    pallas_call x1, Pallas kernels, prepare(): pl.pallas_call(prepare_kernel, in_specs=[smem] * 3 + [anywhere] * 2, out_...  3.29 us
    pallas_call x1, Pallas kernels, project_kv(): pl.pallas_call(kv_kernel, in_specs=[smem] * 4 + [vmem] * len(operands), o...  2.91 us
  transfers between devices with their start and end apart: 21, of which 8 were waited for; matrix products, arithmetic and copies ran while one was open for 0% of the time, Pallas kernels for 26%

profile of v4, /device:TPU:35, one launch (start us, length us, event | category | flops | bytes accessed | tf_op | source)
XLA Modules:
  0.0 81.3 jit_solution(5533642105364607552)
XLA Ops:
  0.0 0.7 collective-permute-start.1
  0.7 0.0 collective-permute-start
  1.3 3.3 %prepare.1 = (bf16[128,4096]{1,0:T(8,128)(2,1)S(1)}, bf16[4096,512]{1,0:T(8,128)(2,1)S(1)}, f32[128,128]{1,0:T(8,128)S(1)}, f32[128,128]{1,0:T(8,128)S(1)}) custom-call(s32[1]{0:T(128)} %bitcast.core_ref, s32[1,1]{1,0:T(1,128)S(6)} %copy.7.owner_ref, s32[4,32]{1,0:T(4,128)} %order_ref.11, bf16[128,4096]{1,0:T(8,128)(2,1)} %bitcast.4, bf16[4096,3072]{1,0:T(8,128)(2,1)} %w_ref.3), custom_call_target="tpu_custom_call" | custom-call | flops 67108864 | bytes 5242880 | tf_op jit(solution)/shard_map/prepare/pallas_call | solution.py:101
  4.6 0.0 collective-permute-done.other_ref
  4.6 0.0 collective-permute-done.1.y_ref
  4.7 2.9 %kv_proj.1 = (f32[128,128]{1,0:T(8,128)S(1)}, f32[128,128]{1,0:T(8,128)S(1)}, bf16[256,512]{1,0:T(8,128)(2,1)S(1)}, bf16[256,512]{1,0:T(8,128)(2,1)S(1)}, bf16[2...) custom-call(s32[1]{0:T(128)} %bitcast.core_ref, s32[1,1]{1,0:T(1,128)} %collective-permute-done.other_ref, ...), custom_call_target="tpu_custom_call" | custom-call | flops 1073741824 | bytes 4194304 | tf_op jit(solution)/shard_map/kv_proj/pallas_call | solution.py:194
  7.6 1.3 %collective-permute-start.2 = (bf16[256,512]{1,0:T(8,128)(2,1)S(1)}, bf16[256,512]{1,0:T(8,128)(2,1)S(1)}, u32[]{:S(2)}, u32[]{:S(2)}) collective-permute-start(bf16[256,512]{1,0:T(8,128)(2,1)S(1)} %get-tuple-element.42), channel_id=1, source_target_pairs={{0,32},{1,33},{2,34},{3,35},{4,36},{5,37},{6,38},{7,39},{8,40},{9,... | collective-permute-start | bytes 786440 | tf_op jit(solution)/shard_map/ppermute | solution.py:51
  8.9 0.3 collective-permute-start.3
  9.1 1.8 %collective-permute-start.4 = (bf16[256,512]{1,0:T(8,128)(2,1)S(1)}, bf16[256,512]{1,0:T(8,128)(2,1)S(1)}, u32[]{:S(2)}, u32[]{:S(2)}) collective-permute-start(bf16[256,512]{1,0:T(8,128)(2,1)S(1)} %get-tuple-element.44), channel_id=1, source_target_pairs={{0,64},{1,65},{2,66},{3,67},{4,68},{5,69},{6,70},{7,71},{8,72},{9,... | collective-permute-start | bytes 786440 | tf_op jit(solution)/shard_map/ppermute | solution.py:51
  11.0 4.0 %collective-permute-done.2 = bf16[256,512]{1,0:T(8,128)(2,1)S(1)} collective-permute-done((bf16[256,512]{1,0:T(8,128)(2,1)S(1)}, bf16[256,512]{1,0:T(8,128)(2,1)S(1)}, u32[]{:S(2)}, u32[]{:S(2)}) %collective-permute-start.2) | collective-permute-done | bytes 262176 | tf_op jit(solution)/shard_map/ppermute | solution.py:51
  15.0 0.9 %collective-permute-done.3 = bf16[256,512]{1,0:T(8,128)(2,1)S(1)} collective-permute-done((bf16[256,512]{1,0:T(8,128)(2,1)S(1)}, bf16[256,512]{1,0:T(8,128)(2,1)S(1)}, u32[]{:S(2)}, u32[]{:S(2)}) %collective-permute-start.3) | collective-permute-done | bytes 262176 | tf_op jit(solution)/shard_map/ppermute | solution.py:51
  15.9 6.3 %collective-permute-done.4 = bf16[256,512]{1,0:T(8,128)(2,1)S(1)} collective-permute-done((bf16[256,512]{1,0:T(8,128)(2,1)S(1)}, bf16[256,512]{1,0:T(8,128)(2,1)S(1)}, u32[]{:S(2)}, u32[]{:S(2)}) %collective-permute-start.4) | collective-permute-done | bytes 262176 | tf_op jit(solution)/shard_map/ppermute | solution.py:51
  22.2 0.1 add_add_fusion
  22.2 1.4 %collective-permute-start.5 = (bf16[256,512]{1,0:T(8,128)(2,1)S(1)}, bf16[256,512]{1,0:T(8,128)(2,1)S(1)}, u32[]{:S(2)}, u32[]{:S(2)}) collective-permute-start(bf16[256,512]{1,0:T(8,128)(2,1)S(1)} %add_add_fusion), channel_id=1, source_target_pairs={{0,8},{1,3},{2,10},{3,5},{4,12},{5,7},{6,14},{7,1},{8,16},{9,11},{... | collective-permute-start | bytes 786440 | tf_op jit(solution)/shard_map/ppermute | solution.py:51
  23.6 2.6 %collective-permute-start.9 = (bf16[256,512]{1,0:T(8,128)(2,1)S(1)}, bf16[256,512]{1,0:T(8,128)(2,1)S(1)}, u32[]{:S(2)}, u32[]{:S(2)}) collective-permute-start(bf16[256,512]{1,0:T(8,128)(2,1)S(1)} %add_add_fusion), channel_id=1, source_target_pairs={{0,16},{1,5},{2,18},{3,7},{4,20},{5,1},{6,22},{7,3},{8,24},{9,13},... | collective-permute-start | bytes 786440 | tf_op jit(solution)/shard_map/ppermute | solution.py:51
  26.2 1.1 %collective-permute-start.8 = (bf16[256,512]{1,0:T(8,128)(2,1)S(1)}, bf16[256,512]{1,0:T(8,128)(2,1)S(1)}, u32[]{:S(2)}, u32[]{:S(2)}) collective-permute-start(bf16[256,512]{1,0:T(8,128)(2,1)S(1)} %add_add_fusion), channel_id=1, source_target_pairs={{0,24},{1,7},{2,26},{3,1},{4,28},{5,3},{6,30},{7,5},{8,0},{9,15},{... | collective-permute-start | bytes 786440 | tf_op jit(solution)/shard_map/ppermute | solution.py:51
  27.3 6.2 %q_proj.1 = (bf16[128,1024]{1,0:T(8,128)(2,1)S(1)}, bf16[128,1024]{1,0:T(8,128)(2,1)S(1)}, bf16[128,1024]{1,0:T(8,128)(2,1)S(1)}, bf16[128,1024]{1,0:T(8,128)(2,...) custom-call(s32[1]{0:T(128)} %bitcast.core_ref, ...), custom_call_target="tpu_custom_call" | custom-call | flops 2147483648 | bytes 8388608 | tf_op jit(solution)/shard_map/q_proj/pallas_call | solution.py:216
  33.5 0.1 collective-permute-start.12
  33.5 0.0 collective-permute-done.5
  33.6 1.7 %collective-permute-start.6 = (bf16[512,512]{1,0:T(8,128)(2,1)S(1)}, bf16[512,512]{1,0:T(8,128)(2,1)S(1)}, u32[]{:S(2)}, u32[]{:S(2)}) collective-permute-start(bf16[512,512]{1,0:T(8,128)(2,1)S(1)} %pad_maximum_fusion.refs_0_), channel_id=1, source_target_pairs={{0,2},{1,9},{2,4},{3,11},{4,6},{5,13},{6,0},{7,15},{8,10},{9,17},{... | collective-permute-start | bytes 1572872 | tf_op jit(solution)/shard_map/ppermute | solution.py:51
  35.3 0.0 collective-permute-done.8
  35.4 0.0 collective-permute-done.9
  35.4 0.1 collective-permute-start.10
  35.5 1.5 %collective-permute-start.13 = (bf16[128,1024]{1,0:T(8,128)(2,1)S(1)}, bf16[128,1024]{1,0:T(8,128)(2,1)S(1)}, u32[]{:S(2)}, u32[]{:S(2)}) collective-permute-start(bf16[128,1024]{1,0:T(8,128)(2,1)S(1)} %get-tuple-element.49), channel_id=1, source_target_pairs={{0,96},{1,97},{2,98},{3,99},{4,100},{5,101},{6,102},{7,103},{8,104... | collective-permute-start | bytes 786440 | tf_op jit(solution)/shard_map/ppermute | solution.py:51
  37.0 0.1 collective-permute-start.17
  37.0 1.7 %collective-permute-done.12.refs_3_.refs_5_ = bf16[128,1024]{1,0:T(8,128)(2,1)S(1)} collective-permute-done((bf16[128,1024]{1,0:T(8,128)(2,1)S(1)}, bf16[128,1024]{1,0:T(8,128)(2,1)S(1)}, u32[]{:S(2)}, u32[]{:S(2)}) %collective-permute-start.12) | collective-permute-done | bytes 262176 | tf_op jit(solution)/shard_map/ppermute | solution.py:51
  38.8 2.6 %collective-permute-start.18 = (bf16[128,1024]{1,0:T(8,128)(2,1)S(1)}, bf16[128,1024]{1,0:T(8,128)(2,1)S(1)}, u32[]{:S(2)}, u32[]{:S(2)}) collective-permute-start(bf16[128,1024]{1,0:T(8,128)(2,1)S(1)} %get-tuple-element.56), channel_id=1, source_target_pairs={{0,96},{1,97},{2,98},{3,99},{4,100},{5,101},{6,102},{7,103},{8,104... | collective-permute-start | bytes 786440 | tf_op jit(solution)/shard_map/ppermute | solution.py:51
  41.4 0.0 collective-permute-done.13.refs_4_.refs_6_
  41.4 3.5 %collective-permute-start.19 = (bf16[128,1024]{1,0:T(8,128)(2,1)S(1)}, bf16[128,1024]{1,0:T(8,128)(2,1)S(1)}, u32[]{:S(2)}, u32[]{:S(2)}) collective-permute-start(bf16[128,1024]{1,0:T(8,128)(2,1)S(1)} %get-tuple-element.57), channel_id=1, source_target_pairs={{0,64},{1,65},{2,66},{3,67},{4,68},{5,69},{6,70},{7,71},{8,72},{9,... | collective-permute-start | bytes 786440 | tf_op jit(solution)/shard_map/ppermute | solution.py:51
  44.9 1.9 %collective-permute-start.16 = (bf16[512,512]{1,0:T(8,128)(2,1)S(1)}, bf16[512,512]{1,0:T(8,128)(2,1)S(1)}, u32[]{:S(2)}, u32[]{:S(2)}) collective-permute-start(bf16[512,512]{1,0:T(8,128)(2,1)S(1)} %pad_maximum_fusion.refs_0_), channel_id=1, source_target_pairs={{0,6},{1,25},{2,0},{3,27},{4,2},{5,29},{6,4},{7,31},{8,14},{9,1},{... | collective-permute-start | bytes 1572872 | tf_op jit(solution)/shard_map/ppermute | solution.py:51
  46.8 0.5 collective-permute-done.18.refs_4_.refs_13_.refs_11_
  47.3 3.2 %collective-permute-start.15 = (bf16[512,512]{1,0:T(8,128)(2,1)S(1)}, bf16[512,512]{1,0:T(8,128)(2,1)S(1)}, u32[]{:S(2)}, u32[]{:S(2)}) collective-permute-start(bf16[512,512]{1,0:T(8,128)(2,1)S(1)} %constant_dynamic-update-slice_fusion.refs_1_), channel_id=1, source_target_pairs={{0,2},{1,9},{2,4},{3,11},{4,6},{5,13},{6,0},{7,15},{8,10},{9,17},{... | collective-permute-start | bytes 1572872 | tf_op jit(solution)/shard_map/ppermute | solution.py:51
  50.5 0.0 collective-permute-done.6.refs_0_
  50.5 1.8 %collective-permute-start.7 = (bf16[512,512]{1,0:T(8,128)(2,1)S(1)}, bf16[512,512]{1,0:T(8,128)(2,1)S(1)}, u32[]{:S(2)}, u32[]{:S(2)}) collective-permute-start(bf16[512,512]{1,0:T(8,128)(2,1)S(1)} %collective-permute-done.6.refs_0_), channel_id=1, source_target_pairs={{0,2},{1,9},{2,4},{3,11},{4,6},{5,13},{6,0},{7,15},{8,10},{9,17},{... | collective-permute-start | bytes 1572872 | tf_op jit(solution)/shard_map/ppermute | solution.py:51
  52.3 0.0 collective-permute-done.10.refs_2_
  52.3 0.0 collective-permute-start.11
  52.3 0.5 collective-permute-done.19.refs_5_.refs_14_.refs_12_
  52.9 3.4 %collective-permute-start.14 = (bf16[128,1024]{1,0:T(8,128)(2,1)S(1)}, bf16[128,1024]{1,0:T(8,128)(2,1)S(1)}, u32[]{:S(2)}, u32[]{:S(2)}) collective-permute-start(bf16[128,1024]{1,0:T(8,128)(2,1)S(1)} %get-tuple-element.50), channel_id=1, source_target_pairs={{0,64},{1,65},{2,66},{3,67},{4,68},{5,69},{6,70},{7,71},{8,72},{9,... | collective-permute-start | bytes 786440 | tf_op jit(solution)/shard_map/ppermute | solution.py:51
  56.3 2.0 %shard_map.56 = (f32[2,128,512]{2,1,0:T(8,128)S(1)}, f32[2,8,512]{2,1,0:T(8,128)S(1)}, f32[2,8,512]{2,1,0:T(8,128)S(1)}) custom-call(s32[4,32]{1,0:T(4,128)} %sequence_ref.7, s32[4,32]{1,0:T(4,128)} %order_ref.11, bf16[512,512]{1,0:T(8,128)(2,1)S(1)} %pad_maximum_fusion.refs_0_, bf16[512,512]{1,0:T(8,128)(2,1)S(1)} %constant_dynamic-update-slice_fusion.refs_1_, ...), custom_call_target="tpu_custom_call" | custom-call | flops 268435456 | bytes 2097152 | tf_op jit(solution)/shard_map/pallas_call | solution.py:391
  58.3 2.0 %collective-permute-done.14.refs_5_.refs_7_ = bf16[128,1024]{1,0:T(8,128)(2,1)S(1)} collective-permute-done((bf16[128,1024]{1,0:T(8,128)(2,1)S(1)}, bf16[128,1024]{1,0:T(8,128)(2,1)S(1)}, u32[]{:S(2)}, u32[]{:S(2)}) %collective-permute-start.14) | collective-permute-done | bytes 262176 | tf_op jit(solution)/shard_map/ppermute | solution.py:51
  60.3 2.8 %shard_map.55 = (f32[2,128,512]{2,1,0:T(8,128)S(1)}, f32[2,8,512]{2,1,0:T(8,128)S(1)}, f32[2,8,512]{2,1,0:T(8,128)S(1)}) custom-call(s32[4,32]{1,0:T(4,128)} %sequence_ref.7, s32[4,32]{1,0:T(4,128)} %order_ref.11, bf16[512,512]{1,0:T(8,128)(2,1)S(1)} %pad_maximum_fusion.refs_0_, bf16[512,512]{1,0:T(8,128)(2,1)S(1)} %constant_dynamic-update-slice_fusion.refs_1_, ...), custom_call_target="tpu_custom_call" | custom-call | flops 268435456 | bytes 2097152 | tf_op jit(solution)/shard_map/pallas_call | solution.py:391
  63.2 0.0 collective-permute-done.16.refs_3_
  63.2 6.6 %shard_map.57 = (f32[2,128,512]{2,1,0:T(8,128)S(1)}, f32[2,8,512]{2,1,0:T(8,128)S(1)}, f32[2,8,512]{2,1,0:T(8,128)S(1)}, f32[2,128,512]{2,1,0:T(8,128)S(1)}, f32...) custom-call(s32[4,32]{1,0:T(4,128)} %sequence_ref.7, s32[4,32]{1,0:T(4,128)} %order_ref.11, ...), custom_call_target="tpu_custom_call" | custom-call | flops 536870912 | bytes 2097152 | tf_op jit(solution)/shard_map/pallas_call | solution.py:391
  69.8 0.0 collective-permute-done.11.refs_1_
  69.8 1.5 %shard_map.58 = (bf16[128,1024]{1,0:T(8,128)(2,1)S(1)}, bf16[128,1024]{1,0:T(8,128)(2,1)S(1)}) custom-call(s32[4,32]{1,0:T(4,128)} %sequence_ref.7, s32[4,32]{1,0:T(4,128)} %order_ref.11, bf16[512,512]{1,0:T(8,128)(2,1)S(1)} %collective-permute-done.7.refs_0_, bf16[512,512]{1,0:T(8,128)(2,1)S(1)} %collective-permute-done.11.refs_1_, ...), custom_call_target="tpu_custom_call" | custom-call | flops 268435456 | bytes 2097152 | tf_op jit(solution)/shard_map/pallas_call | solution.py:391
  71.3 8.0 %collective-permute-start.20 = (bf16[128,1024]{1,0:T(8,128)(2,1)S(1)}, bf16[128,1024]{1,0:T(8,128)(2,1)S(1)}, u32[]{:S(2)}, u32[]{:S(2)}) collective-permute-start(bf16[128,1024]{1,0:T(8,128)(2,1)S(1)} %get-tuple-element.68), channel_id=1, source_target_pairs={{0,1},{1,0},{2,3},{3,2},{4,5},{5,4},{6,7},{7,6},{8,9},{9,8},{10,11... | collective-permute-start | bytes 786440 | tf_op jit(solution)/shard_map/ppermute | solution.py:51
  79.3 1.2 %collective-permute-done.20.received_ref = bf16[128,1024]{1,0:T(8,128)(2,1)S(1)} collective-permute-done((bf16[128,1024]{1,0:T(8,128)(2,1)S(1)}, bf16[128,1024]{1,0:T(8,128)(2,1)S(1)}, u32[]{:S(2)}, u32[]{:S(2)}) %collective-permute-start.20) | collective-permute-done | bytes 262176 | tf_op jit(solution)/shard_map/ppermute | solution.py:51
  80.5 0.8 %join.1 = bf16[128,2048]{1,0:T(8,128)(2,1)} custom-call(s32[1]{0:T(128)} %bitcast.core_ref, bf16[128,1024]{1,0:T(8,128)(2,1)S(1)} %get-tuple-element.67.kept_ref, bf16[128,1024]{1,0:T(8,128)(2,1)S(1)} %collective-permute-done.20.received_ref), custom_call_target="tpu_custom_call" | custom-call | flops 262144 | bytes 1048576 | tf_op jit(solution)/shard_map/join/pallas_call | solution.py:414
  (6 shorter events, 0.1 us)
Async XLA Ops:
  0.0 4.6 %collective-permute-start.1 = (bf16[128,4096]{1,0:T(8,128)(2,1)}, bf16[128,4096]{1,0:T(8,128)(2,1)S(1)}, u32[]{:S(2)}, u32[]{:S(2)}) collective-permute-start(bf16[128,4096]{1,0:T(8,128)(2,1)} %bitcast.3), channel_id=1, source_target_pairs={{0,1},{1,0},{2,3},{3,2},{4,5},{5,4},{6,7},{7,6},{8,9},{9,8},{10,11... | collective-permute-start | bytes 3145736 | tf_op jit(solution)/shard_map/ppermute | solution.py:51
  0.7 4.0 %collective-permute-start = (s32[1,1]{1,0:T(1,128)}, s32[1,1]{1,0:T(1,128)}, u32[]{:S(2)}, u32[]{:S(2)}) collective-permute-start(s32[1,1]{1,0:T(1,128)} %param.7), channel_id=1, source_target_pairs={{0,1},{1,0},{2,3},{3,2},{4,5},{5,4},{6,7},{7,6},{8,9},{9,8},{10,11... | collective-permute-start | bytes 20 | tf_op jit(solution)/shard_map/ppermute | solution.py:51
  7.6 7.4 %collective-permute-start.2 = (bf16[256,512]{1,0:T(8,128)(2,1)S(1)}, bf16[256,512]{1,0:T(8,128)(2,1)S(1)}, u32[]{:S(2)}, u32[]{:S(2)}) collective-permute-start(bf16[256,512]{1,0:T(8,128)(2,1)S(1)} %get-tuple-element.42), channel_id=1, source_target_pairs={{0,32},{1,33},{2,34},{3,35},{4,36},{5,37},{6,38},{7,39},{8,40},{9,... | collective-permute-start | bytes 786440 | tf_op jit(solution)/shard_map/ppermute | solution.py:51
  8.9 7.1 %collective-permute-start.3 = (bf16[256,512]{1,0:T(8,128)(2,1)S(1)}, bf16[256,512]{1,0:T(8,128)(2,1)S(1)}, u32[]{:S(2)}, u32[]{:S(2)}) collective-permute-start(bf16[256,512]{1,0:T(8,128)(2,1)S(1)} %get-tuple-element.43), channel_id=1, source_target_pairs={{0,96},{1,97},{2,98},{3,99},{4,100},{5,101},{6,102},{7,103},{8,104... | collective-permute-start | bytes 786440 | tf_op jit(solution)/shard_map/ppermute | solution.py:51
  9.1 13.1 %collective-permute-start.4 = (bf16[256,512]{1,0:T(8,128)(2,1)S(1)}, bf16[256,512]{1,0:T(8,128)(2,1)S(1)}, u32[]{:S(2)}, u32[]{:S(2)}) collective-permute-start(bf16[256,512]{1,0:T(8,128)(2,1)S(1)} %get-tuple-element.44), channel_id=1, source_target_pairs={{0,64},{1,65},{2,66},{3,67},{4,68},{5,69},{6,70},{7,71},{8,72},{9,... | collective-permute-start | bytes 786440 | tf_op jit(solution)/shard_map/ppermute | solution.py:51
  22.2 11.3 %collective-permute-start.5 = (bf16[256,512]{1,0:T(8,128)(2,1)S(1)}, bf16[256,512]{1,0:T(8,128)(2,1)S(1)}, u32[]{:S(2)}, u32[]{:S(2)}) collective-permute-start(bf16[256,512]{1,0:T(8,128)(2,1)S(1)} %add_add_fusion), channel_id=1, source_target_pairs={{0,8},{1,3},{2,10},{3,5},{4,12},{5,7},{6,14},{7,1},{8,16},{9,11},{... | collective-permute-start | bytes 786440 | tf_op jit(solution)/shard_map/ppermute | solution.py:51
  23.6 11.7 %collective-permute-start.9 = (bf16[256,512]{1,0:T(8,128)(2,1)S(1)}, bf16[256,512]{1,0:T(8,128)(2,1)S(1)}, u32[]{:S(2)}, u32[]{:S(2)}) collective-permute-start(bf16[256,512]{1,0:T(8,128)(2,1)S(1)} %add_add_fusion), channel_id=1, source_target_pairs={{0,16},{1,5},{2,18},{3,7},{4,20},{5,1},{6,22},{7,3},{8,24},{9,13},... | collective-permute-start | bytes 786440 | tf_op jit(solution)/shard_map/ppermute | solution.py:51
  26.2 9.1 %collective-permute-start.8 = (bf16[256,512]{1,0:T(8,128)(2,1)S(1)}, bf16[256,512]{1,0:T(8,128)(2,1)S(1)}, u32[]{:S(2)}, u32[]{:S(2)}) collective-permute-start(bf16[256,512]{1,0:T(8,128)(2,1)S(1)} %add_add_fusion), channel_id=1, source_target_pairs={{0,24},{1,7},{2,26},{3,1},{4,28},{5,3},{6,30},{7,5},{8,0},{9,15},{... | collective-permute-start | bytes 786440 | tf_op jit(solution)/shard_map/ppermute | solution.py:51
  33.5 5.3 %collective-permute-start.12 = (bf16[128,1024]{1,0:T(8,128)(2,1)S(1)}, bf16[128,1024]{1,0:T(8,128)(2,1)S(1)}, u32[]{:S(2)}, u32[]{:S(2)}) collective-permute-start(bf16[128,1024]{1,0:T(8,128)(2,1)S(1)} %get-tuple-element.48), channel_id=1, source_target_pairs={{0,32},{1,33},{2,34},{3,35},{4,36},{5,37},{6,38},{7,39},{8,40},{9,... | collective-permute-start | bytes 786440 | tf_op jit(solution)/shard_map/ppermute | solution.py:51
  33.6 16.9 %collective-permute-start.6 = (bf16[512,512]{1,0:T(8,128)(2,1)S(1)}, bf16[512,512]{1,0:T(8,128)(2,1)S(1)}, u32[]{:S(2)}, u32[]{:S(2)}) collective-permute-start(bf16[512,512]{1,0:T(8,128)(2,1)S(1)} %pad_maximum_fusion.refs_0_), channel_id=1, source_target_pairs={{0,2},{1,9},{2,4},{3,11},{4,6},{5,13},{6,0},{7,15},{8,10},{9,17},{... | collective-permute-start | bytes 1572872 | tf_op jit(solution)/shard_map/ppermute | solution.py:51
  35.4 16.9 %collective-permute-start.10 = (bf16[512,512]{1,0:T(8,128)(2,1)S(1)}, bf16[512,512]{1,0:T(8,128)(2,1)S(1)}, u32[]{:S(2)}, u32[]{:S(2)}) collective-permute-start(bf16[512,512]{1,0:T(8,128)(2,1)S(1)} %constant_dynamic-update-slice_fusion.refs_1_), channel_id=1, source_target_pairs={{0,6},{1,25},{2,0},{3,27},{4,2},{5,29},{6,4},{7,31},{8,14},{9,1},{... | collective-permute-start | bytes 1572872 | tf_op jit(solution)/shard_map/ppermute | solution.py:51
  35.5 5.9 %collective-permute-start.13 = (bf16[128,1024]{1,0:T(8,128)(2,1)S(1)}, bf16[128,1024]{1,0:T(8,128)(2,1)S(1)}, u32[]{:S(2)}, u32[]{:S(2)}) collective-permute-start(bf16[128,1024]{1,0:T(8,128)(2,1)S(1)} %get-tuple-element.49), channel_id=1, source_target_pairs={{0,96},{1,97},{2,98},{3,99},{4,100},{5,101},{6,102},{7,103},{8,104... | collective-permute-start | bytes 786440 | tf_op jit(solution)/shard_map/ppermute | solution.py:51
  37.0 7.9 %collective-permute-start.17 = (bf16[128,1024]{1,0:T(8,128)(2,1)S(1)}, bf16[128,1024]{1,0:T(8,128)(2,1)S(1)}, u32[]{:S(2)}, u32[]{:S(2)}) collective-permute-start(bf16[128,1024]{1,0:T(8,128)(2,1)S(1)} %get-tuple-element.55), channel_id=1, source_target_pairs={{0,32},{1,33},{2,34},{3,35},{4,36},{5,37},{6,38},{7,39},{8,40},{9,... | collective-permute-start | bytes 786440 | tf_op jit(solution)/shard_map/ppermute | solution.py:51
  38.8 8.5 %collective-permute-start.18 = (bf16[128,1024]{1,0:T(8,128)(2,1)S(1)}, bf16[128,1024]{1,0:T(8,128)(2,1)S(1)}, u32[]{:S(2)}, u32[]{:S(2)}) collective-permute-start(bf16[128,1024]{1,0:T(8,128)(2,1)S(1)} %get-tuple-element.56), channel_id=1, source_target_pairs={{0,96},{1,97},{2,98},{3,99},{4,100},{5,101},{6,102},{7,103},{8,104... | collective-permute-start | bytes 786440 | tf_op jit(solution)/shard_map/ppermute | solution.py:51
  41.4 11.5 %collective-permute-start.19 = (bf16[128,1024]{1,0:T(8,128)(2,1)S(1)}, bf16[128,1024]{1,0:T(8,128)(2,1)S(1)}, u32[]{:S(2)}, u32[]{:S(2)}) collective-permute-start(bf16[128,1024]{1,0:T(8,128)(2,1)S(1)} %get-tuple-element.57), channel_id=1, source_target_pairs={{0,64},{1,65},{2,66},{3,67},{4,68},{5,69},{6,70},{7,71},{8,72},{9,... | collective-permute-start | bytes 786440 | tf_op jit(solution)/shard_map/ppermute | solution.py:51
  44.9 18.3 %collective-permute-start.16 = (bf16[512,512]{1,0:T(8,128)(2,1)S(1)}, bf16[512,512]{1,0:T(8,128)(2,1)S(1)}, u32[]{:S(2)}, u32[]{:S(2)}) collective-permute-start(bf16[512,512]{1,0:T(8,128)(2,1)S(1)} %pad_maximum_fusion.refs_0_), channel_id=1, source_target_pairs={{0,6},{1,25},{2,0},{3,27},{4,2},{5,29},{6,4},{7,31},{8,14},{9,1},{... | collective-permute-start | bytes 1572872 | tf_op jit(solution)/shard_map/ppermute | solution.py:51
  47.3 15.9 %collective-permute-start.15 = (bf16[512,512]{1,0:T(8,128)(2,1)S(1)}, bf16[512,512]{1,0:T(8,128)(2,1)S(1)}, u32[]{:S(2)}, u32[]{:S(2)}) collective-permute-start(bf16[512,512]{1,0:T(8,128)(2,1)S(1)} %constant_dynamic-update-slice_fusion.refs_1_), channel_id=1, source_target_pairs={{0,2},{1,9},{2,4},{3,11},{4,6},{5,13},{6,0},{7,15},{8,10},{9,17},{... | collective-permute-start | bytes 1572872 | tf_op jit(solution)/shard_map/ppermute | solution.py:51
  50.5 19.3 %collective-permute-start.7 = (bf16[512,512]{1,0:T(8,128)(2,1)S(1)}, bf16[512,512]{1,0:T(8,128)(2,1)S(1)}, u32[]{:S(2)}, u32[]{:S(2)}) collective-permute-start(bf16[512,512]{1,0:T(8,128)(2,1)S(1)} %collective-permute-done.6.refs_0_), channel_id=1, source_target_pairs={{0,2},{1,9},{2,4},{3,11},{4,6},{5,13},{6,0},{7,15},{8,10},{9,17},{... | collective-permute-start | bytes 1572872 | tf_op jit(solution)/shard_map/ppermute | solution.py:51
  52.3 17.5 %collective-permute-start.11 = (bf16[512,512]{1,0:T(8,128)(2,1)S(1)}, bf16[512,512]{1,0:T(8,128)(2,1)S(1)}, u32[]{:S(2)}, u32[]{:S(2)}) collective-permute-start(bf16[512,512]{1,0:T(8,128)(2,1)S(1)} %collective-permute-done.10.refs_2_), channel_id=1, source_target_pairs={{0,6},{1,25},{2,0},{3,27},{4,2},{5,29},{6,4},{7,31},{8,14},{9,1},{... | collective-permute-start | bytes 1572872 | tf_op jit(solution)/shard_map/ppermute | solution.py:51
  52.9 7.5 %collective-permute-start.14 = (bf16[128,1024]{1,0:T(8,128)(2,1)S(1)}, bf16[128,1024]{1,0:T(8,128)(2,1)S(1)}, u32[]{:S(2)}, u32[]{:S(2)}) collective-permute-start(bf16[128,1024]{1,0:T(8,128)(2,1)S(1)} %get-tuple-element.50), channel_id=1, source_target_pairs={{0,64},{1,65},{2,66},{3,67},{4,68},{5,69},{6,70},{7,71},{8,72},{9,... | collective-permute-start | bytes 786440 | tf_op jit(solution)/shard_map/ppermute | solution.py:51
  71.3 9.2 %collective-permute-start.20 = (bf16[128,1024]{1,0:T(8,128)(2,1)S(1)}, bf16[128,1024]{1,0:T(8,128)(2,1)S(1)}, u32[]{:S(2)}, u32[]{:S(2)}) collective-permute-start(bf16[128,1024]{1,0:T(8,128)(2,1)S(1)} %get-tuple-element.68), channel_id=1, source_target_pairs={{0,1},{1,0},{2,3},{3,2},{4,5},{5,4},{6,7},{7,6},{8,9},{9,8},{10,11... | collective-permute-start | bytes 786440 | tf_op jit(solution)/shard_map/ppermute | solution.py:51

commit v5 on v4

--- a/solution.py
+++ b/solution.py
@@ -52,14 +52,18 @@
 
 
 def rope_tables(order, cos_ref, sin_ref):
-    lane = lax.broadcasted_iota(jnp.int32, (SLAB, HD), 1)
-    half = jnp.where(lane < HD // 2, lane, lane - HD // 2).astype(jnp.float32)
-    frequency = jnp.exp(half * (-2.0 / HD * 13.122363377404328))
-    row = lax.broadcasted_iota(jnp.int32, (SLAB, HD), 0)
-    angle = (order * SLAB + row).astype(jnp.float32) * frequency
-    cos_ref[...] = jnp.cos(angle)
-    sine = jnp.sin(angle)
-    sin_ref[...] = jnp.where(lane < HD // 2, -sine, sine)
+    half_rows = SLAB // 2
+    lane = lax.broadcasted_iota(jnp.int32, (half_rows, HD), 1)
+    row = lax.broadcasted_iota(jnp.int32, (half_rows, HD), 0)
+    left = lane < HD // 2
+    index = jnp.where(left, lane, lane - HD // 2).astype(jnp.float32)
+    frequency = jnp.exp(index * (-2.0 / HD * 13.122363377404328))
+    token = jnp.where(left, row, row + half_rows)
+    angle = (order * SLAB + token).astype(jnp.float32) * frequency
+    for value, ref, sign in ((jnp.cos(angle), cos_ref, 1.0), (jnp.sin(angle), sin_ref, -1.0)):
+        turned = pltpu.roll(value, HD // 2, 1)
+        ref[:half_rows] = jnp.where(left, sign * value, turned)
+        ref[half_rows:] = jnp.where(left, sign * turned, value)
 
 
 def rope(block, table):
@@ -69,8 +73,9 @@
 CHUNKS = 4
 
 
-def prepare_kernel(core_ref, owner_ref, order_ref, x_ref, w_ref, *refs):
-    x_out, w_out, cos_ref, sin_ref, sems = refs
+def prepare_kernel(core_ref, other_ref, owner_ref, order_ref, x_ref, w_ref, *refs):
+    x_out, w_out = refs[:2]
+    sems = refs[6]
     core = core_ref[0]
     width = 2 * HD
     rows = w_out.shape[0] // CHUNKS
@@ -88,31 +93,32 @@
             )
     for copy in copies:
         copy.start()
-    rope_tables(order_ref[owner_ref[0, 0], lax.axis_index("cp")], cos_ref, sin_ref)
+    column = lax.axis_index("cp")
+    rope_tables(order_ref[other_ref[0, 0], column + 1 - 2 * core], *refs[2:4])
+    rope_tables(order_ref[owner_ref[0, 0], column], *refs[4:6])
     for copy in copies:
         copy.wait()
 
 
-def prepare(core, owner, slab_order, rows, weight):
+def prepare(core, owners, slab_order, rows, weight):
     smem = pl.BlockSpec(memory_space=pltpu.SMEM)
     anywhere = pl.BlockSpec(memory_space=pl.ANY)
     vmem = pl.BlockSpec(memory_space=pltpu.VMEM)
     depth = rows.shape[1]
     return pl.pallas_call(
         prepare_kernel,
-        in_specs=[smem] * 3 + [anywhere] * 2,
-        out_specs=[vmem] * 4,
+        in_specs=[smem] * 4 + [anywhere] * 2,
+        out_specs=[vmem] * 6,
         out_shape=[
             pltpu.VMEM(rows.shape, rows.dtype),
             pltpu.VMEM((depth, 4 * HD), weight.dtype),
-            pltpu.VMEM((SLAB, HD), jnp.float32),
-            pltpu.VMEM((SLAB, HD), jnp.float32),
-        ],
+        ]
+        + [pltpu.VMEM((SLAB, HD), jnp.float32)] * 4,
         scratch_shapes=[pltpu.SemaphoreType.DMA((2 * CHUNKS + 1,))],
         compiler_params=pltpu.CompilerParams(vmem_limit_bytes=8 << 20),
         cost_estimate=pl.CostEstimate(flops=1 << 26, bytes_accessed=5 << 20, transcendentals=1 << 16),
         name="prepare",
-    )(core, owner, in_hbm(slab_order), in_hbm(rows), in_hbm(weight))
+    )(core, *owners, in_hbm(slab_order), in_hbm(rows), in_hbm(weight))
 
 
 def store_masked(outs, owner, rows, first, value):
@@ -123,10 +129,8 @@
         out[rows, columns] = jnp.where(mine, value, jnp.zeros_like(value))
 
 
-def kv_kernel(core_ref, other_ref, owner_ref, order_ref, y_ref, x_ref, w_ref, *refs):
-    ropes, outs = (refs[2:4], refs[:2]), refs[4:]
-    column = lax.axis_index("cp") + 1 - 2 * core_ref[0]
-    rope_tables(order_ref[other_ref[0, 0], column], *ropes[0])
+def kv_kernel(other_ref, owner_ref, y_ref, x_ref, w_ref, *refs):
+    ropes, outs = (refs[:2], refs[2:4]), refs[4:]
     owners = (other_ref[0, 0], owner_ref[0, 0])
     both = jnp.concatenate([y_ref[...], x_ref[...]], axis=0)
     wide = 512
@@ -187,22 +191,21 @@
     return pltpu.with_memory_space_constraint(value, pltpu.HBM)
 
 
-def project_kv(core, owners, slab_order, others, rows, weight, tables):
+def project_kv(owners, others, rows, weight, tables):
     smem = pl.BlockSpec(memory_space=pltpu.SMEM)
     vmem = pl.BlockSpec(memory_space=pltpu.VMEM)
     operands = [in_vmem(v) for v in (others, rows, weight, *tables)]
     return pl.pallas_call(
         kv_kernel,
-        in_specs=[smem] * 4 + [vmem] * len(operands),
-        out_specs=[vmem] * 6,
-        out_shape=[pltpu.VMEM((SLAB, HD), jnp.float32)] * 2
-        + [pltpu.VMEM((2 * SLAB, 4 * HD), jnp.bfloat16)] * 4,
+        in_specs=[smem] * 2 + [vmem] * len(operands),
+        out_specs=[vmem] * 4,
+        out_shape=[pltpu.VMEM((2 * SLAB, 4 * HD), jnp.bfloat16)] * 4,
         compiler_params=pltpu.CompilerParams(vmem_limit_bytes=24 << 20),
         cost_estimate=pl.CostEstimate(
             flops=4 * SLAB * rows.shape[1] * 4 * HD, bytes_accessed=4 << 20, transcendentals=0
         ),
         name="kv_proj",
-    )(core, *owners, in_hbm(slab_order), *operands)
+    )(*owners, *operands)
 
 
 QPARTS = 2
@@ -267,12 +270,16 @@
     return count
 
 
-def attend_slab(t, spots, pieces, parts, old, new, out, sequence_ref, order_ref, q_ref, kv, scores_ref):
-    acc, peak, total = new
+def attend_slab(t, spots, pieces, parts, old, new, out, sequence_ref, order_ref, kv, scores_ref):
+    acc, peak, total = new[:3]
     first = old is None
+    if first:
+        q_ref = new[3]
+        q_ref[...] = parts[0][...] + parts[1][...] + parts[2][...] + parts[3][...]
+    else:
+        (q_ref,) = parts
     count = collect(t, spots, pieces, sequence_ref, order_ref, kv)
     pairs_here = (count + 1) // 2
-    q_ref[...] = parts[0][...] + parts[1][...] + parts[2][...] + parts[3][...]
     starts = []
     for g in range(2):
         if first:
@@ -350,22 +357,22 @@
     pieces, refs = refs[: len(spots)], refs[len(spots) :]
     given = []
     for t, start, first in jobs:
-        parts, refs = refs[:4], refs[4:]
+        parts, refs = (refs[:4], refs[4:]) if first else (refs[:1], refs[1:])
         old = None
         if not first:
             old, refs = refs[:3], refs[3:]
         given.append((parts, old))
-    per = 1 if last else 3
+    per = 1 if last else 4 if jobs[0][2] else 3
     outs, refs = refs[: per * len(jobs)], refs[per * len(jobs) :]
     state, refs = (refs[:3], refs[3:]) if last else (None, refs)
-    q_ref, kv, scores_ref = refs
+    kv, scores_ref = refs
     for n, (t, start, first) in enumerate(jobs):
         parts, old = given[n]
-        new = state if last else outs[3 * n : 3 * n + 3]
+        new = state if last else outs[per * n : per * n + per]
         out = outs[n] if last else None
         attend_slab(
             t, spots[start:], pieces[start:], parts, old, new, out,
-            sequence_ref, order_ref, q_ref, kv, scores_ref,
+            sequence_ref, order_ref, kv, scores_ref,
         )
 
 
@@ -373,7 +380,6 @@
     vmem = pl.BlockSpec(memory_space=pltpu.VMEM)
     smem = pl.BlockSpec(memory_space=pltpu.SMEM)
     scratch = [
-        pltpu.VMEM((SLAB, HALF), jnp.bfloat16),
         pltpu.VMEM((16, SLAB, 4 * HD), jnp.bfloat16),
         pltpu.VMEM((9, 2, 2 * SLAB, WIDE), jnp.float32),
     ]
@@ -387,7 +393,10 @@
         out_shape = [pltpu.VMEM((SLAB, HALF), jnp.bfloat16)] * len(jobs)
         scratch = [pltpu.VMEM(s, jnp.float32) for s in STATE] + scratch
     else:
-        out_shape = [pltpu.VMEM(s, jnp.float32) for s in STATE] * len(jobs)
+        out_shape = [pltpu.VMEM(s, jnp.float32) for s in STATE]
+        if jobs[0][2]:
+            out_shape.append(pltpu.VMEM((SLAB, HALF), jnp.bfloat16))
+        out_shape = out_shape * len(jobs)
     return pl.pallas_call(
         functools.partial(attend_kernel, jobs, spots, last),
         in_specs=[smem, smem] + [vmem] * len(operands),
@@ -428,16 +437,15 @@
     others = permute(rows, OTHER_CORE)
     owners = (permute(owner_slot, OTHER_CORE), owner_slot)
     core = core.reshape(1)
-    rows, kv_weight, *tables = prepare(core, owner_slot, slab_order, rows, qkv_weight)
-    other_cos, other_sin, *kv = project_kv(
-        core, owners, slab_order, others, rows, kv_weight, tables
-    )
-    tables = (other_cos, other_sin, *tables)
+    rows, kv_weight, *tables = prepare(core, owners, slab_order, rows, qkv_weight)
+    kv = project_kv(owners, others, rows, kv_weight, tables)
     queries = project_q(core, owners, others, rows, qkv_weight, tables)
     moved = [permute(kv[k], shift_x(k)) for k in (1, 3, 2)]
     parts = [[queries[0]] + [permute(queries[k], shift_x(k)) for k in (1, 3, 2)]]
     own = kv[0] + moved[0] + moved[1] + moved[2]
-    first = [permute(own, shift_first(k)) for k in (1, 3, 2)]
+    first = []
+    for k in (1, 3, 2):
+        first.append(permute(own, shift_first(k)))
     parts.append([queries[4]] + [permute(queries[4 + k], shift_x(k)) for k in (1, 3, 2)])
     low = jnp.concatenate([own, first[0]], axis=0)
     high = jnp.concatenate([first[1], first[2]], axis=0)
@@ -450,7 +458,8 @@
     tables = (slab_sequence, slab_order)
     state = [None, None]
     for t in (0, 1):
-        state[t] = attend([(t, 0, True)], *tables, local_items, parts, state, False)
+        *state[t], query = attend([(t, 0, True)], *tables, local_items, parts, state, False)
+        parts[t] = [query]
     both = attend([(0, 0, False), (1, 0, False)], *tables, near_items, parts, state, False)
     state = [both[:3], both[3:]]
     sent, kept = attend([(0, 0, False), (1, 0, False)], *tables, far_items, parts, state, True)

time: 81.6 us -> 83.9 us (1.028)
  the two profiles are of different devices: /device:TPU:35 before, /device:TPU:99 now
where the time goes in v5:
time: 83.9 us; the launch traced here: 83.6 us
  waiting for transfers between devices  29.3 us (35%)
  starting transfers between devices  26.8 us (32%)
  Pallas kernels  26.5 us (32%)
  between operations  0.84 us (1%)
    ppermute x21, waiting for transfers between devices, permute(): return lax.ppermute(value, AXES, table)  29.3 us
    ppermute x21, starting transfers between devices, permute(): return lax.ppermute(value, AXES, table)  26.8 us
    pallas_call x4, Pallas kernels, attend(): pl.pallas_call(functools.partial(attend_kernel, jobs, spots, last), in_sp...  13.3 us
    pallas_call x1, Pallas kernels, project_q(): pl.pallas_call(q_kernel, in_specs=[smem] * 3 + [pl.BlockSpec(memory_space...  6.19 us
    pallas_call x1, Pallas kernels, prepare(): pl.pallas_call(prepare_kernel, in_specs=[smem] * 4 + [anywhere] * 2, out_...  4.04 us
    pallas_call x1, Pallas kernels, project_kv(): pl.pallas_call(kv_kernel, in_specs=[smem] * 2 + [vmem] * len(operands), o...  2.16 us
  transfers between devices with their start and end apart: 21, of which 9 were waited for; matrix products, arithmetic and copies ran while one was open for 0% of the time, Pallas kernels for 23%

profile of v5, /device:TPU:99, one launch (start us, length us, event | category | flops | bytes accessed | tf_op | source)
XLA Modules:
  0.0 83.6 jit_solution(2211627269372069658)
XLA Ops:
  0.0 0.7 collective-permute-start.1
  0.7 0.0 collective-permute-start
  1.3 1.8 %collective-permute-done.other_ref = s32[1,1]{1,0:T(1,128)} collective-permute-done((s32[1,1]{1,0:T(1,128)}, s32[1,1]{1,0:T(1,128)}, u32[]{:S(2)}, u32[]{:S(2)}) %collective-permute-start) | collective-permute-done | bytes 36 | tf_op jit(solution)/shard_map/ppermute | solution.py:51
  3.2 4.0 %prepare.1 = (bf16[128,4096]{1,0:T(8,128)(2,1)S(1)}, bf16[4096,512]{1,0:T(8,128)(2,1)S(1)}, f32[128,128]{1,0:T(8,128)S(1)}, f32[128,128]{1,0:T(8,128)S(1)}, f32[...) custom-call(s32[1]{0:T(128)} %bitcast.core_ref, s32[1,1]{1,0:T(1,128)} %collective-permute-done.other_ref, ...), custom_call_target="tpu_custom_call" | custom-call | flops 67108864 | bytes 5242880 | tf_op jit(solution)/shard_map/prepare/pallas_call | solution.py:108
  7.2 0.0 collective-permute-done.1.y_ref
  7.2 2.2 %kv_proj.1 = (bf16[256,512]{1,0:T(8,128)(2,1)S(1)}, bf16[256,512]{1,0:T(8,128)(2,1)S(1)}, bf16[256,512]{1,0:T(8,128)(2,1)S(1)}, bf16[256,512]{1,0:T(8,128)(2,1)S(1)}) custom-call(s32[1,1]{1,0:T(1,128)} %collective-permute-done.other_ref, s32[1,1]{1,0:T(1,128)S(6)} %copy.7.owner_ref, bf16[128,4096]{1,0:T(8,128)(2,1)S(1)} %collective-permute-done.1.y_ref, ...), custom_call_target="tpu_custom_call" | custom-call | flops 1073741824 | bytes 4194304 | tf_op jit(solution)/shard_map/kv_proj/pallas_call | solution.py:198
  9.4 1.3 %collective-permute-start.2 = (bf16[256,512]{1,0:T(8,128)(2,1)S(1)}, bf16[256,512]{1,0:T(8,128)(2,1)S(1)}, u32[]{:S(2)}, u32[]{:S(2)}) collective-permute-start(bf16[256,512]{1,0:T(8,128)(2,1)S(1)} %get-tuple-element.46), channel_id=1, source_target_pairs={{0,32},{1,33},{2,34},{3,35},{4,36},{5,37},{6,38},{7,39},{8,40},{9,... | collective-permute-start | bytes 786440 | tf_op jit(solution)/shard_map/ppermute | solution.py:51
  10.7 0.3 collective-permute-start.3
  10.9 1.8 %collective-permute-start.4 = (bf16[256,512]{1,0:T(8,128)(2,1)S(1)}, bf16[256,512]{1,0:T(8,128)(2,1)S(1)}, u32[]{:S(2)}, u32[]{:S(2)}) collective-permute-start(bf16[256,512]{1,0:T(8,128)(2,1)S(1)} %get-tuple-element.48), channel_id=1, source_target_pairs={{0,64},{1,65},{2,66},{3,67},{4,68},{5,69},{6,70},{7,71},{8,72},{9,... | collective-permute-start | bytes 786440 | tf_op jit(solution)/shard_map/ppermute | solution.py:51
  12.8 4.2 %collective-permute-done.2 = bf16[256,512]{1,0:T(8,128)(2,1)S(1)} collective-permute-done((bf16[256,512]{1,0:T(8,128)(2,1)S(1)}, bf16[256,512]{1,0:T(8,128)(2,1)S(1)}, u32[]{:S(2)}, u32[]{:S(2)}) %collective-permute-start.2) | collective-permute-done | bytes 262176 | tf_op jit(solution)/shard_map/ppermute | solution.py:51
  17.0 0.9 %collective-permute-done.3 = bf16[256,512]{1,0:T(8,128)(2,1)S(1)} collective-permute-done((bf16[256,512]{1,0:T(8,128)(2,1)S(1)}, bf16[256,512]{1,0:T(8,128)(2,1)S(1)}, u32[]{:S(2)}, u32[]{:S(2)}) %collective-permute-start.3) | collective-permute-done | bytes 262176 | tf_op jit(solution)/shard_map/ppermute | solution.py:51
  17.9 6.3 %collective-permute-done.4 = bf16[256,512]{1,0:T(8,128)(2,1)S(1)} collective-permute-done((bf16[256,512]{1,0:T(8,128)(2,1)S(1)}, bf16[256,512]{1,0:T(8,128)(2,1)S(1)}, u32[]{:S(2)}, u32[]{:S(2)}) %collective-permute-start.4) | collective-permute-done | bytes 262176 | tf_op jit(solution)/shard_map/ppermute | solution.py:51
  24.1 0.1 add_add_fusion
  24.2 1.4 %collective-permute-start.5 = (bf16[256,512]{1,0:T(8,128)(2,1)S(1)}, bf16[256,512]{1,0:T(8,128)(2,1)S(1)}, u32[]{:S(2)}, u32[]{:S(2)}) collective-permute-start(bf16[256,512]{1,0:T(8,128)(2,1)S(1)} %add_add_fusion), channel_id=1, source_target_pairs={{0,8},{1,3},{2,10},{3,5},{4,12},{5,7},{6,14},{7,1},{8,16},{9,11},{... | collective-permute-start | bytes 786440 | tf_op jit(solution)/shard_map/ppermute | solution.py:51
  25.6 2.6 %collective-permute-start.9 = (bf16[256,512]{1,0:T(8,128)(2,1)S(1)}, bf16[256,512]{1,0:T(8,128)(2,1)S(1)}, u32[]{:S(2)}, u32[]{:S(2)}) collective-permute-start(bf16[256,512]{1,0:T(8,128)(2,1)S(1)} %add_add_fusion), channel_id=1, source_target_pairs={{0,16},{1,5},{2,18},{3,7},{4,20},{5,1},{6,22},{7,3},{8,24},{9,13},... | collective-permute-start | bytes 786440 | tf_op jit(solution)/shard_map/ppermute | solution.py:51
  28.2 1.1 %collective-permute-start.8 = (bf16[256,512]{1,0:T(8,128)(2,1)S(1)}, bf16[256,512]{1,0:T(8,128)(2,1)S(1)}, u32[]{:S(2)}, u32[]{:S(2)}) collective-permute-start(bf16[256,512]{1,0:T(8,128)(2,1)S(1)} %add_add_fusion), channel_id=1, source_target_pairs={{0,24},{1,7},{2,26},{3,1},{4,28},{5,3},{6,30},{7,5},{8,0},{9,15},{... | collective-permute-start | bytes 786440 | tf_op jit(solution)/shard_map/ppermute | solution.py:51
  29.2 6.2 %q_proj.1 = (bf16[128,1024]{1,0:T(8,128)(2,1)S(1)}, bf16[128,1024]{1,0:T(8,128)(2,1)S(1)}, bf16[128,1024]{1,0:T(8,128)(2,1)S(1)}, bf16[128,1024]{1,0:T(8,128)(2,...) custom-call(s32[1]{0:T(128)} %bitcast.core_ref, ...), custom_call_target="tpu_custom_call" | custom-call | flops 2147483648 | bytes 8388608 | tf_op jit(solution)/shard_map/q_proj/pallas_call | solution.py:219
  35.5 0.1 collective-permute-start.12
  35.5 0.0 collective-permute-done.5
  35.6 0.1 collective-permute-start.6
  35.7 0.0 collective-permute-done.8
  35.7 0.0 collective-permute-done.9
  35.7 1.5 %collective-permute-start.10 = (bf16[512,512]{1,0:T(8,128)(2,1)S(1)}, bf16[512,512]{1,0:T(8,128)(2,1)S(1)}, u32[]{:S(2)}, u32[]{:S(2)}) collective-permute-start(bf16[512,512]{1,0:T(8,128)(2,1)S(1)} %constant_dynamic-update-slice_fusion.refs_1_), channel_id=1, source_target_pairs={{0,6},{1,25},{2,0},{3,27},{4,2},{5,29},{6,4},{7,31},{8,14},{9,1},{... | collective-permute-start | bytes 1572872 | tf_op jit(solution)/shard_map/ppermute | solution.py:51
  37.3 1.4 %collective-permute-start.13 = (bf16[128,1024]{1,0:T(8,128)(2,1)S(1)}, bf16[128,1024]{1,0:T(8,128)(2,1)S(1)}, u32[]{:S(2)}, u32[]{:S(2)}) collective-permute-start(bf16[128,1024]{1,0:T(8,128)(2,1)S(1)} %get-tuple-element.51), channel_id=1, source_target_pairs={{0,96},{1,97},{2,98},{3,99},{4,100},{5,101},{6,102},{7,103},{8,104... | collective-permute-start | bytes 786440 | tf_op jit(solution)/shard_map/ppermute | solution.py:51
  38.7 1.2 %collective-permute-start.14 = (bf16[128,1024]{1,0:T(8,128)(2,1)S(1)}, bf16[128,1024]{1,0:T(8,128)(2,1)S(1)}, u32[]{:S(2)}, u32[]{:S(2)}) collective-permute-start(bf16[128,1024]{1,0:T(8,128)(2,1)S(1)} %get-tuple-element.52), channel_id=1, source_target_pairs={{0,64},{1,65},{2,66},{3,67},{4,68},{5,69},{6,70},{7,71},{8,72},{9,... | collective-permute-start | bytes 786440 | tf_op jit(solution)/shard_map/ppermute | solution.py:51
  39.9 3.5 %collective-permute-done.12.refs_3_ = bf16[128,1024]{1,0:T(8,128)(2,1)S(1)} collective-permute-done((bf16[128,1024]{1,0:T(8,128)(2,1)S(1)}, bf16[128,1024]{1,0:T(8,128)(2,1)S(1)}, u32[]{:S(2)}, u32[]{:S(2)}) %collective-permute-start.12) | collective-permute-done | bytes 262176 | tf_op jit(solution)/shard_map/ppermute | solution.py:51
  43.4 0.0 collective-permute-start.17
  43.4 0.0 collective-permute-done.13.refs_4_
  43.4 2.6 %collective-permute-start.18 = (bf16[128,1024]{1,0:T(8,128)(2,1)S(1)}, bf16[128,1024]{1,0:T(8,128)(2,1)S(1)}, u32[]{:S(2)}, u32[]{:S(2)}) collective-permute-start(bf16[128,1024]{1,0:T(8,128)(2,1)S(1)} %get-tuple-element.59), channel_id=1, source_target_pairs={{0,96},{1,97},{2,98},{3,99},{4,100},{5,101},{6,102},{7,103},{8,104... | collective-permute-start | bytes 786440 | tf_op jit(solution)/shard_map/ppermute | solution.py:51
  46.1 4.5 %collective-permute-done.14.refs_5_ = bf16[128,1024]{1,0:T(8,128)(2,1)S(1)} collective-permute-done((bf16[128,1024]{1,0:T(8,128)(2,1)S(1)}, bf16[128,1024]{1,0:T(8,128)(2,1)S(1)}, u32[]{:S(2)}, u32[]{:S(2)}) %collective-permute-start.14) | collective-permute-done | bytes 262176 | tf_op jit(solution)/shard_map/ppermute | solution.py:51
  50.6 0.0 collective-permute-start.16
  50.6 3.0 %collective-permute-done.17.refs_3_ = bf16[128,1024]{1,0:T(8,128)(2,1)S(1)} collective-permute-done((bf16[128,1024]{1,0:T(8,128)(2,1)S(1)}, bf16[128,1024]{1,0:T(8,128)(2,1)S(1)}, u32[]{:S(2)}, u32[]{:S(2)}) %collective-permute-start.17) | collective-permute-done | bytes 262176 | tf_op jit(solution)/shard_map/ppermute | solution.py:51
  53.6 0.0 collective-permute-start.15
  53.6 0.0 collective-permute-start.7
  53.6 0.0 collective-permute-done.10.refs_2_
  53.6 2.9 %collective-permute-start.11 = (bf16[512,512]{1,0:T(8,128)(2,1)S(1)}, bf16[512,512]{1,0:T(8,128)(2,1)S(1)}, u32[]{:S(2)}, u32[]{:S(2)}) collective-permute-start(bf16[512,512]{1,0:T(8,128)(2,1)S(1)} %collective-permute-done.10.refs_2_), channel_id=1, source_target_pairs={{0,6},{1,25},{2,0},{3,27},{4,2},{5,29},{6,4},{7,31},{8,14},{9,1},{... | collective-permute-start | bytes 1572872 | tf_op jit(solution)/shard_map/ppermute | solution.py:51
  56.5 1.1 %collective-permute-start.19 = (bf16[128,1024]{1,0:T(8,128)(2,1)S(1)}, bf16[128,1024]{1,0:T(8,128)(2,1)S(1)}, u32[]{:S(2)}, u32[]{:S(2)}) collective-permute-start(bf16[128,1024]{1,0:T(8,128)(2,1)S(1)} %get-tuple-element.60), channel_id=1, source_target_pairs={{0,64},{1,65},{2,66},{3,67},{4,68},{5,69},{6,70},{7,71},{8,72},{9,... | collective-permute-start | bytes 786440 | tf_op jit(solution)/shard_map/ppermute | solution.py:51
  57.6 2.0 %shard_map.55 = (f32[2,128,512]{2,1,0:T(8,128)S(1)}, f32[2,8,512]{2,1,0:T(8,128)S(1)}, f32[2,8,512]{2,1,0:T(8,128)S(1)}, bf16[128,1024]{1,0:T(8,128)(2,1)S(1)}) custom-call(s32[4,32]{1,0:T(4,128)} %sequence_ref.7, s32[4,32]{1,0:T(4,128)} %order_ref.9, bf16[512,512]{1,0:T(8,128)(2,1)S(1)} %pad_maximum_fusion.refs_0_, ...), custom_call_target="tpu_custom_call" | custom-call | flops 268435456 | bytes 2097152 | tf_op jit(solution)/shard_map/pallas_call | solution.py:400
  59.6 3.9 %collective-permute-done.19.refs_5_ = bf16[128,1024]{1,0:T(8,128)(2,1)S(1)} collective-permute-done((bf16[128,1024]{1,0:T(8,128)(2,1)S(1)}, bf16[128,1024]{1,0:T(8,128)(2,1)S(1)}, u32[]{:S(2)}, u32[]{:S(2)}) %collective-permute-start.19) | collective-permute-done | bytes 262176 | tf_op jit(solution)/shard_map/ppermute | solution.py:51
  63.5 2.2 %shard_map.56 = (f32[2,128,512]{2,1,0:T(8,128)S(1)}, f32[2,8,512]{2,1,0:T(8,128)S(1)}, f32[2,8,512]{2,1,0:T(8,128)S(1)}, bf16[128,1024]{1,0:T(8,128)(2,1)S(1)}) custom-call(s32[4,32]{1,0:T(4,128)} %sequence_ref.7, s32[4,32]{1,0:T(4,128)} %order_ref.9, bf16[512,512]{1,0:T(8,128)(2,1)S(1)} %pad_maximum_fusion.refs_0_, ...), custom_call_target="tpu_custom_call" | custom-call | flops 268435456 | bytes 2097152 | tf_op jit(solution)/shard_map/pallas_call | solution.py:400
  65.7 0.0 collective-permute-done.16.refs_3_
  65.7 0.0 collective-permute-done.15.refs_1_
  65.7 5.2 %shard_map.57 = (f32[2,128,512]{2,1,0:T(8,128)S(1)}, f32[2,8,512]{2,1,0:T(8,128)S(1)}, f32[2,8,512]{2,1,0:T(8,128)S(1)}, f32[2,128,512]{2,1,0:T(8,128)S(1)}, f32...) custom-call(s32[4,32]{1,0:T(4,128)} %sequence_ref.7, s32[4,32]{1,0:T(4,128)} %order_ref.9, ...), custom_call_target="tpu_custom_call" | custom-call | flops 536870912 | bytes 2097152 | tf_op jit(solution)/shard_map/pallas_call | solution.py:400
  70.9 0.0 collective-permute-done.7.refs_0_
  70.9 3.9 %shard_map.58 = (bf16[128,1024]{1,0:T(8,128)(2,1)S(1)}, bf16[128,1024]{1,0:T(8,128)(2,1)S(1)}) custom-call(s32[4,32]{1,0:T(4,128)} %sequence_ref.7, s32[4,32]{1,0:T(4,128)} %order_ref.9, bf16[512,512]{1,0:T(8,128)(2,1)S(1)} %collective-permute-done.7.refs_0_, bf16[512,512]{1,0:T(8,128)(2,1)S(1)} %collective-permute-done.11.refs_1_, ...), custom_call_target="tpu_custom_call" | custom-call | flops 268435456 | bytes 2097152 | tf_op jit(solution)/shard_map/pallas_call | solution.py:400
  74.8 6.7 %collective-permute-start.20 = (bf16[128,1024]{1,0:T(8,128)(2,1)S(1)}, bf16[128,1024]{1,0:T(8,128)(2,1)S(1)}, u32[]{:S(2)}, u32[]{:S(2)}) collective-permute-start(bf16[128,1024]{1,0:T(8,128)(2,1)S(1)} %get-tuple-element.72), channel_id=1, source_target_pairs={{0,1},{1,0},{2,3},{3,2},{4,5},{5,4},{6,7},{7,6},{8,9},{9,8},{10,11... | collective-permute-start | bytes 786440 | tf_op jit(solution)/shard_map/ppermute | solution.py:51
  81.6 1.2 %collective-permute-done.20.received_ref = bf16[128,1024]{1,0:T(8,128)(2,1)S(1)} collective-permute-done((bf16[128,1024]{1,0:T(8,128)(2,1)S(1)}, bf16[128,1024]{1,0:T(8,128)(2,1)S(1)}, u32[]{:S(2)}, u32[]{:S(2)}) %collective-permute-start.20) | collective-permute-done | bytes 262176 | tf_op jit(solution)/shard_map/ppermute | solution.py:51
  82.7 0.8 join.1
  (6 shorter events, 0.1 us)
Async XLA Ops:
  0.0 7.2 %collective-permute-start.1 = (bf16[128,4096]{1,0:T(8,128)(2,1)}, bf16[128,4096]{1,0:T(8,128)(2,1)S(1)}, u32[]{:S(2)}, u32[]{:S(2)}) collective-permute-start(bf16[128,4096]{1,0:T(8,128)(2,1)} %bitcast.3), channel_id=1, source_target_pairs={{0,1},{1,0},{2,3},{3,2},{4,5},{5,4},{6,7},{7,6},{8,9},{9,8},{10,11... | collective-permute-start | bytes 3145736 | tf_op jit(solution)/shard_map/ppermute | solution.py:51
  0.7 2.5 %collective-permute-start = (s32[1,1]{1,0:T(1,128)}, s32[1,1]{1,0:T(1,128)}, u32[]{:S(2)}, u32[]{:S(2)}) collective-permute-start(s32[1,1]{1,0:T(1,128)} %param.7), channel_id=1, source_target_pairs={{0,1},{1,0},{2,3},{3,2},{4,5},{5,4},{6,7},{7,6},{8,9},{9,8},{10,11... | collective-permute-start | bytes 20 | tf_op jit(solution)/shard_map/ppermute | solution.py:51
  9.4 7.6 %collective-permute-start.2 = (bf16[256,512]{1,0:T(8,128)(2,1)S(1)}, bf16[256,512]{1,0:T(8,128)(2,1)S(1)}, u32[]{:S(2)}, u32[]{:S(2)}) collective-permute-start(bf16[256,512]{1,0:T(8,128)(2,1)S(1)} %get-tuple-element.46), channel_id=1, source_target_pairs={{0,32},{1,33},{2,34},{3,35},{4,36},{5,37},{6,38},{7,39},{8,40},{9,... | collective-permute-start | bytes 786440 | tf_op jit(solution)/shard_map/ppermute | solution.py:51
  10.7 7.2 %collective-permute-start.3 = (bf16[256,512]{1,0:T(8,128)(2,1)S(1)}, bf16[256,512]{1,0:T(8,128)(2,1)S(1)}, u32[]{:S(2)}, u32[]{:S(2)}) collective-permute-start(bf16[256,512]{1,0:T(8,128)(2,1)S(1)} %get-tuple-element.47), channel_id=1, source_target_pairs={{0,96},{1,97},{2,98},{3,99},{4,100},{5,101},{6,102},{7,103},{8,104... | collective-permute-start | bytes 786440 | tf_op jit(solution)/shard_map/ppermute | solution.py:51
  10.9 13.2 %collective-permute-start.4 = (bf16[256,512]{1,0:T(8,128)(2,1)S(1)}, bf16[256,512]{1,0:T(8,128)(2,1)S(1)}, u32[]{:S(2)}, u32[]{:S(2)}) collective-permute-start(bf16[256,512]{1,0:T(8,128)(2,1)S(1)} %get-tuple-element.48), channel_id=1, source_target_pairs={{0,64},{1,65},{2,66},{3,67},{4,68},{5,69},{6,70},{7,71},{8,72},{9,... | collective-permute-start | bytes 786440 | tf_op jit(solution)/shard_map/ppermute | solution.py:51
  24.2 11.3 %collective-permute-start.5 = (bf16[256,512]{1,0:T(8,128)(2,1)S(1)}, bf16[256,512]{1,0:T(8,128)(2,1)S(1)}, u32[]{:S(2)}, u32[]{:S(2)}) collective-permute-start(bf16[256,512]{1,0:T(8,128)(2,1)S(1)} %add_add_fusion), channel_id=1, source_target_pairs={{0,8},{1,3},{2,10},{3,5},{4,12},{5,7},{6,14},{7,1},{8,16},{9,11},{... | collective-permute-start | bytes 786440 | tf_op jit(solution)/shard_map/ppermute | solution.py:51
  25.6 10.1 %collective-permute-start.9 = (bf16[256,512]{1,0:T(8,128)(2,1)S(1)}, bf16[256,512]{1,0:T(8,128)(2,1)S(1)}, u32[]{:S(2)}, u32[]{:S(2)}) collective-permute-start(bf16[256,512]{1,0:T(8,128)(2,1)S(1)} %add_add_fusion), channel_id=1, source_target_pairs={{0,16},{1,5},{2,18},{3,7},{4,20},{5,1},{6,22},{7,3},{8,24},{9,13},... | collective-permute-start | bytes 786440 | tf_op jit(solution)/shard_map/ppermute | solution.py:51
  28.2 7.5 %collective-permute-start.8 = (bf16[256,512]{1,0:T(8,128)(2,1)S(1)}, bf16[256,512]{1,0:T(8,128)(2,1)S(1)}, u32[]{:S(2)}, u32[]{:S(2)}) collective-permute-start(bf16[256,512]{1,0:T(8,128)(2,1)S(1)} %add_add_fusion), channel_id=1, source_target_pairs={{0,24},{1,7},{2,26},{3,1},{4,28},{5,3},{6,30},{7,5},{8,0},{9,15},{... | collective-permute-start | bytes 786440 | tf_op jit(solution)/shard_map/ppermute | solution.py:51
  35.5 8.0 %collective-permute-start.12 = (bf16[128,1024]{1,0:T(8,128)(2,1)S(1)}, bf16[128,1024]{1,0:T(8,128)(2,1)S(1)}, u32[]{:S(2)}, u32[]{:S(2)}) collective-permute-start(bf16[128,1024]{1,0:T(8,128)(2,1)S(1)} %get-tuple-element.50), channel_id=1, source_target_pairs={{0,32},{1,33},{2,34},{3,35},{4,36},{5,37},{6,38},{7,39},{8,40},{9,... | collective-permute-start | bytes 786440 | tf_op jit(solution)/shard_map/ppermute | solution.py:51
  35.6 18.0 %collective-permute-start.6 = (bf16[512,512]{1,0:T(8,128)(2,1)S(1)}, bf16[512,512]{1,0:T(8,128)(2,1)S(1)}, u32[]{:S(2)}, u32[]{:S(2)}) collective-permute-start(bf16[512,512]{1,0:T(8,128)(2,1)S(1)} %pad_maximum_fusion.refs_0_), channel_id=1, source_target_pairs={{0,2},{1,9},{2,4},{3,11},{4,6},{5,13},{6,0},{7,15},{8,10},{9,17},{... | collective-permute-start | bytes 1572872 | tf_op jit(solution)/shard_map/ppermute | solution.py:51
  35.7 17.8 %collective-permute-start.10 = (bf16[512,512]{1,0:T(8,128)(2,1)S(1)}, bf16[512,512]{1,0:T(8,128)(2,1)S(1)}, u32[]{:S(2)}, u32[]{:S(2)}) collective-permute-start(bf16[512,512]{1,0:T(8,128)(2,1)S(1)} %constant_dynamic-update-slice_fusion.refs_1_), channel_id=1, source_target_pairs={{0,6},{1,25},{2,0},{3,27},{4,2},{5,29},{6,4},{7,31},{8,14},{9,1},{... | collective-permute-start | bytes 1572872 | tf_op jit(solution)/shard_map/ppermute | solution.py:51
  37.3 6.2 %collective-permute-start.13 = (bf16[128,1024]{1,0:T(8,128)(2,1)S(1)}, bf16[128,1024]{1,0:T(8,128)(2,1)S(1)}, u32[]{:S(2)}, u32[]{:S(2)}) collective-permute-start(bf16[128,1024]{1,0:T(8,128)(2,1)S(1)} %get-tuple-element.51), channel_id=1, source_target_pairs={{0,96},{1,97},{2,98},{3,99},{4,100},{5,101},{6,102},{7,103},{8,104... | collective-permute-start | bytes 786440 | tf_op jit(solution)/shard_map/ppermute | solution.py:51
  38.7 11.9 %collective-permute-start.14 = (bf16[128,1024]{1,0:T(8,128)(2,1)S(1)}, bf16[128,1024]{1,0:T(8,128)(2,1)S(1)}, u32[]{:S(2)}, u32[]{:S(2)}) collective-permute-start(bf16[128,1024]{1,0:T(8,128)(2,1)S(1)} %get-tuple-element.52), channel_id=1, source_target_pairs={{0,64},{1,65},{2,66},{3,67},{4,68},{5,69},{6,70},{7,71},{8,72},{9,... | collective-permute-start | bytes 786440 | tf_op jit(solution)/shard_map/ppermute | solution.py:51
  43.4 10.1 %collective-permute-start.17 = (bf16[128,1024]{1,0:T(8,128)(2,1)S(1)}, bf16[128,1024]{1,0:T(8,128)(2,1)S(1)}, u32[]{:S(2)}, u32[]{:S(2)}) collective-permute-start(bf16[128,1024]{1,0:T(8,128)(2,1)S(1)} %get-tuple-element.58), channel_id=1, source_target_pairs={{0,32},{1,33},{2,34},{3,35},{4,36},{5,37},{6,38},{7,39},{8,40},{9,... | collective-permute-start | bytes 786440 | tf_op jit(solution)/shard_map/ppermute | solution.py:51
  43.4 13.1 %collective-permute-start.18 = (bf16[128,1024]{1,0:T(8,128)(2,1)S(1)}, bf16[128,1024]{1,0:T(8,128)(2,1)S(1)}, u32[]{:S(2)}, u32[]{:S(2)}) collective-permute-start(bf16[128,1024]{1,0:T(8,128)(2,1)S(1)} %get-tuple-element.59), channel_id=1, source_target_pairs={{0,96},{1,97},{2,98},{3,99},{4,100},{5,101},{6,102},{7,103},{8,104... | collective-permute-start | bytes 786440 | tf_op jit(solution)/shard_map/ppermute | solution.py:51
  50.6 15.1 %collective-permute-start.16 = (bf16[512,512]{1,0:T(8,128)(2,1)S(1)}, bf16[512,512]{1,0:T(8,128)(2,1)S(1)}, u32[]{:S(2)}, u32[]{:S(2)}) collective-permute-start(bf16[512,512]{1,0:T(8,128)(2,1)S(1)} %pad_maximum_fusion.refs_0_), channel_id=1, source_target_pairs={{0,6},{1,25},{2,0},{3,27},{4,2},{5,29},{6,4},{7,31},{8,14},{9,1},{... | collective-permute-start | bytes 1572872 | tf_op jit(solution)/shard_map/ppermute | solution.py:51
  53.6 12.1 %collective-permute-start.15 = (bf16[512,512]{1,0:T(8,128)(2,1)S(1)}, bf16[512,512]{1,0:T(8,128)(2,1)S(1)}, u32[]{:S(2)}, u32[]{:S(2)}) collective-permute-start(bf16[512,512]{1,0:T(8,128)(2,1)S(1)} %constant_dynamic-update-slice_fusion.refs_1_), channel_id=1, source_target_pairs={{0,2},{1,9},{2,4},{3,11},{4,6},{5,13},{6,0},{7,15},{8,10},{9,17},{... | collective-permute-start | bytes 1572872 | tf_op jit(solution)/shard_map/ppermute | solution.py:51
  53.6 17.3 %collective-permute-start.7 = (bf16[512,512]{1,0:T(8,128)(2,1)S(1)}, bf16[512,512]{1,0:T(8,128)(2,1)S(1)}, u32[]{:S(2)}, u32[]{:S(2)}) collective-permute-start(bf16[512,512]{1,0:T(8,128)(2,1)S(1)} %collective-permute-done.6.refs_0_), channel_id=1, source_target_pairs={{0,2},{1,9},{2,4},{3,11},{4,6},{5,13},{6,0},{7,15},{8,10},{9,17},{... | collective-permute-start | bytes 1572872 | tf_op jit(solution)/shard_map/ppermute | solution.py:51
  53.6 17.3 %collective-permute-start.11 = (bf16[512,512]{1,0:T(8,128)(2,1)S(1)}, bf16[512,512]{1,0:T(8,128)(2,1)S(1)}, u32[]{:S(2)}, u32[]{:S(2)}) collective-permute-start(bf16[512,512]{1,0:T(8,128)(2,1)S(1)} %collective-permute-done.10.refs_2_), channel_id=1, source_target_pairs={{0,6},{1,25},{2,0},{3,27},{4,2},{5,29},{6,4},{7,31},{8,14},{9,1},{... | collective-permute-start | bytes 1572872 | tf_op jit(solution)/shard_map/ppermute | solution.py:51
  56.5 7.0 %collective-permute-start.19 = (bf16[128,1024]{1,0:T(8,128)(2,1)S(1)}, bf16[128,1024]{1,0:T(8,128)(2,1)S(1)}, u32[]{:S(2)}, u32[]{:S(2)}) collective-permute-start(bf16[128,1024]{1,0:T(8,128)(2,1)S(1)} %get-tuple-element.60), channel_id=1, source_target_pairs={{0,64},{1,65},{2,66},{3,67},{4,68},{5,69},{6,70},{7,71},{8,72},{9,... | collective-permute-start | bytes 786440 | tf_op jit(solution)/shard_map/ppermute | solution.py:51
  74.8 7.9 %collective-permute-start.20 = (bf16[128,1024]{1,0:T(8,128)(2,1)S(1)}, bf16[128,1024]{1,0:T(8,128)(2,1)S(1)}, u32[]{:S(2)}, u32[]{:S(2)}) collective-permute-start(bf16[128,1024]{1,0:T(8,128)(2,1)S(1)} %get-tuple-element.72), channel_id=1, source_target_pairs={{0,1},{1,0},{2,3},{3,2},{4,5},{5,4},{6,7},{7,6},{8,9},{9,8},{10,11... | collective-permute-start | bytes 786440 | tf_op jit(solution)/shard_map/ppermute | solution.py:51

commit v6 on v5

--- a/solution.py
+++ b/solution.py
@@ -73,9 +73,8 @@
 CHUNKS = 4
 
 
-def prepare_kernel(core_ref, other_ref, owner_ref, order_ref, x_ref, w_ref, *refs):
-    x_out, w_out = refs[:2]
-    sems = refs[6]
+def prepare_kernel(core_ref, owner_ref, order_ref, x_ref, w_ref, *refs):
+    x_out, w_out, cos_ref, sin_ref, sems = refs
     core = core_ref[0]
     width = 2 * HD
     rows = w_out.shape[0] // CHUNKS
@@ -93,32 +92,30 @@
             )
     for copy in copies:
         copy.start()
-    column = lax.axis_index("cp")
-    rope_tables(order_ref[other_ref[0, 0], column + 1 - 2 * core], *refs[2:4])
-    rope_tables(order_ref[owner_ref[0, 0], column], *refs[4:6])
+    rope_tables(order_ref[owner_ref[0, 0], lax.axis_index("cp")], cos_ref, sin_ref)
     for copy in copies:
         copy.wait()
 
 
-def prepare(core, owners, slab_order, rows, weight):
+def prepare(core, owner, slab_order, rows, weight):
     smem = pl.BlockSpec(memory_space=pltpu.SMEM)
     anywhere = pl.BlockSpec(memory_space=pl.ANY)
     vmem = pl.BlockSpec(memory_space=pltpu.VMEM)
     depth = rows.shape[1]
     return pl.pallas_call(
         prepare_kernel,
-        in_specs=[smem] * 4 + [anywhere] * 2,
-        out_specs=[vmem] * 6,
+        in_specs=[smem] * 3 + [anywhere] * 2,
+        out_specs=[vmem] * 4,
         out_shape=[
             pltpu.VMEM(rows.shape, rows.dtype),
             pltpu.VMEM((depth, 4 * HD), weight.dtype),
         ]
-        + [pltpu.VMEM((SLAB, HD), jnp.float32)] * 4,
+        + [pltpu.VMEM((SLAB, HD), jnp.float32)] * 2,
         scratch_shapes=[pltpu.SemaphoreType.DMA((2 * CHUNKS + 1,))],
         compiler_params=pltpu.CompilerParams(vmem_limit_bytes=8 << 20),
         cost_estimate=pl.CostEstimate(flops=1 << 26, bytes_accessed=5 << 20, transcendentals=1 << 16),
         name="prepare",
-    )(core, *owners, in_hbm(slab_order), in_hbm(rows), in_hbm(weight))
+    )(core, owner, in_hbm(slab_order), in_hbm(rows), in_hbm(weight))
 
 
 def store_masked(outs, owner, rows, first, value):
@@ -129,8 +126,10 @@
         out[rows, columns] = jnp.where(mine, value, jnp.zeros_like(value))
 
 
-def kv_kernel(other_ref, owner_ref, y_ref, x_ref, w_ref, *refs):
-    ropes, outs = (refs[:2], refs[2:4]), refs[4:]
+def kv_kernel(core_ref, other_ref, owner_ref, order_ref, y_ref, x_ref, w_ref, *refs):
+    ropes, outs = (refs[2:4], refs[:2]), refs[4:]
+    column = lax.axis_index("cp") + 1 - 2 * core_ref[0]
+    rope_tables(order_ref[other_ref[0, 0], column], *ropes[0])
     owners = (other_ref[0, 0], owner_ref[0, 0])
     both = jnp.concatenate([y_ref[...], x_ref[...]], axis=0)
     wide = 512
@@ -191,21 +190,22 @@
     return pltpu.with_memory_space_constraint(value, pltpu.HBM)
 
 
-def project_kv(owners, others, rows, weight, tables):
+def project_kv(core, owners, slab_order, others, rows, weight, tables):
     smem = pl.BlockSpec(memory_space=pltpu.SMEM)
     vmem = pl.BlockSpec(memory_space=pltpu.VMEM)
     operands = [in_vmem(v) for v in (others, rows, weight, *tables)]
     return pl.pallas_call(
         kv_kernel,
-        in_specs=[smem] * 2 + [vmem] * len(operands),
-        out_specs=[vmem] * 4,
-        out_shape=[pltpu.VMEM((2 * SLAB, 4 * HD), jnp.bfloat16)] * 4,
+        in_specs=[smem] * 4 + [vmem] * len(operands),
+        out_specs=[vmem] * 6,
+        out_shape=[pltpu.VMEM((SLAB, HD), jnp.float32)] * 2
+        + [pltpu.VMEM((2 * SLAB, 4 * HD), jnp.bfloat16)] * 4,
         compiler_params=pltpu.CompilerParams(vmem_limit_bytes=24 << 20),
         cost_estimate=pl.CostEstimate(
             flops=4 * SLAB * rows.shape[1] * 4 * HD, bytes_accessed=4 << 20, transcendentals=0
         ),
         name="kv_proj",
-    )(*owners, *operands)
+    )(core, *owners, in_hbm(slab_order), *operands)
 
 
 QPARTS = 2
@@ -345,7 +345,7 @@
     lax.fori_loop(0, pairs_here, weigh, 0)
     if out is not None:
         for g in range(2):
-            context = acc[g] / jnp.sum(total[g], axis=0, keepdims=True)
+            context = acc[g] * (1.0 / jnp.sum(total[g], axis=0, keepdims=True))
             for h in range(GROUP):
                 head = g * GROUP + h
                 out[:, head * HD : (head + 1) * HD] = context[:, h * SLAB : (h + 1) * SLAB].T.astype(
@@ -437,8 +437,11 @@
     others = permute(rows, OTHER_CORE)
     owners = (permute(owner_slot, OTHER_CORE), owner_slot)
     core = core.reshape(1)
-    rows, kv_weight, *tables = prepare(core, owners, slab_order, rows, qkv_weight)
-    kv = project_kv(owners, others, rows, kv_weight, tables)
+    rows, kv_weight, *tables = prepare(core, owner_slot, slab_order, rows, qkv_weight)
+    other_cos, other_sin, *kv = project_kv(
+        core, owners, slab_order, others, rows, kv_weight, tables
+    )
+    tables = (other_cos, other_sin, *tables)
     queries = project_q(core, owners, others, rows, qkv_weight, tables)
     moved = [permute(kv[k], shift_x(k)) for k in (1, 3, 2)]
     parts = [[queries[0]] + [permute(queries[k], shift_x(k)) for k in (1, 3, 2)]]

time: 83.9 us -> 82.4 us (0.982)
  the two profiles are of different devices: /device:TPU:99 before, /device:TPU:75 now
where the time goes in v6:
time: 82.4 us; the launch traced here: 82.1 us
  Pallas kernels  27.7 us (34%)
  waiting for transfers between devices  27.1 us (33%)
  starting transfers between devices  26.4 us (32%)
    ppermute x21, waiting for transfers between devices, permute(): return lax.ppermute(value, AXES, table)  27.1 us
    ppermute x21, starting transfers between devices, permute(): return lax.ppermute(value, AXES, table)  26.4 us
    pallas_call x4, Pallas kernels, attend(): pl.pallas_call(functools.partial(attend_kernel, jobs, spots, last), in_sp...  14.6 us
    pallas_call x1, Pallas kernels, project_q(): pl.pallas_call(q_kernel, in_specs=[smem] * 3 + [pl.BlockSpec(memory_space...  6.17 us
    pallas_call x1, Pallas kernels, prepare(): pl.pallas_call(prepare_kernel, in_specs=[smem] * 3 + [anywhere] * 2, out_...  3.33 us
    pallas_call x1, Pallas kernels, project_kv(): pl.pallas_call(kv_kernel, in_specs=[smem] * 4 + [vmem] * len(operands), o...  2.85 us
  transfers between devices with their start and end apart: 21, of which 9 were waited for; matrix products, arithmetic and copies ran while one was open for 0% of the time, Pallas kernels for 25%

profile of v6, /device:TPU:75, one launch (start us, length us, event | category | flops | bytes accessed | tf_op | source)
XLA Modules:
  0.0 82.1 jit_solution(3552144139138194763)
XLA Ops:
  0.0 0.7 collective-permute-start.1
  0.7 0.0 collective-permute-start
  1.3 3.3 %prepare.1 = (bf16[128,4096]{1,0:T(8,128)(2,1)S(1)}, bf16[4096,512]{1,0:T(8,128)(2,1)S(1)}, f32[128,128]{1,0:T(8,128)S(1)}, f32[128,128]{1,0:T(8,128)S(1)}) custom-call(s32[1]{0:T(128)} %bitcast.core_ref, s32[1,1]{1,0:T(1,128)S(6)} %copy.7.owner_ref, s32[4,32]{1,0:T(4,128)} %order_ref.11, bf16[128,4096]{1,0:T(8,128)(2,1)} %bitcast.4, bf16[4096,3072]{1,0:T(8,128)(2,1)} %w_ref.3), custom_call_target="tpu_custom_call" | custom-call | flops 67108864 | bytes 5242880 | tf_op jit(solution)/shard_map/prepare/pallas_call | solution.py:105
  4.7 0.0 collective-permute-done.other_ref
  4.7 0.0 collective-permute-done.1.y_ref
  4.7 2.8 %kv_proj.1 = (f32[128,128]{1,0:T(8,128)S(1)}, f32[128,128]{1,0:T(8,128)S(1)}, bf16[256,512]{1,0:T(8,128)(2,1)S(1)}, bf16[256,512]{1,0:T(8,128)(2,1)S(1)}, bf16[2...) custom-call(s32[1]{0:T(128)} %bitcast.core_ref, s32[1,1]{1,0:T(1,128)} %collective-permute-done.other_ref, ...), custom_call_target="tpu_custom_call" | custom-call | flops 1073741824 | bytes 4194304 | tf_op jit(solution)/shard_map/kv_proj/pallas_call | solution.py:197
  7.5 1.3 %collective-permute-start.2 = (bf16[256,512]{1,0:T(8,128)(2,1)S(1)}, bf16[256,512]{1,0:T(8,128)(2,1)S(1)}, u32[]{:S(2)}, u32[]{:S(2)}) collective-permute-start(bf16[256,512]{1,0:T(8,128)(2,1)S(1)} %get-tuple-element.44), channel_id=1, source_target_pairs={{0,32},{1,33},{2,34},{3,35},{4,36},{5,37},{6,38},{7,39},{8,40},{9,... | collective-permute-start | bytes 786440 | tf_op jit(solution)/shard_map/ppermute | solution.py:51
  8.8 0.3 collective-permute-start.3
  9.1 1.8 %collective-permute-start.4 = (bf16[256,512]{1,0:T(8,128)(2,1)S(1)}, bf16[256,512]{1,0:T(8,128)(2,1)S(1)}, u32[]{:S(2)}, u32[]{:S(2)}) collective-permute-start(bf16[256,512]{1,0:T(8,128)(2,1)S(1)} %get-tuple-element.46), channel_id=1, source_target_pairs={{0,64},{1,65},{2,66},{3,67},{4,68},{5,69},{6,70},{7,71},{8,72},{9,... | collective-permute-start | bytes 786440 | tf_op jit(solution)/shard_map/ppermute | solution.py:51
  10.9 4.0 %collective-permute-done.2 = bf16[256,512]{1,0:T(8,128)(2,1)S(1)} collective-permute-done((bf16[256,512]{1,0:T(8,128)(2,1)S(1)}, bf16[256,512]{1,0:T(8,128)(2,1)S(1)}, u32[]{:S(2)}, u32[]{:S(2)}) %collective-permute-start.2) | collective-permute-done | bytes 262176 | tf_op jit(solution)/shard_map/ppermute | solution.py:51
  15.0 0.9 %collective-permute-done.3 = bf16[256,512]{1,0:T(8,128)(2,1)S(1)} collective-permute-done((bf16[256,512]{1,0:T(8,128)(2,1)S(1)}, bf16[256,512]{1,0:T(8,128)(2,1)S(1)}, u32[]{:S(2)}, u32[]{:S(2)}) %collective-permute-start.3) | collective-permute-done | bytes 262176 | tf_op jit(solution)/shard_map/ppermute | solution.py:51
  15.9 6.3 %collective-permute-done.4 = bf16[256,512]{1,0:T(8,128)(2,1)S(1)} collective-permute-done((bf16[256,512]{1,0:T(8,128)(2,1)S(1)}, bf16[256,512]{1,0:T(8,128)(2,1)S(1)}, u32[]{:S(2)}, u32[]{:S(2)}) %collective-permute-start.4) | collective-permute-done | bytes 262176 | tf_op jit(solution)/shard_map/ppermute | solution.py:51
  22.2 0.1 add_add_fusion
  22.2 1.4 %collective-permute-start.5 = (bf16[256,512]{1,0:T(8,128)(2,1)S(1)}, bf16[256,512]{1,0:T(8,128)(2,1)S(1)}, u32[]{:S(2)}, u32[]{:S(2)}) collective-permute-start(bf16[256,512]{1,0:T(8,128)(2,1)S(1)} %add_add_fusion), channel_id=1, source_target_pairs={{0,8},{1,3},{2,10},{3,5},{4,12},{5,7},{6,14},{7,1},{8,16},{9,11},{... | collective-permute-start | bytes 786440 | tf_op jit(solution)/shard_map/ppermute | solution.py:51
  23.6 0.8 collective-permute-start.9
  24.4 2.0 %collective-permute-start.8 = (bf16[256,512]{1,0:T(8,128)(2,1)S(1)}, bf16[256,512]{1,0:T(8,128)(2,1)S(1)}, u32[]{:S(2)}, u32[]{:S(2)}) collective-permute-start(bf16[256,512]{1,0:T(8,128)(2,1)S(1)} %add_add_fusion), channel_id=1, source_target_pairs={{0,24},{1,7},{2,26},{3,1},{4,28},{5,3},{6,30},{7,5},{8,0},{9,15},{... | collective-permute-start | bytes 786440 | tf_op jit(solution)/shard_map/ppermute | solution.py:51
  26.4 6.2 %q_proj.1 = (bf16[128,1024]{1,0:T(8,128)(2,1)S(1)}, bf16[128,1024]{1,0:T(8,128)(2,1)S(1)}, bf16[128,1024]{1,0:T(8,128)(2,1)S(1)}, bf16[128,1024]{1,0:T(8,128)(2,...) custom-call(s32[1]{0:T(128)} %bitcast.core_ref, ...), custom_call_target="tpu_custom_call" | custom-call | flops 2147483648 | bytes 8388608 | tf_op jit(solution)/shard_map/q_proj/pallas_call | solution.py:219
  32.5 0.1 collective-permute-start.12
  32.6 0.0 collective-permute-done.5
  32.7 1.4 %collective-permute-start.6 = (bf16[512,512]{1,0:T(8,128)(2,1)S(1)}, bf16[512,512]{1,0:T(8,128)(2,1)S(1)}, u32[]{:S(2)}, u32[]{:S(2)}) collective-permute-start(bf16[512,512]{1,0:T(8,128)(2,1)S(1)} %pad_maximum_fusion.refs_0_), channel_id=1, source_target_pairs={{0,2},{1,9},{2,4},{3,11},{4,6},{5,13},{6,0},{7,15},{8,10},{9,17},{... | collective-permute-start | bytes 1572872 | tf_op jit(solution)/shard_map/ppermute | solution.py:51
  34.1 0.0 collective-permute-done.8
  34.1 0.0 collective-permute-done.9
  34.2 0.2 collective-permute-start.10
  34.4 1.4 %collective-permute-start.13 = (bf16[128,1024]{1,0:T(8,128)(2,1)S(1)}, bf16[128,1024]{1,0:T(8,128)(2,1)S(1)}, u32[]{:S(2)}, u32[]{:S(2)}) collective-permute-start(bf16[128,1024]{1,0:T(8,128)(2,1)S(1)} %get-tuple-element.51), channel_id=1, source_target_pairs={{0,96},{1,97},{2,98},{3,99},{4,100},{5,101},{6,102},{7,103},{8,104... | collective-permute-start | bytes 786440 | tf_op jit(solution)/shard_map/ppermute | solution.py:51
  35.8 1.3 %collective-permute-start.14 = (bf16[128,1024]{1,0:T(8,128)(2,1)S(1)}, bf16[128,1024]{1,0:T(8,128)(2,1)S(1)}, u32[]{:S(2)}, u32[]{:S(2)}) collective-permute-start(bf16[128,1024]{1,0:T(8,128)(2,1)S(1)} %get-tuple-element.52), channel_id=1, source_target_pairs={{0,64},{1,65},{2,66},{3,67},{4,68},{5,69},{6,70},{7,71},{8,72},{9,... | collective-permute-start | bytes 786440 | tf_op jit(solution)/shard_map/ppermute | solution.py:51
  37.1 2.6 %collective-permute-done.12.refs_3_ = bf16[128,1024]{1,0:T(8,128)(2,1)S(1)} collective-permute-done((bf16[128,1024]{1,0:T(8,128)(2,1)S(1)}, bf16[128,1024]{1,0:T(8,128)(2,1)S(1)}, u32[]{:S(2)}, u32[]{:S(2)}) %collective-permute-start.12) | collective-permute-done | bytes 262176 | tf_op jit(solution)/shard_map/ppermute | solution.py:51
  39.6 0.3 collective-permute-start.17
  39.9 0.7 collective-permute-done.13.refs_4_
  40.6 2.2 %collective-permute-start.18 = (bf16[128,1024]{1,0:T(8,128)(2,1)S(1)}, bf16[128,1024]{1,0:T(8,128)(2,1)S(1)}, u32[]{:S(2)}, u32[]{:S(2)}) collective-permute-start(bf16[128,1024]{1,0:T(8,128)(2,1)S(1)} %get-tuple-element.59), channel_id=1, source_target_pairs={{0,96},{1,97},{2,98},{3,99},{4,100},{5,101},{6,102},{7,103},{8,104... | collective-permute-start | bytes 786440 | tf_op jit(solution)/shard_map/ppermute | solution.py:51
  42.8 4.3 %collective-permute-done.14.refs_5_ = bf16[128,1024]{1,0:T(8,128)(2,1)S(1)} collective-permute-done((bf16[128,1024]{1,0:T(8,128)(2,1)S(1)}, bf16[128,1024]{1,0:T(8,128)(2,1)S(1)}, u32[]{:S(2)}, u32[]{:S(2)}) %collective-permute-start.14) | collective-permute-done | bytes 262176 | tf_op jit(solution)/shard_map/ppermute | solution.py:51
  47.1 0.0 collective-permute-start.16
  47.1 3.1 %collective-permute-done.17.refs_3_ = bf16[128,1024]{1,0:T(8,128)(2,1)S(1)} collective-permute-done((bf16[128,1024]{1,0:T(8,128)(2,1)S(1)}, bf16[128,1024]{1,0:T(8,128)(2,1)S(1)}, u32[]{:S(2)}, u32[]{:S(2)}) %collective-permute-start.17) | collective-permute-done | bytes 262176 | tf_op jit(solution)/shard_map/ppermute | solution.py:51
  50.3 2.1 %collective-permute-start.15 = (bf16[512,512]{1,0:T(8,128)(2,1)S(1)}, bf16[512,512]{1,0:T(8,128)(2,1)S(1)}, u32[]{:S(2)}, u32[]{:S(2)}) collective-permute-start(bf16[512,512]{1,0:T(8,128)(2,1)S(1)} %constant_dynamic-update-slice_fusion.refs_1_), channel_id=1, source_target_pairs={{0,2},{1,9},{2,4},{3,11},{4,6},{5,13},{6,0},{7,15},{8,10},{9,17},{... | collective-permute-start | bytes 1572872 | tf_op jit(solution)/shard_map/ppermute | solution.py:51
  52.4 0.0 collective-permute-done.6.refs_0_
  52.4 0.1 collective-permute-start.7
  52.6 0.0 collective-permute-done.10.refs_2_
  52.6 1.3 %collective-permute-start.11 = (bf16[512,512]{1,0:T(8,128)(2,1)S(1)}, bf16[512,512]{1,0:T(8,128)(2,1)S(1)}, u32[]{:S(2)}, u32[]{:S(2)}) collective-permute-start(bf16[512,512]{1,0:T(8,128)(2,1)S(1)} %collective-permute-done.10.refs_2_), channel_id=1, source_target_pairs={{0,6},{1,25},{2,0},{3,27},{4,2},{5,29},{6,4},{7,31},{8,14},{9,1},{... | collective-permute-start | bytes 1572872 | tf_op jit(solution)/shard_map/ppermute | solution.py:51
  53.9 0.0 collective-permute-done.18.refs_4_
  53.9 0.8 collective-permute-start.19
  54.7 2.0 %shard_map.55 = (f32[2,128,512]{2,1,0:T(8,128)S(1)}, f32[2,8,512]{2,1,0:T(8,128)S(1)}, f32[2,8,512]{2,1,0:T(8,128)S(1)}, bf16[128,1024]{1,0:T(8,128)(2,1)S(1)}) custom-call(s32[4,32]{1,0:T(4,128)} %sequence_ref.7, s32[4,32]{1,0:T(4,128)} %order_ref.11, bf16[512,512]{1,0:T(8,128)(2,1)S(1)} %pad_maximum_fusion.refs_0_, ...), custom_call_target="tpu_custom_call" | custom-call | flops 268435456 | bytes 2097152 | tf_op jit(solution)/shard_map/pallas_call | solution.py:400
  56.7 3.9 %collective-permute-done.19.refs_5_ = bf16[128,1024]{1,0:T(8,128)(2,1)S(1)} collective-permute-done((bf16[128,1024]{1,0:T(8,128)(2,1)S(1)}, bf16[128,1024]{1,0:T(8,128)(2,1)S(1)}, u32[]{:S(2)}, u32[]{:S(2)}) %collective-permute-start.19) | collective-permute-done | bytes 262176 | tf_op jit(solution)/shard_map/ppermute | solution.py:51
  60.6 2.8 %shard_map.56 = (f32[2,128,512]{2,1,0:T(8,128)S(1)}, f32[2,8,512]{2,1,0:T(8,128)S(1)}, f32[2,8,512]{2,1,0:T(8,128)S(1)}, bf16[128,1024]{1,0:T(8,128)(2,1)S(1)}) custom-call(s32[4,32]{1,0:T(4,128)} %sequence_ref.7, s32[4,32]{1,0:T(4,128)} %order_ref.11, bf16[512,512]{1,0:T(8,128)(2,1)S(1)} %pad_maximum_fusion.refs_0_, ...), custom_call_target="tpu_custom_call" | custom-call | flops 268435456 | bytes 2097152 | tf_op jit(solution)/shard_map/pallas_call | solution.py:400
  63.5 0.0 collective-permute-done.16.refs_3_
  63.5 5.8 %shard_map.57 = (f32[2,128,512]{2,1,0:T(8,128)S(1)}, f32[2,8,512]{2,1,0:T(8,128)S(1)}, f32[2,8,512]{2,1,0:T(8,128)S(1)}, f32[2,128,512]{2,1,0:T(8,128)S(1)}, f32...) custom-call(s32[4,32]{1,0:T(4,128)} %sequence_ref.7, s32[4,32]{1,0:T(4,128)} %order_ref.11, ...), custom_call_target="tpu_custom_call" | custom-call | flops 536870912 | bytes 2097152 | tf_op jit(solution)/shard_map/pallas_call | solution.py:400
  69.3 3.9 %shard_map.58 = (bf16[128,1024]{1,0:T(8,128)(2,1)S(1)}, bf16[128,1024]{1,0:T(8,128)(2,1)S(1)}) custom-call(s32[4,32]{1,0:T(4,128)} %sequence_ref.7, s32[4,32]{1,0:T(4,128)} %order_ref.11, bf16[512,512]{1,0:T(8,128)(2,1)S(1)} %collective-permute-done.7.refs_0_, bf16[512,512]{1,0:T(8,128)(2,1)S(1)} %collective-permute-done.11.refs_1_, ...), custom_call_target="tpu_custom_call" | custom-call | flops 268435456 | bytes 2097152 | tf_op jit(solution)/shard_map/pallas_call | solution.py:400
  73.2 6.9 %collective-permute-start.20 = (bf16[128,1024]{1,0:T(8,128)(2,1)S(1)}, bf16[128,1024]{1,0:T(8,128)(2,1)S(1)}, u32[]{:S(2)}, u32[]{:S(2)}) collective-permute-start(bf16[128,1024]{1,0:T(8,128)(2,1)S(1)} %get-tuple-element.72), channel_id=1, source_target_pairs={{0,1},{1,0},{2,3},{3,2},{4,5},{5,4},{6,7},{7,6},{8,9},{9,8},{10,11... | collective-permute-start | bytes 786440 | tf_op jit(solution)/shard_map/ppermute | solution.py:51
  80.1 1.2 %collective-permute-done.20.received_ref = bf16[128,1024]{1,0:T(8,128)(2,1)S(1)} collective-permute-done((bf16[128,1024]{1,0:T(8,128)(2,1)S(1)}, bf16[128,1024]{1,0:T(8,128)(2,1)S(1)}, u32[]{:S(2)}, u32[]{:S(2)}) %collective-permute-start.20) | collective-permute-done | bytes 262176 | tf_op jit(solution)/shard_map/ppermute | solution.py:51
  81.3 0.8 %join.1 = bf16[128,2048]{1,0:T(8,128)(2,1)} custom-call(s32[1]{0:T(128)} %bitcast.core_ref, bf16[128,1024]{1,0:T(8,128)(2,1)S(1)} %get-tuple-element.71.kept_ref, bf16[128,1024]{1,0:T(8,128)(2,1)S(1)} %collective-permute-done.20.received_ref), custom_call_target="tpu_custom_call" | custom-call | flops 262144 | bytes 1048576 | tf_op jit(solution)/shard_map/join/pallas_call | solution.py:423
  (6 shorter events, 0.1 us)
Async XLA Ops:
  0.0 4.7 %collective-permute-start.1 = (bf16[128,4096]{1,0:T(8,128)(2,1)}, bf16[128,4096]{1,0:T(8,128)(2,1)S(1)}, u32[]{:S(2)}, u32[]{:S(2)}) collective-permute-start(bf16[128,4096]{1,0:T(8,128)(2,1)} %bitcast.3), channel_id=1, source_target_pairs={{0,1},{1,0},{2,3},{3,2},{4,5},{5,4},{6,7},{7,6},{8,9},{9,8},{10,11... | collective-permute-start | bytes 3145736 | tf_op jit(solution)/shard_map/ppermute | solution.py:51
  0.7 4.0 %collective-permute-start = (s32[1,1]{1,0:T(1,128)}, s32[1,1]{1,0:T(1,128)}, u32[]{:S(2)}, u32[]{:S(2)}) collective-permute-start(s32[1,1]{1,0:T(1,128)} %param.7), channel_id=1, source_target_pairs={{0,1},{1,0},{2,3},{3,2},{4,5},{5,4},{6,7},{7,6},{8,9},{9,8},{10,11... | collective-permute-start | bytes 20 | tf_op jit(solution)/shard_map/ppermute | solution.py:51
  7.5 7.4 %collective-permute-start.2 = (bf16[256,512]{1,0:T(8,128)(2,1)S(1)}, bf16[256,512]{1,0:T(8,128)(2,1)S(1)}, u32[]{:S(2)}, u32[]{:S(2)}) collective-permute-start(bf16[256,512]{1,0:T(8,128)(2,1)S(1)} %get-tuple-element.44), channel_id=1, source_target_pairs={{0,32},{1,33},{2,34},{3,35},{4,36},{5,37},{6,38},{7,39},{8,40},{9,... | collective-permute-start | bytes 786440 | tf_op jit(solution)/shard_map/ppermute | solution.py:51
  8.8 7.1 %collective-permute-start.3 = (bf16[256,512]{1,0:T(8,128)(2,1)S(1)}, bf16[256,512]{1,0:T(8,128)(2,1)S(1)}, u32[]{:S(2)}, u32[]{:S(2)}) collective-permute-start(bf16[256,512]{1,0:T(8,128)(2,1)S(1)} %get-tuple-element.45), channel_id=1, source_target_pairs={{0,96},{1,97},{2,98},{3,99},{4,100},{5,101},{6,102},{7,103},{8,104... | collective-permute-start | bytes 786440 | tf_op jit(solution)/shard_map/ppermute | solution.py:51
  9.1 13.1 %collective-permute-start.4 = (bf16[256,512]{1,0:T(8,128)(2,1)S(1)}, bf16[256,512]{1,0:T(8,128)(2,1)S(1)}, u32[]{:S(2)}, u32[]{:S(2)}) collective-permute-start(bf16[256,512]{1,0:T(8,128)(2,1)S(1)} %get-tuple-element.46), channel_id=1, source_target_pairs={{0,64},{1,65},{2,66},{3,67},{4,68},{5,69},{6,70},{7,71},{8,72},{9,... | collective-permute-start | bytes 786440 | tf_op jit(solution)/shard_map/ppermute | solution.py:51
  22.2 10.4 %collective-permute-start.5 = (bf16[256,512]{1,0:T(8,128)(2,1)S(1)}, bf16[256,512]{1,0:T(8,128)(2,1)S(1)}, u32[]{:S(2)}, u32[]{:S(2)}) collective-permute-start(bf16[256,512]{1,0:T(8,128)(2,1)S(1)} %add_add_fusion), channel_id=1, source_target_pairs={{0,8},{1,3},{2,10},{3,5},{4,12},{5,7},{6,14},{7,1},{8,16},{9,11},{... | collective-permute-start | bytes 786440 | tf_op jit(solution)/shard_map/ppermute | solution.py:51
  23.6 10.6 %collective-permute-start.9 = (bf16[256,512]{1,0:T(8,128)(2,1)S(1)}, bf16[256,512]{1,0:T(8,128)(2,1)S(1)}, u32[]{:S(2)}, u32[]{:S(2)}) collective-permute-start(bf16[256,512]{1,0:T(8,128)(2,1)S(1)} %add_add_fusion), channel_id=1, source_target_pairs={{0,16},{1,5},{2,18},{3,7},{4,20},{5,1},{6,22},{7,3},{8,24},{9,13},... | collective-permute-start | bytes 786440 | tf_op jit(solution)/shard_map/ppermute | solution.py:51
  24.4 9.7 %collective-permute-start.8 = (bf16[256,512]{1,0:T(8,128)(2,1)S(1)}, bf16[256,512]{1,0:T(8,128)(2,1)S(1)}, u32[]{:S(2)}, u32[]{:S(2)}) collective-permute-start(bf16[256,512]{1,0:T(8,128)(2,1)S(1)} %add_add_fusion), channel_id=1, source_target_pairs={{0,24},{1,7},{2,26},{3,1},{4,28},{5,3},{6,30},{7,5},{8,0},{9,15},{... | collective-permute-start | bytes 786440 | tf_op jit(solution)/shard_map/ppermute | solution.py:51
  32.5 7.1 %collective-permute-start.12 = (bf16[128,1024]{1,0:T(8,128)(2,1)S(1)}, bf16[128,1024]{1,0:T(8,128)(2,1)S(1)}, u32[]{:S(2)}, u32[]{:S(2)}) collective-permute-start(bf16[128,1024]{1,0:T(8,128)(2,1)S(1)} %get-tuple-element.50), channel_id=1, source_target_pairs={{0,32},{1,33},{2,34},{3,35},{4,36},{5,37},{6,38},{7,39},{8,40},{9,... | collective-permute-start | bytes 786440 | tf_op jit(solution)/shard_map/ppermute | solution.py:51
  32.7 19.7 %collective-permute-start.6 = (bf16[512,512]{1,0:T(8,128)(2,1)S(1)}, bf16[512,512]{1,0:T(8,128)(2,1)S(1)}, u32[]{:S(2)}, u32[]{:S(2)}) collective-permute-start(bf16[512,512]{1,0:T(8,128)(2,1)S(1)} %pad_maximum_fusion.refs_0_), channel_id=1, source_target_pairs={{0,2},{1,9},{2,4},{3,11},{4,6},{5,13},{6,0},{7,15},{8,10},{9,17},{... | collective-permute-start | bytes 1572872 | tf_op jit(solution)/shard_map/ppermute | solution.py:51
  34.2 18.4 %collective-permute-start.10 = (bf16[512,512]{1,0:T(8,128)(2,1)S(1)}, bf16[512,512]{1,0:T(8,128)(2,1)S(1)}, u32[]{:S(2)}, u32[]{:S(2)}) collective-permute-start(bf16[512,512]{1,0:T(8,128)(2,1)S(1)} %constant_dynamic-update-slice_fusion.refs_1_), channel_id=1, source_target_pairs={{0,6},{1,25},{2,0},{3,27},{4,2},{5,29},{6,4},{7,31},{8,14},{9,1},{... | collective-permute-start | bytes 1572872 | tf_op jit(solution)/shard_map/ppermute | solution.py:51
  34.4 6.3 %collective-permute-start.13 = (bf16[128,1024]{1,0:T(8,128)(2,1)S(1)}, bf16[128,1024]{1,0:T(8,128)(2,1)S(1)}, u32[]{:S(2)}, u32[]{:S(2)}) collective-permute-start(bf16[128,1024]{1,0:T(8,128)(2,1)S(1)} %get-tuple-element.51), channel_id=1, source_target_pairs={{0,96},{1,97},{2,98},{3,99},{4,100},{5,101},{6,102},{7,103},{8,104... | collective-permute-start | bytes 786440 | tf_op jit(solution)/shard_map/ppermute | solution.py:51
  35.8 11.3 %collective-permute-start.14 = (bf16[128,1024]{1,0:T(8,128)(2,1)S(1)}, bf16[128,1024]{1,0:T(8,128)(2,1)S(1)}, u32[]{:S(2)}, u32[]{:S(2)}) collective-permute-start(bf16[128,1024]{1,0:T(8,128)(2,1)S(1)} %get-tuple-element.52), channel_id=1, source_target_pairs={{0,64},{1,65},{2,66},{3,67},{4,68},{5,69},{6,70},{7,71},{8,72},{9,... | collective-permute-start | bytes 786440 | tf_op jit(solution)/shard_map/ppermute | solution.py:51
  39.6 10.6 %collective-permute-start.17 = (bf16[128,1024]{1,0:T(8,128)(2,1)S(1)}, bf16[128,1024]{1,0:T(8,128)(2,1)S(1)}, u32[]{:S(2)}, u32[]{:S(2)}) collective-permute-start(bf16[128,1024]{1,0:T(8,128)(2,1)S(1)} %get-tuple-element.58), channel_id=1, source_target_pairs={{0,32},{1,33},{2,34},{3,35},{4,36},{5,37},{6,38},{7,39},{8,40},{9,... | collective-permute-start | bytes 786440 | tf_op jit(solution)/shard_map/ppermute | solution.py:51
  40.6 13.3 %collective-permute-start.18 = (bf16[128,1024]{1,0:T(8,128)(2,1)S(1)}, bf16[128,1024]{1,0:T(8,128)(2,1)S(1)}, u32[]{:S(2)}, u32[]{:S(2)}) collective-permute-start(bf16[128,1024]{1,0:T(8,128)(2,1)S(1)} %get-tuple-element.59), channel_id=1, source_target_pairs={{0,96},{1,97},{2,98},{3,99},{4,100},{5,101},{6,102},{7,103},{8,104... | collective-permute-start | bytes 786440 | tf_op jit(solution)/shard_map/ppermute | solution.py:51
  47.1 16.3 %collective-permute-start.16 = (bf16[512,512]{1,0:T(8,128)(2,1)S(1)}, bf16[512,512]{1,0:T(8,128)(2,1)S(1)}, u32[]{:S(2)}, u32[]{:S(2)}) collective-permute-start(bf16[512,512]{1,0:T(8,128)(2,1)S(1)} %pad_maximum_fusion.refs_0_), channel_id=1, source_target_pairs={{0,6},{1,25},{2,0},{3,27},{4,2},{5,29},{6,4},{7,31},{8,14},{9,1},{... | collective-permute-start | bytes 1572872 | tf_op jit(solution)/shard_map/ppermute | solution.py:51
  50.3 13.2 %collective-permute-start.15 = (bf16[512,512]{1,0:T(8,128)(2,1)S(1)}, bf16[512,512]{1,0:T(8,128)(2,1)S(1)}, u32[]{:S(2)}, u32[]{:S(2)}) collective-permute-start(bf16[512,512]{1,0:T(8,128)(2,1)S(1)} %constant_dynamic-update-slice_fusion.refs_1_), channel_id=1, source_target_pairs={{0,2},{1,9},{2,4},{3,11},{4,6},{5,13},{6,0},{7,15},{8,10},{9,17},{... | collective-permute-start | bytes 1572872 | tf_op jit(solution)/shard_map/ppermute | solution.py:51
  52.4 16.9 %collective-permute-start.7 = (bf16[512,512]{1,0:T(8,128)(2,1)S(1)}, bf16[512,512]{1,0:T(8,128)(2,1)S(1)}, u32[]{:S(2)}, u32[]{:S(2)}) collective-permute-start(bf16[512,512]{1,0:T(8,128)(2,1)S(1)} %collective-permute-done.6.refs_0_), channel_id=1, source_target_pairs={{0,2},{1,9},{2,4},{3,11},{4,6},{5,13},{6,0},{7,15},{8,10},{9,17},{... | collective-permute-start | bytes 1572872 | tf_op jit(solution)/shard_map/ppermute | solution.py:51
  52.6 16.7 %collective-permute-start.11 = (bf16[512,512]{1,0:T(8,128)(2,1)S(1)}, bf16[512,512]{1,0:T(8,128)(2,1)S(1)}, u32[]{:S(2)}, u32[]{:S(2)}) collective-permute-start(bf16[512,512]{1,0:T(8,128)(2,1)S(1)} %collective-permute-done.10.refs_2_), channel_id=1, source_target_pairs={{0,6},{1,25},{2,0},{3,27},{4,2},{5,29},{6,4},{7,31},{8,14},{9,1},{... | collective-permute-start | bytes 1572872 | tf_op jit(solution)/shard_map/ppermute | solution.py:51
  53.9 6.7 %collective-permute-start.19 = (bf16[128,1024]{1,0:T(8,128)(2,1)S(1)}, bf16[128,1024]{1,0:T(8,128)(2,1)S(1)}, u32[]{:S(2)}, u32[]{:S(2)}) collective-permute-start(bf16[128,1024]{1,0:T(8,128)(2,1)S(1)} %get-tuple-element.60), channel_id=1, source_target_pairs={{0,64},{1,65},{2,66},{3,67},{4,68},{5,69},{6,70},{7,71},{8,72},{9,... | collective-permute-start | bytes 786440 | tf_op jit(solution)/shard_map/ppermute | solution.py:51
  73.2 8.0 %collective-permute-start.20 = (bf16[128,1024]{1,0:T(8,128)(2,1)S(1)}, bf16[128,1024]{1,0:T(8,128)(2,1)S(1)}, u32[]{:S(2)}, u32[]{:S(2)}) collective-permute-start(bf16[128,1024]{1,0:T(8,128)(2,1)S(1)} %get-tuple-element.72), channel_id=1, source_target_pairs={{0,1},{1,0},{2,3},{3,2},{4,5},{5,4},{6,7},{7,6},{8,9},{9,8},{10,11... | collective-permute-start | bytes 786440 | tf_op jit(solution)/shard_map/ppermute | solution.py:51

commit v7 on v6

--- a/solution.py
+++ b/solution.py
@@ -443,13 +443,17 @@
     )
     tables = (other_cos, other_sin, *tables)
     queries = project_q(core, owners, others, rows, qkv_weight, tables)
-    moved = [permute(kv[k], shift_x(k)) for k in (1, 3, 2)]
-    parts = [[queries[0]] + [permute(queries[k], shift_x(k)) for k in (1, 3, 2)]]
+    moved = []
+    for k in (2, 1, 3):
+        moved.append(permute(kv[k], shift_x(k)))
+    parts = [[queries[0]], [queries[4]]]
+    for k in (2, 1, 3):
+        parts[0].append(permute(queries[k], shift_x(k)))
+        parts[1].append(permute(queries[4 + k], shift_x(k)))
     own = kv[0] + moved[0] + moved[1] + moved[2]
     first = []
     for k in (1, 3, 2):
         first.append(permute(own, shift_first(k)))
-    parts.append([queries[4]] + [permute(queries[4 + k], shift_x(k)) for k in (1, 3, 2)])
     low = jnp.concatenate([own, first[0]], axis=0)
     high = jnp.concatenate([first[1], first[2]], axis=0)
     left = [permute(v, shift_second(1)) for v in (low, high)]
@@ -465,8 +469,9 @@
         parts[t] = [query]
     both = attend([(0, 0, False), (1, 0, False)], *tables, near_items, parts, state, False)
     state = [both[:3], both[3:]]
-    sent, kept = attend([(0, 0, False), (1, 0, False)], *tables, far_items, parts, state, True)
+    (sent,) = attend([(0, 0, False)], *tables, far_items, parts, state, True)
     received = permute(sent, OTHER_CORE)
+    (kept,) = attend([(1, 0, False)], *tables, far_items, parts, state, True)
     return join(core, kept, received)[None]
 
 

time: 82.4 us -> 82.3 us (level)
  the two profiles are of different devices: /device:TPU:75 before, /device:TPU:33 now
where the time goes in v7:
time: 82.3 us; the launch traced here: 81.9 us
  starting transfers between devices  30 us (36%)
  waiting for transfers between devices  27 us (33%)
  Pallas kernels  24 us (29%)
    ppermute x21, starting transfers between devices, permute(): return lax.ppermute(value, AXES, table)  30 us
    ppermute x21, waiting for transfers between devices, permute(): return lax.ppermute(value, AXES, table)  27 us
    pallas_call x5, Pallas kernels, attend(): pl.pallas_call(functools.partial(attend_kernel, jobs, spots, last), in_sp...  10.9 us
    pallas_call x1, Pallas kernels, project_q(): pl.pallas_call(q_kernel, in_specs=[smem] * 3 + [pl.BlockSpec(memory_space...  6.16 us
    pallas_call x1, Pallas kernels, prepare(): pl.pallas_call(prepare_kernel, in_specs=[smem] * 3 + [anywhere] * 2, out_...  3.33 us
    pallas_call x1, Pallas kernels, project_kv(): pl.pallas_call(kv_kernel, in_specs=[smem] * 4 + [vmem] * len(operands), o...  2.83 us
  transfers between devices with their start and end apart: 21, of which 7 were waited for; matrix products, arithmetic and copies ran while one was open for 0% of the time, Pallas kernels for 24%

profile of v7, /device:TPU:33, one launch (start us, length us, event | category | flops | bytes accessed | tf_op | source)
XLA Modules:
  0.0 81.9 jit_solution(16025288989393999101)
XLA Ops:
  0.0 0.7 collective-permute-start.1
  0.7 0.0 collective-permute-start
  1.3 3.3 %prepare.1 = (bf16[128,4096]{1,0:T(8,128)(2,1)S(1)}, bf16[4096,512]{1,0:T(8,128)(2,1)S(1)}, f32[128,128]{1,0:T(8,128)S(1)}, f32[128,128]{1,0:T(8,128)S(1)}) custom-call(s32[1]{0:T(128)} %bitcast.core_ref, s32[1,1]{1,0:T(1,128)S(6)} %copy.7.owner_ref, s32[4,32]{1,0:T(4,128)} %order_ref.13, bf16[128,4096]{1,0:T(8,128)(2,1)} %bitcast.4, bf16[4096,3072]{1,0:T(8,128)(2,1)} %w_ref.3), custom_call_target="tpu_custom_call" | custom-call | flops 67108864 | bytes 5242880 | tf_op jit(solution)/shard_map/prepare/pallas_call | solution.py:105
  4.7 0.0 collective-permute-done.other_ref
  4.7 0.0 collective-permute-done.1.y_ref
  4.7 2.8 %kv_proj.1 = (f32[128,128]{1,0:T(8,128)S(1)}, f32[128,128]{1,0:T(8,128)S(1)}, bf16[256,512]{1,0:T(8,128)(2,1)S(1)}, bf16[256,512]{1,0:T(8,128)(2,1)S(1)}, bf16[2...) custom-call(s32[1]{0:T(128)} %bitcast.core_ref, s32[1,1]{1,0:T(1,128)} %collective-permute-done.other_ref, ...), custom_call_target="tpu_custom_call" | custom-call | flops 1073741824 | bytes 4194304 | tf_op jit(solution)/shard_map/kv_proj/pallas_call | solution.py:197
  7.5 2.8 %collective-permute-start.2 = (bf16[256,512]{1,0:T(8,128)(2,1)S(1)}, bf16[256,512]{1,0:T(8,128)(2,1)S(1)}, u32[]{:S(2)}, u32[]{:S(2)}) collective-permute-start(bf16[256,512]{1,0:T(8,128)(2,1)S(1)} %get-tuple-element.42), channel_id=1, source_target_pairs={{0,64},{1,65},{2,66},{3,67},{4,68},{5,69},{6,70},{7,71},{8,72},{9,... | collective-permute-start | bytes 786440 | tf_op jit(solution)/shard_map/ppermute | solution.py:51
  10.3 0.3 collective-permute-start.3
  10.7 2.4 %collective-permute-start.4 = (bf16[256,512]{1,0:T(8,128)(2,1)S(1)}, bf16[256,512]{1,0:T(8,128)(2,1)S(1)}, u32[]{:S(2)}, u32[]{:S(2)}) collective-permute-start(bf16[256,512]{1,0:T(8,128)(2,1)S(1)} %get-tuple-element.44), channel_id=1, source_target_pairs={{0,96},{1,97},{2,98},{3,99},{4,100},{5,101},{6,102},{7,103},{8,104... | collective-permute-start | bytes 786440 | tf_op jit(solution)/shard_map/ppermute | solution.py:51
  13.0 3.5 %collective-permute-done.2 = bf16[256,512]{1,0:T(8,128)(2,1)S(1)} collective-permute-done((bf16[256,512]{1,0:T(8,128)(2,1)S(1)}, bf16[256,512]{1,0:T(8,128)(2,1)S(1)}, u32[]{:S(2)}, u32[]{:S(2)}) %collective-permute-start.2) | collective-permute-done | bytes 262176 | tf_op jit(solution)/shard_map/ppermute | solution.py:51
  16.5 6.5 %collective-permute-done.3 = bf16[256,512]{1,0:T(8,128)(2,1)S(1)} collective-permute-done((bf16[256,512]{1,0:T(8,128)(2,1)S(1)}, bf16[256,512]{1,0:T(8,128)(2,1)S(1)}, u32[]{:S(2)}, u32[]{:S(2)}) %collective-permute-start.3) | collective-permute-done | bytes 262176 | tf_op jit(solution)/shard_map/ppermute | solution.py:51
  23.0 0.0 collective-permute-done.4
  23.0 0.1 add_add_fusion
  23.0 1.4 %collective-permute-start.5 = (bf16[256,512]{1,0:T(8,128)(2,1)S(1)}, bf16[256,512]{1,0:T(8,128)(2,1)S(1)}, u32[]{:S(2)}, u32[]{:S(2)}) collective-permute-start(bf16[256,512]{1,0:T(8,128)(2,1)S(1)} %add_add_fusion), channel_id=1, source_target_pairs={{0,8},{1,3},{2,10},{3,5},{4,12},{5,7},{6,14},{7,1},{8,16},{9,11},{... | collective-permute-start | bytes 786440 | tf_op jit(solution)/shard_map/ppermute | solution.py:51
  24.4 2.6 %collective-permute-start.9 = (bf16[256,512]{1,0:T(8,128)(2,1)S(1)}, bf16[256,512]{1,0:T(8,128)(2,1)S(1)}, u32[]{:S(2)}, u32[]{:S(2)}) collective-permute-start(bf16[256,512]{1,0:T(8,128)(2,1)S(1)} %add_add_fusion), channel_id=1, source_target_pairs={{0,16},{1,5},{2,18},{3,7},{4,20},{5,1},{6,22},{7,3},{8,24},{9,13},... | collective-permute-start | bytes 786440 | tf_op jit(solution)/shard_map/ppermute | solution.py:51
  27.0 1.1 %collective-permute-start.8 = (bf16[256,512]{1,0:T(8,128)(2,1)S(1)}, bf16[256,512]{1,0:T(8,128)(2,1)S(1)}, u32[]{:S(2)}, u32[]{:S(2)}) collective-permute-start(bf16[256,512]{1,0:T(8,128)(2,1)S(1)} %add_add_fusion), channel_id=1, source_target_pairs={{0,24},{1,7},{2,26},{3,1},{4,28},{5,3},{6,30},{7,5},{8,0},{9,15},{... | collective-permute-start | bytes 786440 | tf_op jit(solution)/shard_map/ppermute | solution.py:51
  28.1 6.2 %q_proj.1 = (bf16[128,1024]{1,0:T(8,128)(2,1)S(1)}, bf16[128,1024]{1,0:T(8,128)(2,1)S(1)}, bf16[128,1024]{1,0:T(8,128)(2,1)S(1)}, bf16[128,1024]{1,0:T(8,128)(2,...) custom-call(s32[1]{0:T(128)} %bitcast.core_ref, ...), custom_call_target="tpu_custom_call" | custom-call | flops 2147483648 | bytes 8388608 | tf_op jit(solution)/shard_map/q_proj/pallas_call | solution.py:219
  34.3 1.1 %collective-permute-start.12 = (bf16[128,1024]{1,0:T(8,128)(2,1)S(1)}, bf16[128,1024]{1,0:T(8,128)(2,1)S(1)}, u32[]{:S(2)}, u32[]{:S(2)}) collective-permute-start(bf16[128,1024]{1,0:T(8,128)(2,1)S(1)} %get-tuple-element.48), channel_id=1, source_target_pairs={{0,64},{1,65},{2,66},{3,67},{4,68},{5,69},{6,70},{7,71},{8,72},{9,... | collective-permute-start | bytes 786440 | tf_op jit(solution)/shard_map/ppermute | solution.py:51
  35.3 0.0 collective-permute-done.5
  35.4 1.7 %collective-permute-start.6 = (bf16[512,512]{1,0:T(8,128)(2,1)S(1)}, bf16[512,512]{1,0:T(8,128)(2,1)S(1)}, u32[]{:S(2)}, u32[]{:S(2)}) collective-permute-start(bf16[512,512]{1,0:T(8,128)(2,1)S(1)} %pad_maximum_fusion.refs_0_), channel_id=1, source_target_pairs={{0,2},{1,9},{2,4},{3,11},{4,6},{5,13},{6,0},{7,15},{8,10},{9,17},{... | collective-permute-start | bytes 1572872 | tf_op jit(solution)/shard_map/ppermute | solution.py:51
  37.1 0.0 collective-permute-done.8
  37.1 0.0 collective-permute-done.9
  37.2 0.1 collective-permute-start.10
  37.2 2.1 %collective-permute-start.13 = (bf16[128,1024]{1,0:T(8,128)(2,1)S(1)}, bf16[128,1024]{1,0:T(8,128)(2,1)S(1)}, u32[]{:S(2)}, u32[]{:S(2)}) collective-permute-start(bf16[128,1024]{1,0:T(8,128)(2,1)S(1)} %get-tuple-element.49), channel_id=1, source_target_pairs={{0,32},{1,33},{2,34},{3,35},{4,36},{5,37},{6,38},{7,39},{8,40},{9,... | collective-permute-start | bytes 786440 | tf_op jit(solution)/shard_map/ppermute | solution.py:51
  39.3 0.6 collective-permute-start.14
  40.0 2.4 %collective-permute-done.12.refs_3_ = bf16[128,1024]{1,0:T(8,128)(2,1)S(1)} collective-permute-done((bf16[128,1024]{1,0:T(8,128)(2,1)S(1)}, bf16[128,1024]{1,0:T(8,128)(2,1)S(1)}, u32[]{:S(2)}, u32[]{:S(2)}) %collective-permute-start.12) | collective-permute-done | bytes 262176 | tf_op jit(solution)/shard_map/ppermute | solution.py:51
  42.3 0.3 collective-permute-start.17
  42.6 5.7 %collective-permute-done.13.refs_4_ = bf16[128,1024]{1,0:T(8,128)(2,1)S(1)} collective-permute-done((bf16[128,1024]{1,0:T(8,128)(2,1)S(1)}, bf16[128,1024]{1,0:T(8,128)(2,1)S(1)}, u32[]{:S(2)}, u32[]{:S(2)}) %collective-permute-start.13) | collective-permute-done | bytes 262176 | tf_op jit(solution)/shard_map/ppermute | solution.py:51
  48.4 0.0 collective-permute-start.18
  48.4 0.7 collective-permute-start.16
  49.0 4.5 %collective-permute-done.17.refs_3_ = bf16[128,1024]{1,0:T(8,128)(2,1)S(1)} collective-permute-done((bf16[128,1024]{1,0:T(8,128)(2,1)S(1)}, bf16[128,1024]{1,0:T(8,128)(2,1)S(1)}, u32[]{:S(2)}, u32[]{:S(2)}) %collective-permute-start.17) | collective-permute-done | bytes 262176 | tf_op jit(solution)/shard_map/ppermute | solution.py:51
  53.6 2.8 %collective-permute-start.15 = (bf16[512,512]{1,0:T(8,128)(2,1)S(1)}, bf16[512,512]{1,0:T(8,128)(2,1)S(1)}, u32[]{:S(2)}, u32[]{:S(2)}) collective-permute-start(bf16[512,512]{1,0:T(8,128)(2,1)S(1)} %constant_dynamic-update-slice_fusion.refs_1_), channel_id=1, source_target_pairs={{0,2},{1,9},{2,4},{3,11},{4,6},{5,13},{6,0},{7,15},{8,10},{9,17},{... | collective-permute-start | bytes 1572872 | tf_op jit(solution)/shard_map/ppermute | solution.py:51
  56.4 0.8 collective-permute-start.7
  57.1 0.0 collective-permute-done.10.refs_2_
  57.1 0.7 collective-permute-start.11
  57.8 1.8 %collective-permute-done.18.refs_4_ = bf16[128,1024]{1,0:T(8,128)(2,1)S(1)} collective-permute-done((bf16[128,1024]{1,0:T(8,128)(2,1)S(1)}, bf16[128,1024]{1,0:T(8,128)(2,1)S(1)}, u32[]{:S(2)}, u32[]{:S(2)}) %collective-permute-start.18) | collective-permute-done | bytes 262176 | tf_op jit(solution)/shard_map/ppermute | solution.py:51
  59.6 0.5 collective-permute-start.19
  60.1 2.6 %shard_map.55 = (f32[2,128,512]{2,1,0:T(8,128)S(1)}, f32[2,8,512]{2,1,0:T(8,128)S(1)}, f32[2,8,512]{2,1,0:T(8,128)S(1)}, bf16[128,1024]{1,0:T(8,128)(2,1)S(1)}) custom-call(s32[4,32]{1,0:T(4,128)} %sequence_ref.9, s32[4,32]{1,0:T(4,128)} %order_ref.13, bf16[512,512]{1,0:T(8,128)(2,1)S(1)} %pad_maximum_fusion.refs_0_, ...), custom_call_target="tpu_custom_call" | custom-call | flops 268435456 | bytes 2097152 | tf_op jit(solution)/shard_map/pallas_call | solution.py:400
  62.8 2.6 %collective-permute-done.19.refs_5_ = bf16[128,1024]{1,0:T(8,128)(2,1)S(1)} collective-permute-done((bf16[128,1024]{1,0:T(8,128)(2,1)S(1)}, bf16[128,1024]{1,0:T(8,128)(2,1)S(1)}, u32[]{:S(2)}, u32[]{:S(2)}) %collective-permute-start.19) | collective-permute-done | bytes 262176 | tf_op jit(solution)/shard_map/ppermute | solution.py:51
  65.4 1.6 %shard_map.56 = (f32[2,128,512]{2,1,0:T(8,128)S(1)}, f32[2,8,512]{2,1,0:T(8,128)S(1)}, f32[2,8,512]{2,1,0:T(8,128)S(1)}, bf16[128,1024]{1,0:T(8,128)(2,1)S(1)}) custom-call(s32[4,32]{1,0:T(4,128)} %sequence_ref.9, s32[4,32]{1,0:T(4,128)} %order_ref.13, bf16[512,512]{1,0:T(8,128)(2,1)S(1)} %pad_maximum_fusion.refs_0_, ...), custom_call_target="tpu_custom_call" | custom-call | flops 268435456 | bytes 2097152 | tf_op jit(solution)/shard_map/pallas_call | solution.py:400
  66.9 0.0 collective-permute-done.16.refs_3_
  67.0 2.6 %shard_map.57 = (f32[2,128,512]{2,1,0:T(8,128)S(1)}, f32[2,8,512]{2,1,0:T(8,128)S(1)}, f32[2,8,512]{2,1,0:T(8,128)S(1)}, f32[2,128,512]{2,1,0:T(8,128)S(1)}, f32...) custom-call(s32[4,32]{1,0:T(4,128)} %sequence_ref.9, s32[4,32]{1,0:T(4,128)} %order_ref.13, ...), custom_call_target="tpu_custom_call" | custom-call | flops 536870912 | bytes 2097152 | tf_op jit(solution)/shard_map/pallas_call | solution.py:400
  69.6 0.0 collective-permute-done.7.refs_0_
  69.6 1.1 %shard_map.59 = bf16[128,1024]{1,0:T(8,128)(2,1)S(1)} custom-call(s32[4,32]{1,0:T(4,128)} %sequence_ref.9, s32[4,32]{1,0:T(4,128)} %order_ref.13, bf16[512,512]{1,0:T(8,128)(2,1)S(1)} %collective-permute-done.7.refs_0_, bf16[512,512]{1,0:T(8,128)(2,1)S(1)} %collective-permute-done.11.refs_1_, bf16[128,1024]{1,0:T(8,128)(2,1)S(1)} %get-tuple-element.56.refs_4_.refs_2_, ...), custom_call_target="tpu_custom_call" | custom-call | flops 268435456 | bytes 2097152 | tf_op jit(solution)/shard_map/pallas_call | solution.py:400
  70.7 7.4 %collective-permute-start.20 = (bf16[128,1024]{1,0:T(8,128)(2,1)S(1)}, bf16[128,1024]{1,0:T(8,128)(2,1)S(1)}, u32[]{:S(2)}, u32[]{:S(2)}) collective-permute-start(bf16[128,1024]{1,0:T(8,128)(2,1)S(1)} %shard_map.59), channel_id=1, source_target_pairs={{0,1},{1,0},{2,3},{3,2},{4,5},{5,4},{6,7},{7,6},{8,9},{9,8},{10,11... | collective-permute-start | bytes 786440 | tf_op jit(solution)/shard_map/ppermute | solution.py:51
  78.1 3.0 %shard_map.58.kept_ref = bf16[128,1024]{1,0:T(8,128)(2,1)S(1)} custom-call(s32[4,32]{1,0:T(4,128)} %sequence_ref.9, s32[4,32]{1,0:T(4,128)} %order_ref.13, bf16[512,512]{1,0:T(8,128)(2,1)S(1)} %collective-permute-done.7.refs_0_, bf16[512,512]{1,0:T(8,128)(2,1)S(1)} %collective-permute-done.11.refs_1_, ...), custom_call_target="tpu_custom_call" | custom-call | flops 268435456 | bytes 2097152 | tf_op jit(solution)/shard_map/pallas_call | solution.py:400
  81.1 0.0 collective-permute-done.20.received_ref
  81.1 0.8 %join.1 = bf16[128,2048]{1,0:T(8,128)(2,1)} custom-call(s32[1]{0:T(128)} %bitcast.core_ref, bf16[128,1024]{1,0:T(8,128)(2,1)S(1)} %shard_map.58.kept_ref, bf16[128,1024]{1,0:T(8,128)(2,1)S(1)} %collective-permute-done.20.received_ref), custom_call_target="tpu_custom_call" | custom-call | flops 262144 | bytes 1048576 | tf_op jit(solution)/shard_map/join/pallas_call | solution.py:423
  (7 shorter events, 0.1 us)
Async XLA Ops:
  0.0 4.7 %collective-permute-start.1 = (bf16[128,4096]{1,0:T(8,128)(2,1)}, bf16[128,4096]{1,0:T(8,128)(2,1)S(1)}, u32[]{:S(2)}, u32[]{:S(2)}) collective-permute-start(bf16[128,4096]{1,0:T(8,128)(2,1)} %bitcast.3), channel_id=1, source_target_pairs={{0,1},{1,0},{2,3},{3,2},{4,5},{5,4},{6,7},{7,6},{8,9},{9,8},{10,11... | collective-permute-start | bytes 3145736 | tf_op jit(solution)/shard_map/ppermute | solution.py:51
  0.7 4.0 %collective-permute-start = (s32[1,1]{1,0:T(1,128)}, s32[1,1]{1,0:T(1,128)}, u32[]{:S(2)}, u32[]{:S(2)}) collective-permute-start(s32[1,1]{1,0:T(1,128)} %param.7), channel_id=1, source_target_pairs={{0,1},{1,0},{2,3},{3,2},{4,5},{5,4},{6,7},{7,6},{8,9},{9,8},{10,11... | collective-permute-start | bytes 20 | tf_op jit(solution)/shard_map/ppermute | solution.py:51
  7.5 9.0 %collective-permute-start.2 = (bf16[256,512]{1,0:T(8,128)(2,1)S(1)}, bf16[256,512]{1,0:T(8,128)(2,1)S(1)}, u32[]{:S(2)}, u32[]{:S(2)}) collective-permute-start(bf16[256,512]{1,0:T(8,128)(2,1)S(1)} %get-tuple-element.42), channel_id=1, source_target_pairs={{0,64},{1,65},{2,66},{3,67},{4,68},{5,69},{6,70},{7,71},{8,72},{9,... | collective-permute-start | bytes 786440 | tf_op jit(solution)/shard_map/ppermute | solution.py:51
  10.3 12.6 %collective-permute-start.3 = (bf16[256,512]{1,0:T(8,128)(2,1)S(1)}, bf16[256,512]{1,0:T(8,128)(2,1)S(1)}, u32[]{:S(2)}, u32[]{:S(2)}) collective-permute-start(bf16[256,512]{1,0:T(8,128)(2,1)S(1)} %get-tuple-element.43), channel_id=1, source_target_pairs={{0,32},{1,33},{2,34},{3,35},{4,36},{5,37},{6,38},{7,39},{8,40},{9,... | collective-permute-start | bytes 786440 | tf_op jit(solution)/shard_map/ppermute | solution.py:51
  10.7 12.3 %collective-permute-start.4 = (bf16[256,512]{1,0:T(8,128)(2,1)S(1)}, bf16[256,512]{1,0:T(8,128)(2,1)S(1)}, u32[]{:S(2)}, u32[]{:S(2)}) collective-permute-start(bf16[256,512]{1,0:T(8,128)(2,1)S(1)} %get-tuple-element.44), channel_id=1, source_target_pairs={{0,96},{1,97},{2,98},{3,99},{4,100},{5,101},{6,102},{7,103},{8,104... | collective-permute-start | bytes 786440 | tf_op jit(solution)/shard_map/ppermute | solution.py:51
  23.0 12.3 %collective-permute-start.5 = (bf16[256,512]{1,0:T(8,128)(2,1)S(1)}, bf16[256,512]{1,0:T(8,128)(2,1)S(1)}, u32[]{:S(2)}, u32[]{:S(2)}) collective-permute-start(bf16[256,512]{1,0:T(8,128)(2,1)S(1)} %add_add_fusion), channel_id=1, source_target_pairs={{0,8},{1,3},{2,10},{3,5},{4,12},{5,7},{6,14},{7,1},{8,16},{9,11},{... | collective-permute-start | bytes 786440 | tf_op jit(solution)/shard_map/ppermute | solution.py:51
  24.4 12.7 %collective-permute-start.9 = (bf16[256,512]{1,0:T(8,128)(2,1)S(1)}, bf16[256,512]{1,0:T(8,128)(2,1)S(1)}, u32[]{:S(2)}, u32[]{:S(2)}) collective-permute-start(bf16[256,512]{1,0:T(8,128)(2,1)S(1)} %add_add_fusion), channel_id=1, source_target_pairs={{0,16},{1,5},{2,18},{3,7},{4,20},{5,1},{6,22},{7,3},{8,24},{9,13},... | collective-permute-start | bytes 786440 | tf_op jit(solution)/shard_map/ppermute | solution.py:51
  27.0 10.1 %collective-permute-start.8 = (bf16[256,512]{1,0:T(8,128)(2,1)S(1)}, bf16[256,512]{1,0:T(8,128)(2,1)S(1)}, u32[]{:S(2)}, u32[]{:S(2)}) collective-permute-start(bf16[256,512]{1,0:T(8,128)(2,1)S(1)} %add_add_fusion), channel_id=1, source_target_pairs={{0,24},{1,7},{2,26},{3,1},{4,28},{5,3},{6,30},{7,5},{8,0},{9,15},{... | collective-permute-start | bytes 786440 | tf_op jit(solution)/shard_map/ppermute | solution.py:51
  34.3 8.1 %collective-permute-start.12 = (bf16[128,1024]{1,0:T(8,128)(2,1)S(1)}, bf16[128,1024]{1,0:T(8,128)(2,1)S(1)}, u32[]{:S(2)}, u32[]{:S(2)}) collective-permute-start(bf16[128,1024]{1,0:T(8,128)(2,1)S(1)} %get-tuple-element.48), channel_id=1, source_target_pairs={{0,64},{1,65},{2,66},{3,67},{4,68},{5,69},{6,70},{7,71},{8,72},{9,... | collective-permute-start | bytes 786440 | tf_op jit(solution)/shard_map/ppermute | solution.py:51
  35.4 21.0 %collective-permute-start.6 = (bf16[512,512]{1,0:T(8,128)(2,1)S(1)}, bf16[512,512]{1,0:T(8,128)(2,1)S(1)}, u32[]{:S(2)}, u32[]{:S(2)}) collective-permute-start(bf16[512,512]{1,0:T(8,128)(2,1)S(1)} %pad_maximum_fusion.refs_0_), channel_id=1, source_target_pairs={{0,2},{1,9},{2,4},{3,11},{4,6},{5,13},{6,0},{7,15},{8,10},{9,17},{... | collective-permute-start | bytes 1572872 | tf_op jit(solution)/shard_map/ppermute | solution.py:51
  37.2 20.0 %collective-permute-start.10 = (bf16[512,512]{1,0:T(8,128)(2,1)S(1)}, bf16[512,512]{1,0:T(8,128)(2,1)S(1)}, u32[]{:S(2)}, u32[]{:S(2)}) collective-permute-start(bf16[512,512]{1,0:T(8,128)(2,1)S(1)} %constant_dynamic-update-slice_fusion.refs_1_), channel_id=1, source_target_pairs={{0,6},{1,25},{2,0},{3,27},{4,2},{5,29},{6,4},{7,31},{8,14},{9,1},{... | collective-permute-start | bytes 1572872 | tf_op jit(solution)/shard_map/ppermute | solution.py:51
  37.2 11.1 %collective-permute-start.13 = (bf16[128,1024]{1,0:T(8,128)(2,1)S(1)}, bf16[128,1024]{1,0:T(8,128)(2,1)S(1)}, u32[]{:S(2)}, u32[]{:S(2)}) collective-permute-start(bf16[128,1024]{1,0:T(8,128)(2,1)S(1)} %get-tuple-element.49), channel_id=1, source_target_pairs={{0,32},{1,33},{2,34},{3,35},{4,36},{5,37},{6,38},{7,39},{8,40},{9,... | collective-permute-start | bytes 786440 | tf_op jit(solution)/shard_map/ppermute | solution.py:51
  39.3 9.0 %collective-permute-start.14 = (bf16[128,1024]{1,0:T(8,128)(2,1)S(1)}, bf16[128,1024]{1,0:T(8,128)(2,1)S(1)}, u32[]{:S(2)}, u32[]{:S(2)}) collective-permute-start(bf16[128,1024]{1,0:T(8,128)(2,1)S(1)} %get-tuple-element.50), channel_id=1, source_target_pairs={{0,96},{1,97},{2,98},{3,99},{4,100},{5,101},{6,102},{7,103},{8,104... | collective-permute-start | bytes 786440 | tf_op jit(solution)/shard_map/ppermute | solution.py:51
  42.3 11.2 %collective-permute-start.17 = (bf16[128,1024]{1,0:T(8,128)(2,1)S(1)}, bf16[128,1024]{1,0:T(8,128)(2,1)S(1)}, u32[]{:S(2)}, u32[]{:S(2)}) collective-permute-start(bf16[128,1024]{1,0:T(8,128)(2,1)S(1)} %get-tuple-element.53), channel_id=1, source_target_pairs={{0,64},{1,65},{2,66},{3,67},{4,68},{5,69},{6,70},{7,71},{8,72},{9,... | collective-permute-start | bytes 786440 | tf_op jit(solution)/shard_map/ppermute | solution.py:51
  48.4 11.3 %collective-permute-start.18 = (bf16[128,1024]{1,0:T(8,128)(2,1)S(1)}, bf16[128,1024]{1,0:T(8,128)(2,1)S(1)}, u32[]{:S(2)}, u32[]{:S(2)}) collective-permute-start(bf16[128,1024]{1,0:T(8,128)(2,1)S(1)} %get-tuple-element.54), channel_id=1, source_target_pairs={{0,32},{1,33},{2,34},{3,35},{4,36},{5,37},{6,38},{7,39},{8,40},{9,... | collective-permute-start | bytes 786440 | tf_op jit(solution)/shard_map/ppermute | solution.py:51
  48.4 18.6 %collective-permute-start.16 = (bf16[512,512]{1,0:T(8,128)(2,1)S(1)}, bf16[512,512]{1,0:T(8,128)(2,1)S(1)}, u32[]{:S(2)}, u32[]{:S(2)}) collective-permute-start(bf16[512,512]{1,0:T(8,128)(2,1)S(1)} %pad_maximum_fusion.refs_0_), channel_id=1, source_target_pairs={{0,6},{1,25},{2,0},{3,27},{4,2},{5,29},{6,4},{7,31},{8,14},{9,1},{... | collective-permute-start | bytes 1572872 | tf_op jit(solution)/shard_map/ppermute | solution.py:51
  53.6 13.4 %collective-permute-start.15 = (bf16[512,512]{1,0:T(8,128)(2,1)S(1)}, bf16[512,512]{1,0:T(8,128)(2,1)S(1)}, u32[]{:S(2)}, u32[]{:S(2)}) collective-permute-start(bf16[512,512]{1,0:T(8,128)(2,1)S(1)} %constant_dynamic-update-slice_fusion.refs_1_), channel_id=1, source_target_pairs={{0,2},{1,9},{2,4},{3,11},{4,6},{5,13},{6,0},{7,15},{8,10},{9,17},{... | collective-permute-start | bytes 1572872 | tf_op jit(solution)/shard_map/ppermute | solution.py:51
  56.4 13.2 %collective-permute-start.7 = (bf16[512,512]{1,0:T(8,128)(2,1)S(1)}, bf16[512,512]{1,0:T(8,128)(2,1)S(1)}, u32[]{:S(2)}, u32[]{:S(2)}) collective-permute-start(bf16[512,512]{1,0:T(8,128)(2,1)S(1)} %collective-permute-done.6.refs_0_), channel_id=1, source_target_pairs={{0,2},{1,9},{2,4},{3,11},{4,6},{5,13},{6,0},{7,15},{8,10},{9,17},{... | collective-permute-start | bytes 1572872 | tf_op jit(solution)/shard_map/ppermute | solution.py:51
  57.1 12.5 %collective-permute-start.11 = (bf16[512,512]{1,0:T(8,128)(2,1)S(1)}, bf16[512,512]{1,0:T(8,128)(2,1)S(1)}, u32[]{:S(2)}, u32[]{:S(2)}) collective-permute-start(bf16[512,512]{1,0:T(8,128)(2,1)S(1)} %collective-permute-done.10.refs_2_), channel_id=1, source_target_pairs={{0,6},{1,25},{2,0},{3,27},{4,2},{5,29},{6,4},{7,31},{8,14},{9,1},{... | collective-permute-start | bytes 1572872 | tf_op jit(solution)/shard_map/ppermute | solution.py:51
  59.6 5.7 %collective-permute-start.19 = (bf16[128,1024]{1,0:T(8,128)(2,1)S(1)}, bf16[128,1024]{1,0:T(8,128)(2,1)S(1)}, u32[]{:S(2)}, u32[]{:S(2)}) collective-permute-start(bf16[128,1024]{1,0:T(8,128)(2,1)S(1)} %get-tuple-element.55), channel_id=1, source_target_pairs={{0,96},{1,97},{2,98},{3,99},{4,100},{5,101},{6,102},{7,103},{8,104... | collective-permute-start | bytes 786440 | tf_op jit(solution)/shard_map/ppermute | solution.py:51
  70.7 10.4 %collective-permute-start.20 = (bf16[128,1024]{1,0:T(8,128)(2,1)S(1)}, bf16[128,1024]{1,0:T(8,128)(2,1)S(1)}, u32[]{:S(2)}, u32[]{:S(2)}) collective-permute-start(bf16[128,1024]{1,0:T(8,128)(2,1)S(1)} %shard_map.59), channel_id=1, source_target_pairs={{0,1},{1,0},{2,3},{3,2},{4,5},{5,4},{6,7},{7,6},{8,9},{9,8},{10,11... | collective-permute-start | bytes 786440 | tf_op jit(solution)/shard_map/ppermute | solution.py:51
